TPU v7x, 32 devices: a whole 2x2x4 slice. The times are simulated.
32 devices in a mesh: pool: 2 (over y), blk: 4 (over x, core), batch: 4 (over z).
Axes of the slice: x: 2, y: 2, z: 4, core: 2. Of those that a mesh axis runs over, the one named last changes fastest.
Arguments:
- prompt: bfloat16 [8, 512, 4096], P(('pool', 'batch'), 'blk'), may hold values from -40 to 40
- prompt_len: int32 [2, 4], P('pool', 'batch'), may hold values from 128 to 512
- dec_tokens: bfloat16 [4, 32, 4096], P(None, ('pool', 'batch')), may hold values from -40 to 40
- cache_k: bfloat16 [32, 4096, 1024], P(('pool', 'batch'), None, 'blk'), may hold values from -72 to 72
- cache_v: bfloat16 [32, 4096, 1024], P(('pool', 'batch'), None, 'blk'), may hold values from -6 to 6
- cache_len: int32 [32], P(('pool', 'batch')), may hold values from 1 to 4092
- assign: int32 [2, 4], P('pool', 'batch'), may hold values from 0 to 3, each once within a row
- slot: int32 [2, 4], P('pool', 'batch'), may hold values from 0 to 3
- gain: float32 [4096], replicated, may hold values from 0.5 to 1.5
- w_qkv: bfloat16 [4096, 6144], P(None, 'blk'), may hold values from -4 to 4
- w_out: bfloat16 [4096, 4096], P('blk'), may hold values from -0.09375 to 0.09375
Outputs:
- prefill_out: bfloat16 [8, 512, 4096], P(('pool', 'batch'), 'blk')
- dec_out: bfloat16 [4, 32, 4096], P(None, ('pool', 'batch'))
Inputs may be any that keep to these rules, and one draw needn't show every extreme that they name: For each pool p, assign[p] is a permutation of the 4 stretch indices of the other pool.
All inputs are finite; a program needn't handle non-finite values.
Results may differ from a plain program's by a relative error of at most 0.011.
Values may be sent and summed in bfloat16 or wider, within the bound.
No kernel may reach another device: no remote copies, remote signals or barrier semaphores. Data moves between devices by JAX's collectives and lax.ppermute only.
A program may use at most 128 MiB of HBM per device.

v0:
```python
import jax
import jax.numpy as jnp
from jax import lax
from jax.sharding import PartitionSpec as P

HEAD_DIM = 128
GROUP = 4


EPSILON = 1e-05
THETA = 500000.0


def rms_norm(values, gain):
    wide = values.astype(jnp.float32)
    factor = lax.rsqrt(jnp.mean(wide * wide, axis=-1, keepdims=True) + EPSILON)
    return (wide * factor * gain).astype(jnp.bfloat16)


def rotate(vector, places):
    half = vector.shape[-1] // 2
    freqs = THETA ** (-jnp.arange(half, dtype=jnp.float32) / half)
    angles = places.astype(jnp.float32)[..., None] * freqs
    cosine = jnp.cos(angles)
    sine = jnp.sin(angles)
    first = vector[..., :half]
    second = vector[..., half:]
    return jnp.concatenate(
        [first * cosine - second * sine, second * cosine + first * sine], axis=-1
    )


def softmax_weights(scores):
    top = jnp.max(scores, axis=-1, keepdims=True)
    expo = jnp.exp(scores - top)
    return (expo / jnp.sum(expo, axis=-1, keepdims=True)).astype(jnp.bfloat16)


def make_picker(wanted, carry, piece):
    count = piece[0].shape[0]
    match = jnp.arange(count, dtype=jnp.int32) == wanted
    keys = jnp.sum(jnp.where(match[:, None, None], piece[0].astype(jnp.float32), 0.0), axis=0)
    values = jnp.sum(jnp.where(match[:, None, None], piece[1].astype(jnp.float32), 0.0), axis=0)
    length = carry[2] + jnp.sum(jnp.where(match, piece[2], 0))
    return (keys, values, length)


def attend(
    query,
    cache_key,
    cache_value,
    lengths,
    fresh,
    new_key,
    new_value,
    new_len,
    own_key,
    own_value,
    own_mask,
):
    f32 = jnp.float32
    scale = query.shape[-1] ** (-0.5)
    old = jnp.einsum("srhgd,rchd->srhgc", query, cache_key, preferred_element_type=f32) * scale
    span = jnp.arange(cache_key.shape[1], dtype=jnp.int32)
    old_ok = (span[None, :] < lengths[:, None]) & jnp.logical_not(fresh)[:, None]
    old = jnp.where(old_ok[None, :, None, None, :], old, -jnp.inf)
    new = jnp.einsum("srhgd,chd->srhgc", query, new_key, preferred_element_type=f32) * scale
    reach = jnp.arange(new_key.shape[0], dtype=jnp.int32)
    new_ok = (reach[None, :] < new_len) & fresh[:, None]
    new = jnp.where(new_ok[None, :, None, None, :], new, -jnp.inf)
    own = jnp.einsum("srhgd,trhd->srhgt", query, own_key, preferred_element_type=f32) * scale
    own = jnp.where(own_mask[:, None, None, None, :], own, -jnp.inf)
    cached = cache_key.shape[1]
    fresh_count = new_key.shape[0]
    probs = softmax_weights(jnp.concatenate([old, new, own], axis=-1))
    mixed = jnp.einsum(
        "srhgc,rchd->srhgd", probs[..., :cached], cache_value, preferred_element_type=f32
    )
    mixed = mixed + jnp.einsum(
        "srhgc,chd->srhgd",
        probs[..., cached : cached + fresh_count],
        new_value,
        preferred_element_type=f32,
    )
    mixed = mixed + jnp.einsum(
        "srhgt,trhd->srhgd",
        probs[..., cached + fresh_count :],
        own_value,
        preferred_element_type=f32,
    )
    return mixed.astype(jnp.bfloat16)


def body(
    prompt, prompt_len, dec_tokens, cache_k, cache_v, cache_len, assign, slot, gain, w_qkv, w_out
):
    f32 = jnp.float32
    bf16 = jnp.bfloat16
    local = w_out.shape[0] // (GROUP * HEAD_DIM)
    scale = HEAD_DIM ** (-0.5)
    normed = rms_norm(prompt[0], gain)
    joined = jnp.dot(
        lax.all_gather(normed, "blk", axis=0, tiled=True), w_qkv, preferred_element_type=f32
    )
    stretch = joined.shape[0]
    joined = joined.reshape(stretch, local, GROUP + 2, HEAD_DIM)
    places = jnp.arange(stretch, dtype=jnp.int32)
    query = rotate(joined[:, :, :GROUP], places[:, None, None]).astype(bf16)
    key = rotate(joined[:, :, GROUP], places[:, None]).astype(bf16)
    value = joined[:, :, GROUP + 1].astype(bf16)
    plen = prompt_len[0, 0]
    scores = jnp.einsum("qhgd,khd->hgqk", query, key, preferred_element_type=f32) * scale
    allowed = (places[None, :] <= places[:, None]) & (places[None, :] < plen)
    scores = jnp.where(allowed, scores, -jnp.inf)
    probs = softmax_weights(scores)
    mixed = jnp.einsum("hgqk,khd->qhgd", probs, value, preferred_element_type=f32).astype(bf16)
    mixed = mixed.reshape(stretch, local * GROUP * HEAD_DIM)
    rows = mixed
    summed = lax.psum_scatter(
        jnp.dot(rows, w_out, preferred_element_type=f32).astype(jnp.bfloat16),
        "blk",
        scatter_dimension=0,
        tiled=True,
    ).astype(jnp.float32)
    prefill_out = (prompt[0].astype(f32) + summed).astype(bf16)[None]
    packet = (
        key.reshape(1, stretch, local * HEAD_DIM),
        value.reshape(1, stretch, local * HEAD_DIM),
        prompt_len.reshape(1),
    )
    empty = (
        jnp.zeros((stretch, local * HEAD_DIM), f32),
        jnp.zeros((stretch, local * HEAD_DIM), f32),
        jnp.zeros((), jnp.int32),
    )
    wanted = assign[0, 0]
    source = (1 - lax.axis_index("pool")) * lax.axis_size("batch") + wanted
    arrived = make_picker(
        source,
        empty,
        (
            lax.all_gather(packet[0], ("pool", "batch"), axis=0, tiled=True),
            lax.all_gather(packet[1], ("pool", "batch"), axis=0, tiled=True),
            lax.all_gather(packet[2], ("pool", "batch"), axis=0, tiled=True),
        ),
    )
    new_key = arrived[0].astype(bf16).reshape(stretch, local, HEAD_DIM)
    new_value = arrived[1].astype(bf16).reshape(stretch, local, HEAD_DIM)
    new_len = arrived[2]
    steps = dec_tokens.shape[0]
    rows = dec_tokens.shape[1]
    cached = cache_k.shape[1]
    cache_key = cache_k.reshape(rows, cached, local, HEAD_DIM)
    cache_value = cache_v.reshape(rows, cached, local, HEAD_DIM)
    fresh = jnp.arange(rows, dtype=jnp.int32) == slot[0, 0]
    begin = jnp.where(fresh, new_len, cache_len)
    normed_steps = rms_norm(dec_tokens, gain)
    joined_all = jnp.dot(normed_steps.reshape(steps * rows, -1), w_qkv, preferred_element_type=f32)
    joined_all = joined_all.reshape(steps, rows, local, GROUP + 2, HEAD_DIM)
    where_all = begin[None, :] + jnp.arange(steps, dtype=jnp.int32)[:, None]
    all_query = rotate(joined_all[:, :, :, :GROUP], where_all[:, :, None, None]).astype(bf16)
    all_key = rotate(joined_all[:, :, :, GROUP], where_all[:, :, None]).astype(bf16)
    all_value = joined_all[:, :, :, GROUP + 1].astype(bf16)
    own_mask = jnp.arange(steps)[None, :] <= jnp.arange(steps)[:, None]
    attended = attend(
        all_query,
        cache_key,
        cache_value,
        cache_len,
        fresh,
        new_key,
        new_value,
        new_len,
        all_key,
        all_value,
        own_mask,
    )
    partial_value = jnp.dot(
        attended.reshape(steps * rows, local * GROUP * HEAD_DIM), w_out, preferred_element_type=f32
    )
    total = lax.psum(partial_value.reshape(steps, rows, -1).astype(jnp.bfloat16), "blk").astype(
        jnp.float32
    )
    dec_out = (dec_tokens.astype(f32) + total).astype(bf16)
    return (prefill_out, dec_out)


def solution(mesh):
    return jax.shard_map(
        body,
        mesh=mesh,
        in_specs=(
            P(("pool", "batch"), "blk", None),
            P("pool", "batch"),
            P(None, ("pool", "batch"), None),
            P(("pool", "batch"), None, "blk"),
            P(("pool", "batch"), None, "blk"),
            P(("pool", "batch")),
            P("pool", "batch"),
            P("pool", "batch"),
            P(),
            P(None, "blk"),
            P("blk", None),
        ),
        out_specs=(P(("pool", "batch"), "blk", None), P(None, ("pool", "batch"), None)),
        check_vma=False,
    )
```

profile of v0, /device:TPU:0, one launch (start us, length us, event | category | flops | bytes accessed | tf_op | source)
XLA Modules:
  0.0 270.2 jit_solution(3102997159037806648)
XLA Ops:
  7.2 0.0 all-gather.5.cloned.1.call-start
  7.2 1.5 fusion.25
  8.8 2.5 fusion.27
  11.3 0.0 all-gather.7.cloned.1.call-start
  12.0 0.6 dynamic-slice
  12.6 0.6 bitcast_dynamic-update-slice_fusion
  13.3 13.0 %all-reduce = s32[8]{0:T(128)S(1)} all-reduce(s32[8]{0:T(128)S(1)} %bitcast_dynamic-update-slice_fusion), channel_id=2, replica_groups=mesh['pool'=2,'blk'=4,'batch'=4] {'pool','batch'}, use_global_device_ids=true, to_apply=%add | all-reduce | flops 8 | bytes 64 | tf_op jit(solution)/shard_map/all_gather | solution.py:144
  27.6 16.9 %copy.77 = bf16[4096,1536]{0,1:T(8,128)(2,1)} copy(bf16[4096,1536]{1,0:T(8,128)(2,1)} %param.20) | data formatting | bytes 25165824 | tf_op args[9]
  44.6 0.7 select_reduce_fusion.2
  45.2 0.6 iota_compare_fusion.3
  45.9 0.2 fusion.49
  46.1 1.0 multiply_cosine_fusion
  47.1 6.6 %fusion.56 = f32[4,4,2,6,128]{4,1,3,2,0:T(4,128)S(1)} fusion(bf16[2,6,128,4096,1]{3,2,1,0,4:T(8,128)(2,1)} %bitcast.123, bf16[4,4,4096]{2,1,0:T(4,128)(2,1)S(1)} %copy-done.6, f32[4096]{0:T(1024)S(1)} %copy-done.11, f32[4,4]{1,0:T(4,128)S(1)} %add_rsqrt_fusion), kind=kOutput, calls=%fused_computation.73 | convolution fusion | flops 201588736 | bytes 12828736 | tf_op jit(solution)/shard_map/dot_general | solution.py:158
  53.7 0.0 all-gather.5.cloned.1.call-done
  53.7 10.7 %fusion.79 = f32[512,1536]{0,1:T(8,128)S(1)} fusion(bf16[512,4096]{1,0:T(8,128)(2,1)} %all-gather.5.cloned.1.call-done, bf16[4096,1536]{1,0:T(8,128)(2,1)} %param.20), kind=kOutput, calls=%fused_computation.120 | convolution fusion | flops 6442450944 | bytes 19922944 | tf_op jit(solution)/shard_map/dot_general | solution.py:102
  64.4 1.6 copy-done.1
  66.1 0.2 copy.121
  66.3 0.2 multiply_subtract_fusion
  66.5 0.1 maximum_convert_fusion
  66.7 0.1 copy.80
  66.9 0.8 copy.81
  67.7 0.0 all-gather.9.cloned.1.call-start
  67.8 0.6 broadcast_select_fusion
  68.4 0.1 multiply_cosine_fusion.1
  68.6 0.1 subtract_convert_fusion.2
  68.7 0.1 maximum_bitcast_fusion
  68.8 0.1 subtract_convert_fusion.1
  68.9 0.1 pad_maximum_fusion
  69.0 0.7 broadcast_and_fusion
  69.6 0.6 fusion.66
  70.2 0.8 fusion.75
  71.0 0.9 fusion.46
  71.9 0.1 fusion.61
  72.0 1.1 fusion.47
  73.1 0.9 copy.89
  74.0 0.2 all-reduce.3.cloned.1.call-start
  74.2 0.6 iota_compare_fusion.5
  74.8 12.5 %reshape.382 = bf16[4,4096,2,128]{3,2,1,0:T(2,128)(2,1)} reshape(bf16[4,4096,256]{2,1,0:T(8,128)(2,1)} %param.14) | data formatting | bytes 16777216 | tf_op jit(solution)/shard_map/reshape | solution.py:153
  87.3 12.7 %reshape.383 = bf16[4,4096,2,128]{3,2,1,0:T(2,128)(2,1)} reshape(bf16[4,4096,256]{2,1,0:T(8,128)(2,1)} %param.15) | data formatting | bytes 16777216 | tf_op jit(solution)/shard_map/reshape | solution.py:154
  100.1 6.5 %fusion.76 = (f32[4,4,2,4]{3,0,2,1:T(4,128)}, f32[4,4,2,4,4096]{4,3,0,2,1:T(4,128)S(1)}) fusion(bf16[4,4096,2,128,1]{3,2,1,0,4:T(2,128)(2,1)} %bitcast.125, bf16[4,4,2,4,128]{4,1,3,2,0:T(4,128)(2,1)S(1)} %pad_maximum_fusion, pred[4,4096]{1,0:T(4,128)(4,1)S(1)} %fusion.61), kind=kOutput, calls=%fused_computation.118 | convolution fusion | flops 135790464 | bytes 10535424 | tf_op jit(solution)/shard_map/srhgd,rchd->srhgc/dot_general | solution.py:63
  106.6 1.2 fusion.73
  107.8 3.2 %copy.122 = f32[512,2,4,64]{3,0,2,1:T(8,128)} copy(f32[512,2,4,64]{0,3,2,1:T(8,128)} %get-tuple-element.7) | data formatting | bytes 2097152
  110.9 2.0 copy.123
  112.9 2.8 %subtract_convert_fusion = (bf16[512,2,4,64]{3,0,2,1:T(8,128)(2,1)S(1)}, bf16[512,2,4,64]{3,0,2,1:T(8,128)(2,1)S(1)}) fusion(f32[512,2,4,64]{3,0,2,1:T(8,128)} %copy.123, f32[512,2,4,64]{3,0,2,1:T(8,128)} %copy.122, f32[512,64]{1,0:T(8,128)} %copy-done.3, f32[512,64]{1,0:T(8,128)S(1)} %get-tuple-element.16), kind=kLoop, calls=%fused_computation.33 | loop fusion | flops 2097152 | bytes 3407872 | tf_op jit(solution)/shard_map/convert.6
  115.8 1.3 fusion.42
  117.1 5.5 %fusion.74 = (f32[2,4,512]{2,1,0:T(4,128)S(1)}, f32[2,4,512,512]{2,3,1,0:T(8,128)}) fusion(f32[2,512,512,4]{2,1,3,0:T(8,128)S(1)} %fusion.42, pred[512,512]{0,1:T(8,128)(4,1)S(1)} %copy-done.8), kind=kOutput, calls=%fused_computation.116 | output fusion | flops 12583423 | bytes 17055744 | tf_op jit(solution)/shard_map/sub | solution.py:35
  122.6 5.5 %fusion.29 = bf16[2,128,4,512]{3,1,2,0:T(8,128)(2,1)} fusion(f32[2,4,512,512]{2,3,1,0:T(8,128)} %get-tuple-element.19, f32[2,4,512]{2,1,0:T(4,128)S(1)} %get-tuple-element.18, f32[512,2,6,128]{0,3,2,1:T(8,128)} %bitcast.129), kind=kOutput, calls=%fused_computation.34 | convolution fusion | flops 541589504 | bytes 9715712 | tf_op jit(solution)/shard_map/hgqk,khd->qhgd/dot_general | solution.py:116
  128.1 36.8 %all-gather.9.cloned.1.call-done = bf16[8,512,256]{2,1,0:T(8,128)(2,1)} async-done(((bf16[1,512,256]{2,1,0:T(8,128)(2,1)}), bf16[8,512,256]{2,1,0:T(8,128)(2,1)}) %all-gather.9.cloned.1.call-update) | async-done | bytes 2097168 | tf_op jit(solution)/shard_map/all_gather | solution.py:143
  165.0 3.9 %select_reduce_fusion = (bf16[512,256]{1,0:T(8,128)(2,1)}, bf16[512,256]{1,0:T(8,128)(2,1)S(1)}) fusion(bf16[8,512,256]{2,1,0:T(8,128)(2,1)} %all-gather.9.cloned.1.call-done, pred[8]{0:T(512)(128)(4,1)S(1)} %copy-done.16, bf16[8,512,256]{2,1,0:T(8,128)(2,1)} %all-gather.7.cloned.1.call-done), kind=kLoop, calls=%fused_computation.16 | loop fusion | flops 6029312 | bytes 4718600 | tf_op jit(solution)/shard_map/reduce_sum | solution.py:43
  168.9 0.1 copy.82
  169.0 0.3 fusion.77
  169.4 1.2 fusion.48
  170.6 1.3 divide_convert_fusion.2
  172.0 1.1 copy.90
  173.1 4.7 %fusion.32 = f32[4,4,2,4,128]{4,3,0,2,1:T(4,128)S(1)} fusion(bf16[4,4096,2,128,1]{3,2,1,0,4:T(2,128)(2,1)} %bitcast.124, bf16[4,4,2,4,4612]{4,3,0,2,1:T(4,128)(2,1)S(1)} %divide_convert_fusion.2), kind=kOutput, calls=%fused_computation.38 | convolution fusion | flops 134217728 | bytes 9502720 | tf_op jit(solution)/shard_map/srhgc,rchd->srhgd/dot_general | solution.py:76
  177.8 0.2 fusion.38
  178.1 0.1 fusion.39
  178.3 5.4 %fusion.11 = bf16[4,4,4096]{2,1,0:T(4,128)(2,1)} fusion(bf16[4,4,1024]{2,1,0:T(4,128)(2,1)S(1)} %dot_general.55, bf16[1024,4096]{1,0:T(8,128)(2,1)} %param.21), kind=kOutput, calls=%fused_computation.13 | convolution fusion | flops 134283264 | bytes 8552448 | tf_op jit(solution)/shard_map/dot_general | solution.py:178
  183.7 0.0 reduce-scatter.2.cloned.1.call-start
  183.8 9.5 %convolution_convert_fusion = bf16[512,4096]{1,0:T(8,128)(2,1)} fusion(bf16[512,1024]{0,1:T(8,128)(2,1)S(1)} %bitcast.140, bf16[1024,4096]{1,0:T(8,128)(2,1)} %param.21), kind=kOutput, calls=%fused_computation.11 | convolution fusion | flops 4297064448 | bytes 13631488 | tf_op jit(solution)/shard_map/dot_general | solution.py:120
  193.3 20.9 %all-reduce.3.cloned.1.call-done = bf16[4,4,4096]{2,1,0:T(4,128)(2,1)} async-done(((bf16[4,4,4096]{2,1,0:T(4,128)(2,1)}), bf16[4,4,4096]{2,1,0:T(4,128)(2,1)}) %all-reduce.3.cloned.1.call-update) | async-done | bytes 131088 | tf_op jit(solution)/shard_map/psum | solution.py:181
  214.2 1.6 fusion.52
  215.8 45.4 %reduce-scatter.2.cloned.1.call-done = bf16[128,4096]{1,0:T(8,128)(2,1)} async-done(((bf16[512,4096]{1,0:T(8,128)(2,1)}), bf16[128,4096]{1,0:T(8,128)(2,1)}) %reduce-scatter.2.cloned.1.call-update) | async-done | bytes 1048592 | tf_op jit(solution)/shard_map/reduce_scatter | solution.py:119
  261.2 2.4 fusion.40
  (58 shorter events, 0.3 us)
Async XLA Ops:
  7.2 4.8 %copy-start.18 = (u32[32]{0:T(128)S(1)}, u32[32]{0:T(128)}, u32[]{:S(2)}) copy-start(u32[32]{0:T(128)} %constant.44) | copy-start | bytes 388
  7.2 46.5 %all-gather.5.cloned.1.call-start = ((), (), s32[]{:S(2)}) async-start(), calls=%async_computation.1 | async-start | bytes 5242880 | tf_op jit(solution)/shard_map/all_gather | solution.py:103
  11.3 116.8 %all-gather.7.cloned.1.call-start = ((), (), s32[]{:S(2)}) async-start(), calls=%async_computation.3 | async-start | bytes 2359296 | tf_op jit(solution)/shard_map/all_gather | solution.py:142
  27.6 18.3 %copy-start.6 = (bf16[4,4,4096]{2,1,0:T(4,128)(2,1)S(1)}, bf16[4,4,4096]{2,1,0:T(4,128)(2,1)}, u32[]{:S(2)}) copy-start(bf16[4,4,4096]{2,1,0:T(4,128)(2,1)} %param.13) | copy-start | bytes 393220
  27.6 19.4 %copy-start.11 = (f32[4096]{0:T(1024)S(1)}, f32[4096]{0:T(1024)}, u32[]{:S(2)}) copy-start(f32[4096]{0:T(1024)} %param.19) | copy-start | bytes 49156
  47.1 19.2 %copy-start.3 = (f32[512,64]{1,0:T(8,128)}, f32[512,64]{1,0:T(8,128)S(1)}, u32[]{:S(2)}) copy-start(f32[512,64]{1,0:T(8,128)S(1)} %get-tuple-element.17) | copy-start | bytes 393220
  64.4 1.6 copy-start.1
  66.0 1.8 copy-start.15
  66.7 20.6 %copy-start.4 = (bf16[512,2,128]{2,0,1:T(8,128)(2,1)}, bf16[512,2,128]{2,0,1:T(8,128)(2,1)S(1)}, u32[]{:S(2)}) copy-start(bf16[512,2,128]{2,0,1:T(8,128)(2,1)S(1)} %maximum_convert_fusion) | copy-start | bytes 786436
  67.7 97.2 %all-gather.9.cloned.1.call-start = ((), (), s32[]{:S(2)}) async-start(), calls=%async_computation.4 | async-start | bytes 2359296 | tf_op jit(solution)/shard_map/all_gather | solution.py:143
  69.0 31.1 %copy-start.9 = (bf16[4,4,2,4,128]{4,1,3,2,0:T(4,128)(2,1)}, bf16[4,4,2,4,128]{4,1,3,2,0:T(4,128)(2,1)S(1)}, u32[]{:S(2)}) copy-start(bf16[4,4,2,4,128]{4,1,3,2,0:T(4,128)(2,1)S(1)} %pad_maximum_fusion) | copy-start | bytes 98308
  74.0 140.2 %all-reduce.3.cloned.1.call-start = ((), (), s32[]{:S(2)}) async-start(), calls=%async_computation.5 | async-start | bytes 262144 | tf_op jit(solution)/shard_map/psum | solution.py:181
  100.1 6.5 %copy-start.2 = (f32[512,1536]{0,1:T(8,128)S(1)}, f32[512,1536]{0,1:T(8,128)}, u32[]{:S(2)}) copy-start(f32[512,1536]{0,1:T(8,128)} %copy-done.1) | copy-start | bytes 9437188
  112.9 2.9 %copy-start.5 = (bf16[512,2,128]{2,0,1:T(8,128)(2,1)S(1)}, bf16[512,2,128]{2,0,1:T(8,128)(2,1)}, u32[]{:S(2)}) copy-start(bf16[512,2,128]{2,0,1:T(8,128)(2,1)} %copy-done.4) | copy-start | bytes 786436
  115.8 1.4 copy-start.8
  122.6 42.3 %copy-start.16 = (pred[8]{0:T(512)(128)(4,1)S(1)}, pred[8]{0:T(512)(128)(4,1)}, u32[]{:S(2)}) copy-start(pred[8]{0:T(512)(128)(4,1)} %iota_compare_fusion.5) | copy-start | bytes 28
  128.1 40.9 %copy-start.10 = (bf16[4,4,2,4,128]{4,1,3,2,0:T(4,128)(2,1)S(1)}, bf16[4,4,2,4,128]{4,1,3,2,0:T(4,128)(2,1)}, u32[]{:S(2)}) copy-start(bf16[4,4,2,4,128]{4,1,3,2,0:T(4,128)(2,1)} %copy-done.9) | copy-start | bytes 98308
  128.1 40.9 %copy-start.14 = (pred[4,512]{1,0:T(4,128)(4,1)S(1)}, pred[4,512]{1,0:T(4,128)(4,1)}, u32[]{:S(2)}) copy-start(pred[4,512]{1,0:T(4,128)(4,1)} %broadcast_and_fusion) | copy-start | bytes 6148
  128.1 41.3 %copy-start.12 = (f32[4,4,2,4]{3,0,2,1:T(4,128)S(1)}, f32[4,4,2,4]{3,0,2,1:T(4,128)}, u32[]{:S(2)}) copy-start(f32[4,4,2,4]{3,0,2,1:T(4,128)} %get-tuple-element.22) | copy-start | bytes 1540
  128.1 41.3 %copy-start.7 = (f32[4,4,2,4,4]{4,3,0,2,1:T(4,128)S(1)}, f32[4,4,2,4,4]{4,3,0,2,1:T(4,128)}, u32[]{:S(2)}) copy-start(f32[4,4,2,4,4]{4,3,0,2,1:T(4,128)} %get-tuple-element.21) | copy-start | bytes 6148
  173.1 5.0 %copy-start.13 = (bf16[4,4,2,128,1]{3,1,2,0,4:T(4,128)(2,1)S(1)}, bf16[4,4,2,128,1]{3,1,2,0,4:T(4,128)(2,1)}, u32[]{:S(2)}) copy-start(bf16[4,4,2,128,1]{3,1,2,0,4:T(4,128)(2,1)} %fusion.66) | copy-start | bytes 24580
  178.3 5.5 %copy-start.17 = (bf16[2,128,4,512]{3,1,2,0:T(8,128)(2,1)S(1)}, bf16[2,128,4,512]{3,1,2,0:T(8,128)(2,1)}, u32[]{:S(2)}) copy-start(bf16[2,128,4,512]{3,1,2,0:T(8,128)(2,1)} %fusion.29) | copy-start | bytes 3145732
  183.7 77.5 %reduce-scatter.2.cloned.1.call-start = ((), (), s32[]{:S(2)}) async-start(), calls=%async_computation.2 | async-start | bytes 5242880 | tf_op jit(solution)/shard_map/reduce_scatter | solution.py:119
  193.3 67.9 %copy-start = (bf16[1,128,4096]{2,1,0:T(8,128)(2,1)S(1)}, bf16[1,128,4096]{2,1,0:T(8,128)(2,1)}, u32[]{:S(2)}) copy-start(bf16[1,128,4096]{2,1,0:T(8,128)(2,1)} %param.11) | copy-start | bytes 3145732
Sparse Core Ops, SparseCore 0:
  11.4 37.1 all-gather.4
  67.8 47.2 all-gather.6
  117.3 47.6 all-gather.8
  183.8 30.3 all-reduce.2
  216.5 44.5 reduce-scatter.1
where the time goes:
time: 272 us; the launch traced here: 270 us
  waiting for transfers between devices  103 us (38%)
  local copies, waits for them, and re-layouts  56.5 us (21%)
  matrix products  51.7 us (19%)
  other arithmetic  29.2 us (11%)
  between operations  16.2 us (6%)
  blocking collectives  13 us (5%)
    reduce_scatter x1, waiting for transfers between devices, body(): lax.psum_scatter(jnp.dot(rows, w_out, preferred_element_type=f32).astype(...  45.4 us
    all_gather x1, waiting for transfers between devices, body(): lax.all_gather(packet[1], ('pool', 'batch'), axis=0, tiled=True)  36.8 us
    unnamed x45, local copies, waits for them, and re-layouts  25.2 us
    psum x1, waiting for transfers between devices, body(): lax.psum(partial_value.reshape(steps, rows, -1).astype(jnp.bfloat16), 'blk')  20.9 us
    all_gather x1, blocking collectives, body(): lax.all_gather(packet[2], ('pool', 'batch'), axis=0, tiled=True)  13 us
    reshape x1, local copies, waits for them, and re-layouts, body(): cache_value = cache_v.reshape(rows, cached, local, HEAD_DIM)  12.7 us
    reshape x1, local copies, waits for them, and re-layouts, body(): cache_key = cache_k.reshape(rows, cached, local, HEAD_DIM)  12.5 us
    dot_general x1, matrix products, body(): jnp.dot(lax.all_gather(normed, 'blk', axis=0, tiled=True), w_qkv, preferr...  10.7 us
  transfers between devices with their start and end apart: 5, of which 3 were waited for; matrix products, arithmetic and copies ran while one was open for 36% of the time, Pallas kernels for 0%

commit v1 on v0

v1 whole, which is shorter than its diff:
```python
import functools

import jax
import jax.numpy as jnp
import numpy as np
from jax import lax
from jax.experimental import pallas as pl
from jax.experimental.pallas import tpu as pltpu
from jax.sharding import PartitionSpec as P


HEAD_DIM = 128
GROUP = 4
KINDS = GROUP + 2
PAIR = 2 * HEAD_DIM
BLOCKS = KINDS // 2
EPSILON = 1e-05
THETA = 500000.0
NEG = -1e30
SCALE = HEAD_DIM ** (-0.5)
OUT_COLS = 1024
f32 = jnp.float32
bf16 = jnp.bfloat16


VMEM = pl.BlockSpec(memory_space=pltpu.MemorySpace.VMEM)
SMEM = pl.BlockSpec(memory_space=pltpu.MemorySpace.SMEM)
HBM = pl.BlockSpec(memory_space=pltpu.MemorySpace.HBM)
ANY = pl.BlockSpec(memory_space=pl.ANY)


def dot(a, b):
    return jnp.dot(a, b, preferred_element_type=f32)


def dot_t(a, b):
    return lax.dot_general(a, b, (((1,), (1,)), ((), ())), preferred_element_type=f32)


def rot(u, cosine, sine):
    return u * cosine + pltpu.roll(u, HEAD_DIM // 2, 1) * sine


def angle_tables(places):
    half = HEAD_DIM // 2
    freqs = THETA ** (-jnp.arange(half, dtype=f32) / half)
    angles = places.astype(f32)[..., None] * freqs
    cosine, sine = jnp.cos(angles), jnp.sin(angles)
    return jnp.concatenate([cosine, cosine], -1), jnp.concatenate([-sine, sine], -1)


def fixed_tables(count):
    half = HEAD_DIM // 2
    freqs = np.float32(THETA) ** (-np.arange(half, dtype=np.float32) / np.float32(half))
    angles = np.arange(count, dtype=np.float32)[:, None] * freqs.astype(np.float32)
    cosine, sine = np.cos(angles).astype(np.float32), np.sin(angles).astype(np.float32)
    return np.concatenate([cosine, cosine], -1), np.concatenate([-sine, sine], -1)


def norm_rows(src, dst, offset, gain_ref):
    rows = src.shape[0]

    def step(i, _):
        at = pl.multiple_of(i * 16, 16)
        wide = src[pl.ds(at, 16), :].astype(f32)
        factor = lax.rsqrt(jnp.mean(wide * wide, axis=-1, keepdims=True) + EPSILON)
        to = pl.multiple_of(offset + i * 16, 16)
        dst[pl.ds(to, 16), :] = (wide * factor * gain_ref[...]).astype(bf16)
        return 0

    lax.fori_loop(0, rows // 16, step, 0, unroll=2)


def weight_copies(w_hbm, w_vmem, sems, width):
    return [
        pltpu.make_async_copy(
            w_hbm.at[:, pl.ds(j * width, width)], w_vmem.at[j], sems.at[j]
        )
        for j in range(w_vmem.shape[0])
    ]


def rotated_pair(acc, cosine, sine, j):
    cosine, sine = cosine[...], sine[...]
    first = rot(acc[:, :HEAD_DIM], cosine, sine)
    second = acc[:, HEAD_DIM:]
    if j % BLOCKS != BLOCKS - 1:
        second = rot(second, cosine, sine)
    return jnp.concatenate([first, second], axis=1).astype(bf16)


def load(pairs, sems):
    copies = [pltpu.make_async_copy(src, dst, sems.at[i]) for i, (src, dst) in enumerate(pairs)]
    for copy in copies:
        copy.start()
    return copies


def norm_token_rows(parts, gain_ref):
    out = []
    for part in parts:
        wide = part.astype(f32)
        factor = lax.rsqrt(jnp.mean(wide * wide, axis=-1, keepdims=True) + EPSILON)
        out.append(wide * factor * gain_ref[...])
    return jnp.concatenate(out, axis=0).astype(bf16)


def first_kernel(
    idx, own_hbm, sib_hbm, dec_hbm, gain_hbm, cos_hbm, sin_hbm, wq_hbm, wo_hbm,
    _a, _b, _c, _d, _e, own_out, sib_out, raw_out, wq, wo, later_hbm,
    own, sib, dec, gain, tabs, normed, q_sems, o_sems, in_sems, later_sem,
):
    rows = own.shape[0]
    steps, decs = dec.shape[:2]
    at = [pl.ds(pl.multiple_of(idx[i] * rows, rows), rows) for i in range(2)]
    weights = weight_copies(wq_hbm, wq, q_sems, PAIR) + weight_copies(wo_hbm, wo, o_sems, OUT_COLS)
    ready = load([(gain_hbm, gain), (own_hbm, own), (dec_hbm, dec), (sib_hbm, sib)], in_sems)
    for i in range(2):
        ready += load(
            [(cos_hbm.at[at[i]], tabs.at[2 * i]), (sin_hbm.at[at[i]], tabs.at[2 * i + 1])],
            in_sems.at[pl.ds(4 + 2 * i, 2)],
        )
    weights[0].start()
    ready[0].wait()
    ready[1].wait()
    through = pltpu.make_async_copy(own, later_hbm, later_sem)
    through.start()
    weights[1].start()
    norm_rows(own, normed, 0, gain)
    ready[2].wait()
    normed[2 * rows :] = norm_token_rows([dec[s] for s in range(steps)], gain)
    ready[3].wait()
    weights[2].start()
    norm_rows(sib, normed, rows, gain)
    for copy in ready[4:]:
        copy.wait()
    for j in range(wq.shape[0]):
        weights[j].wait()
        if j + 3 < len(weights):
            weights[j + 3].start()
        acc = dot(normed[...], wq[j])
        own_out[j] = rotated_pair(acc[:rows], tabs.at[0], tabs.at[1], j)
        sib_out[j] = rotated_pair(acc[rows : 2 * rows], tabs.at[2], tabs.at[3], j)
        for r in range(decs):
            for s in range(steps):
                row = 2 * rows + s * decs + r
                raw_out[r, j, s : s + 1] = acc[row : row + 1]
    for j in range(wq.shape[0], len(weights)):
        weights[j].wait()
        if j + 3 < len(weights):
            weights[j + 3].start()
    through.wait()


def own_tail(q, k_own, steps):
    s = dot_t(q, k_own) * SCALE
    at = lax.broadcasted_iota(jnp.int32, s.shape, 0)
    t = lax.broadcasted_iota(jnp.int32, s.shape, 1)
    return jnp.where(t <= lax.rem(at, steps), s, NEG)


def stacked_queries(raw, h, cosine, sine):
    parts = []
    for g in range(GROUP):
        block = raw(h * BLOCKS + g // 2)
        parts.append(rot(block[:, (g % 2) * HEAD_DIM : (g % 2 + 1) * HEAD_DIM], cosine, sine))
    return jnp.concatenate(parts, axis=0).astype(bf16)


def own_pair(raw, h, cosine, sine, pad):
    block = raw(h * BLOCKS + BLOCKS - 1)
    key = rot(block[:, :HEAD_DIM], cosine, sine)
    fill = jnp.zeros((pad - key.shape[0], HEAD_DIM), f32)
    key = jnp.concatenate([key, fill], axis=0).astype(bf16)
    value = jnp.concatenate([block[:, HEAD_DIM:], fill], axis=0).astype(bf16)
    return key, value


def decode_kernel(
    lens, slot, raw_ref, cos_ref, sin_ref, k_hbm, v_hbm,
    out_ref, k_s, v_s, q_s, ko_s, vo_s, m_s, l_s, acc_s, k_sem, v_sem,
):
    n_rows, count, width = k_s.shape[:3]
    steps = raw_ref.shape[2]
    heads = k_s.shape[3] // HEAD_DIM
    many = GROUP * steps

    def copies(r, j):
        at = pl.ds(j * width, width)
        return (
            pltpu.make_async_copy(k_hbm.at[r, at], k_s.at[r, j], k_sem.at[r, j]),
            pltpu.make_async_copy(v_hbm.at[r, at], v_s.at[r, j], v_sem.at[r, j]),
        )

    def live(r, j):
        return (j * width < lens[r]) & (slot[0, 0] != r)

    def fetch(r):
        for j in range(count):

            @pl.when(live(r, j))
            def _(r=r, j=j):
                for copy in copies(r, j):
                    copy.start()

    for r in range(min(2, n_rows)):
        fetch(r)
    for r in range(n_rows):
        raw = lambda b, r=r: raw_ref[r, b]
        q_s[r] = jnp.zeros_like(q_s[r])
        for h in range(heads):
            lanes = slice(h * HEAD_DIM, (h + 1) * HEAD_DIM)
            q_s[r, h * many : (h + 1) * many, lanes] = stacked_queries(raw, h, cos_ref[r], sin_ref[r])
            key, value = own_pair(raw, h, cos_ref[r], sin_ref[r], ko_s.shape[1])
            ko_s[r, :, lanes] = key
            vo_s[r, :, lanes] = value
    for r in range(n_rows):
        s = own_tail(q_s[r], ko_s[r], steps)
        m = jnp.max(s, axis=-1, keepdims=True)
        e = jnp.exp(s - m)
        m_s[r] = m
        l_s[r] = jnp.sum(e, axis=-1, keepdims=True)
        acc_s[r] = dot(e.astype(bf16), vo_s[r])

    for r in range(n_rows):
        for j in range(count):

            @pl.when(live(r, j))
            def _(r=r, j=j):
                k_copy, v_copy = copies(r, j)
                k_copy.wait()
                s = dot_t(q_s[r], k_s[r, j]) * SCALE
                at = j * width + lax.broadcasted_iota(jnp.int32, s.shape, 1)
                s = jnp.where(at < lens[r], s, NEG)
                m = jnp.maximum(m_s[r], jnp.max(s, axis=-1, keepdims=True))
                fade = jnp.exp(m_s[r] - m)
                e = jnp.exp(s - m)
                m_s[r] = m
                l_s[r] = l_s[r] * fade + jnp.sum(e, axis=-1, keepdims=True)
                v_copy.wait()
                acc_s[r] = acc_s[r] * fade + dot(e.astype(bf16), v_s[r, j])

        if r + 2 < n_rows:
            fetch(r + 2)

    for r in range(n_rows):
        mixed = acc_s[r] / l_s[r]
        for h in range(heads):
            for g in range(GROUP):
                to = (h * GROUP + g) * HEAD_DIM
                for s in range(steps):
                    at = h * many + g * steps + s
                    row = s * n_rows + r
                    out_ref[row : row + 1, to : to + HEAD_DIM] = mixed[
                        at : at + 1, h * HEAD_DIM : (h + 1) * HEAD_DIM
                    ]


def attend(queries, q_shard, pieces, plen, out_ref, offset, heads):
    for h in range(heads):
        parts = []
        for g in range(GROUP):
            block = queries(h * BLOCKS + g // 2)
            parts.append(block[:, (g % 2) * HEAD_DIM : (g % 2 + 1) * HEAD_DIM])
        rows = parts[0].shape[0]
        q = jnp.concatenate(parts, axis=0)
        q_at = q_shard * rows + lax.rem(lax.broadcasted_iota(jnp.int32, (GROUP * rows, 1), 0), rows)
        scores, values = [], []
        for kv, shard in pieces:
            pair = kv(h)
            count = pair.shape[0]
            k_at = shard * count + lax.broadcasted_iota(jnp.int32, (1, count), 1)
            k_at = jnp.where(k_at < plen, k_at, jnp.int32(1 << 30))
            s = dot_t(q, pair[:, :HEAD_DIM]) * SCALE
            scores.append(jnp.where(k_at <= q_at, s, NEG))
            values.append(pair[:, HEAD_DIM:])
        top = functools.reduce(jnp.maximum, scores)
        top = jnp.max(top, axis=-1, keepdims=True)
        total, mixed = None, None
        for s, value in zip(scores, values):
            e = jnp.exp(s - top)
            total = e if total is None else total + e
            term = dot(e.astype(bf16), value)
            mixed = term if mixed is None else mixed + term
        mixed = (mixed / jnp.sum(total, axis=-1, keepdims=True)).astype(bf16)
        for g in range(GROUP):
            to = (h * GROUP + g) * HEAD_DIM
            out_ref[offset : offset + rows, to : to + HEAD_DIM] = mixed[g * rows : (g + 1) * rows]


def attend_new(raw, cosine, sine, pieces, plen, out_ref, heads, steps):
    spread = out_ref.shape[0] // steps
    for h in range(heads):
        q = stacked_queries(raw, h, cosine, sine)
        key, value = own_pair(raw, h, cosine, sine, 16)
        scores, values = [own_tail(q, key, steps)], [value]
        for kv, shard in pieces:
            pair = kv(h)
            count = pair.shape[0]
            k_at = shard * count + lax.broadcasted_iota(jnp.int32, (1, count), 1)
            s = dot_t(q, pair[:, :HEAD_DIM]) * SCALE
            scores.append(jnp.where(k_at < plen, s, NEG))
            values.append(pair[:, HEAD_DIM:])
        top = functools.reduce(jnp.maximum, [jnp.max(s, axis=-1, keepdims=True) for s in scores])
        total, mixed = 0.0, 0.0
        for s, v in zip(scores, values):
            e = jnp.exp(s - top)
            total = total + jnp.sum(e, axis=-1, keepdims=True)
            mixed = mixed + dot(e.astype(bf16), v)
        mixed = mixed / total
        for g in range(GROUP):
            to = (h * GROUP + g) * HEAD_DIM
            rows = [
                jnp.broadcast_to(mixed[g * steps + s : g * steps + s + 1], (spread, HEAD_DIM))
                for s in range(steps)
            ]
            out_ref[:, to : to + HEAD_DIM] = jnp.concatenate(rows, axis=0).astype(bf16)


def chunk_kernel(which, n_full, n_kv, n_ask, answers, kv_only, *refs):
    refs = list(refs)
    take = lambda n: [refs.pop(0) for _ in range(n)]
    idx, plen, there, passed, gain_hbm, cos_hbm, sin_hbm, wq, wo = take(9)
    full, kvs, asks = take(n_full), take(n_kv), take(n_ask)
    new_raw, new_cos, new_sin = take(3) if answers else (None,) * 3
    take(1)
    kv_out = take(1)[0]
    part_out = None if kv_only else take(1)[0]
    raw_out = take(1)[0] if n_ask else None
    new_out = take(1)[0] if answers else None
    x, gain, tabs, normed, qkv, in_sem = take(6)
    attn = None if kv_only else take(1)[0]
    rows = x.shape[0]
    heads = kv_out.shape[0]
    shard = idx[which]
    at = pl.ds(pl.multiple_of(shard * rows, rows), rows)
    direct = lax.rem(idx[0], 2) == (which - n_full) % 2

    @pl.when(direct)
    def _():
        pltpu.make_async_copy(there, x, in_sem.at[0]).start()

    @pl.when(jnp.logical_not(direct))
    def _():
        pltpu.make_async_copy(passed, x, in_sem.at[0]).start()

    gain_copy = pltpu.make_async_copy(gain_hbm, gain, in_sem.at[1])
    gain_copy.start()
    tab_copies = [
        pltpu.make_async_copy(cos_hbm.at[at], tabs.at[0], in_sem.at[2]),
        pltpu.make_async_copy(sin_hbm.at[at], tabs.at[1], in_sem.at[3]),
    ]
    for copy in tab_copies:
        copy.start()
    gain_copy.wait()
    if n_ask:
        here = idx[idx.shape[0] - 1].astype(f32)
        steps = asks[0].shape[0] // 2
        new = jnp.zeros((steps, x.shape[1]), f32)
        for ref in asks:
            wide = ref[...].astype(f32)
            new = jnp.where(wide[steps : steps + 1] == here, wide[:steps], new)
        fill = jnp.zeros((16 - steps, x.shape[1]), f32)
        normed[rows:] = norm_token_rows([new, fill], gain)
    pltpu.make_async_copy(there, x, in_sem.at[0]).wait()
    norm_rows(x, normed, 0, gain)
    for copy in tab_copies:
        copy.wait()

    for j in range(wq.shape[0]):
        acc = dot(normed[...], wq[j])
        qkv[j] = rotated_pair(acc[:rows], tabs.at[0], tabs.at[1], j)
        if n_ask:
            raw_out[j] = acc[rows : rows + raw_out.shape[1]]
    for h in range(heads):
        kv_out[h] = qkv[h * BLOCKS + BLOCKS - 1]
    if kv_only:
        return
    pieces = [(lambda h, ref=ref: ref[h * BLOCKS + BLOCKS - 1], idx[i]) for i, ref in enumerate(full)]
    pieces += [(lambda h, ref=ref: ref[h], at) for ref, at in zip(kvs, kv_places(idx, which, n_full, n_kv))]
    pieces += [(lambda h: qkv[h * BLOCKS + BLOCKS - 1], shard)]
    if answers:
        steps = new_cos.shape[0]
        raw = lambda b: new_raw[b, :steps]
        attend_new(raw, new_cos[...], new_sin[...], pieces, plen[0, 0], new_out, heads, steps)
    attend(lambda b: qkv[b], shard, pieces, plen[0, 0], attn, 0, heads)

    for j in range(wo.shape[0]):
        part_out[:, j * OUT_COLS : (j + 1) * OUT_COLS] = dot(attn[...], wo[j]).astype(bf16)


def kv_places(idx, which, first, count):
    others = [i for i in range(first, first + count + 1) if i != which]
    return [idx[i] for i in others[:count]]


def last_kernel(n_kv, n_ret, n_rows, *refs):
    refs = list(refs)
    take = lambda n: [refs.pop(0) for _ in range(n)]
    idx, plen, slot, assign, own, sib = take(6)
    kvs = take(n_kv)
    dec, = take(1)
    rets = take(n_ret)
    wo, own_part, sib_part, dec_part, attn = take(5)
    rows = own.shape[1]
    heads = kvs[0].shape[0]
    pieces = [(lambda h, ref=ref: ref[h * BLOCKS + BLOCKS - 1], idx[i]) for i, ref in enumerate((own, sib))]
    pieces += [(lambda h, ref=ref: ref[h], idx[2 + i]) for i, ref in enumerate(kvs)]
    for i, ref in enumerate((own, sib)):
        attend(lambda b, ref=ref: ref[b], idx[i], pieces, plen[0, 0], attn, i * rows, heads)
    pick = lax.rem(idx[idx.shape[0] - 1] - assign[0, 0] + n_ret, n_ret)
    new = rets[0][...].astype(f32)
    for k in range(1, n_ret):
        new = jnp.where(pick == k, rets[k][...].astype(f32), new)
    at = lax.rem(lax.broadcasted_iota(jnp.int32, dec.shape, 0), n_rows)
    attn[2 * rows :] = jnp.where(at == slot[0, 0], new, dec[...]).astype(bf16)
    for j in range(wo.shape[0]):
        part = dot(attn[...], wo[j]).astype(bf16)
        cols = slice(j * OUT_COLS, (j + 1) * OUT_COLS)
        own_part[:, cols] = part[:rows]
        sib_part[:, cols] = part[rows:]
        dec_part[:, cols] = part[2 * rows :]


def add_kernel(start, a, b, out):
    rows = out.shape[0]

    def step(i, _):
        at = pl.ds(pl.multiple_of(i * 16, 16), 16)
        to = pl.ds(pl.multiple_of(start + i * 16, 16), 16)
        out[at, :] = (a[at, :].astype(f32) + b[to, :].astype(f32)).astype(bf16)
        return 0

    lax.fori_loop(0, rows // 16, step, 0)


def base_kernel(shard_hbm, own, sib, out, shard, sem):
    copy = pltpu.make_async_copy(shard_hbm, shard, sem)
    copy.start()
    copy.wait()

    def step(i, _):
        at = pl.ds(pl.multiple_of(i * 16, 16), 16)
        out[at, :] = shard[at, :].astype(f32) + own[at, :].astype(f32) + sib[at, :].astype(f32)
        return 0

    lax.fori_loop(0, out.shape[0] // 16, step, 0)


def sum_kernel(count, idx, base, *refs):
    parts, out, got, sems, out_sem = refs[: 2 * count], *refs[2 * count :]
    pieces = sems.shape[1]
    rows = out.shape[0] // pieces
    core = lax.rem(idx[0], 2)
    for k in range(2):

        @pl.when(core == k)
        def _(k=k):
            for n in range(pieces):
                at = pl.ds(n * rows, rows)
                for d in range(count):
                    pltpu.make_async_copy(parts[2 * d + k].at[at], got.at[d, at], sems.at[d, n]).start()

    done = []
    for n in range(pieces):
        at = slice(n * rows, (n + 1) * rows)
        total = base[at]
        for d in range(count):
            pltpu.make_async_copy(parts[2 * d].at[pl.ds(n * rows, rows)], got.at[d, at], sems.at[d, n]).wait()
            total = total + got[d, at].astype(f32)
        got[0, at] = total.astype(bf16)
        done.append(pltpu.make_async_copy(got.at[0, at], out.at[pl.ds(n * rows, rows)], out_sem.at[n]))
        done[-1].start()
    for copy in done:
        copy.wait()


def dec_kernel(tokens, a, b, out):
    steps, n_rows = tokens.shape[:2]
    total = a[...].astype(f32) + b[...].astype(f32)
    for s in range(steps):
        rows = total[s * n_rows : (s + 1) * n_rows]
        out[s] = (tokens[s].astype(f32) + rows).astype(bf16)


def params(mib):
    return pltpu.CompilerParams(vmem_limit_bytes=mib << 20)


def layer(
    prompt, prompt_len, dec_tokens, cache_k, cache_v, cache_len, assign, slot, gain, w_qkv, w_out
):
    n_blk, n_pool, n_batch = lax.axis_size("blk"), lax.axis_size("pool"), lax.axis_size("batch")
    n_chip = n_blk // 2
    shard = prompt[0]
    rows, width = shard.shape
    steps, n_rows = dec_tokens.shape[:2]
    heads = w_qkv.shape[1] // (KINDS * HEAD_DIM)
    blocks = heads * BLOCKS
    attn_cols = heads * GROUP * HEAD_DIM
    out_blocks = width // OUT_COLS
    decs = steps * n_rows

    blk = lax.axis_index("blk")
    chip, core = blk // 2, blk % 2
    batch = lax.axis_index("batch")
    at = jnp.arange(n_blk + 1, dtype=jnp.int32)
    far = (chip + n_chip - at // 2) % n_chip
    idx = jnp.where(at < 2, 2 * chip + (core + at) % 2, 2 * far + at % 2)
    idx = jnp.where(at == n_blk, batch, idx).astype(jnp.int32)
    gain_row = gain.reshape(1, width)
    cos_t, sin_t = (jnp.asarray(t) for t in fixed_tables(n_blk * rows))
    place = cache_len[:, None] + jnp.arange(steps, dtype=jnp.int32)[None, :]
    dec_cos, dec_sin = angle_tables(place)
    new_cos, new_sin = angle_tables(prompt_len[0, 0] + jnp.arange(steps, dtype=jnp.int32))

    swap = [(i, i ^ 1) for i in range(n_blk)]
    hop = lambda k, d: [(2 * c + k, 2 * ((c + d) % n_chip) + k) for c in range(n_chip)]
    toward = lambda k: [(2 * c + 1 - k, 2 * c + k) for c in range(n_chip)]
    shift = [
        [
            (p * n_batch + b, ((p + n_pool // 2) % n_pool) * n_batch + (b + k) % n_batch)
            for p in range(n_pool)
            for b in range(n_batch)
        ]
        for k in range(n_batch)
    ]
    groups = ("pool", "batch")
    near = lambda x: pltpu.with_memory_space_constraint(x, pltpu.MemorySpace.VMEM)
    stay = lambda x: pltpu.with_memory_space_constraint(x, pltpu.MemorySpace.HBM)

    row = lax.dynamic_index_in_dim(dec_tokens, slot[0, 0], 1, keepdims=False)
    wanted = jnp.full((steps, width), assign[0, 0]).astype(bf16)
    ask = jnp.concatenate([row, wanted], axis=0)
    sib_x = lax.ppermute(shard, "blk", swap)
    order = [(d, k) for d in range(1, n_chip) for k in range(2)]
    far_x = {}
    for d, k in order:
        if k == 0:
            far_x[d, k] = lax.ppermute(shard, "blk", hop(k, d))
    asks = [lax.ppermute(ask, groups, perm) for perm in shift]

    own, sib, raw, wq, wo, shard_later = pl.pallas_call(
        first_kernel,
        in_specs=[SMEM] + [HBM] * 8 + [ANY] * 5,
        out_specs=[VMEM] * 5 + [HBM],
        out_shape=[
            jax.ShapeDtypeStruct((blocks, rows, PAIR), bf16),
            jax.ShapeDtypeStruct((blocks, rows, PAIR), bf16),
            jax.ShapeDtypeStruct((n_rows, blocks, steps, PAIR), f32),
            pltpu.VMEM((blocks, width, PAIR), bf16),
            pltpu.VMEM((out_blocks, attn_cols, OUT_COLS), bf16),
            jax.ShapeDtypeStruct((rows, width), bf16),
        ],
        scratch_shapes=[
            pltpu.VMEM((rows, width), bf16),
            pltpu.VMEM((rows, width), bf16),
            pltpu.VMEM((steps, n_rows, width), bf16),
            pltpu.VMEM((1, width), f32),
            pltpu.VMEM((4, rows, HEAD_DIM), f32),
            pltpu.VMEM((2 * rows + decs, width), bf16),
            pltpu.SemaphoreType.DMA((blocks,)),
            pltpu.SemaphoreType.DMA((out_blocks,)),
            pltpu.SemaphoreType.DMA((8,)),
            pltpu.SemaphoreType.DMA,
        ],
        compiler_params=params(10),
        name="first",
    )(
        idx, stay(shard), sib_x, stay(dec_tokens), stay(gain_row), stay(cos_t), stay(sin_t),
        stay(w_qkv), stay(w_out), ask, dec_cos, dec_sin, new_cos, new_sin,
    )
    for d, k in order:
        if k == 1:
            far_x[d, k] = lax.ppermute(shard_later, "blk", hop(k, d))

    cached = cache_k.shape[1]
    step_rows = min(2048, cached)
    count = cached // step_rows
    kv_width = heads * HEAD_DIM
    many = GROUP * steps * heads
    dec_attn = pl.pallas_call(
        decode_kernel,
        in_specs=[SMEM] * 2 + [VMEM] * 3 + [HBM] * 2,
        out_specs=VMEM,
        out_shape=jax.ShapeDtypeStruct((decs, attn_cols), f32),
        scratch_shapes=[
            pltpu.VMEM((n_rows, count, step_rows, kv_width), bf16),
            pltpu.VMEM((n_rows, count, step_rows, kv_width), bf16),
            pltpu.VMEM((n_rows, many, kv_width), bf16),
            pltpu.VMEM((n_rows, 16, kv_width), bf16),
            pltpu.VMEM((n_rows, 16, kv_width), bf16),
            pltpu.VMEM((n_rows, many, 1), f32),
            pltpu.VMEM((n_rows, many, 1), f32),
            pltpu.VMEM((n_rows, many, kv_width), f32),
            pltpu.SemaphoreType.DMA((n_rows, count)),
            pltpu.SemaphoreType.DMA((n_rows, count)),
        ],
        compiler_params=params(20),
        name="decode",
    )(cache_len, slot, raw, dec_cos, dec_sin, stay(cache_k), stay(cache_v))

    def chunk(i, k, x, kvs, asks, answer, turn, kv_only):
        passed = lax.ppermute(x, "blk", [(b, a) for a, b in toward(k)])
        outs = [jax.ShapeDtypeStruct((heads, rows, PAIR), bf16)]
        tall = rows + (16 if asks else 0)
        scratch = [
            pltpu.VMEM((rows, width), bf16),
            pltpu.VMEM((1, width), f32),
            pltpu.VMEM((2, rows, HEAD_DIM), f32),
            pltpu.VMEM((tall, width), bf16),
            pltpu.VMEM((blocks, rows, PAIR), bf16),
            pltpu.SemaphoreType.DMA((4,)),
        ]
        if not kv_only:
            outs.append(jax.ShapeDtypeStruct((rows, width), bf16))
            scratch.append(pltpu.VMEM((rows, attn_cols), bf16))
        if asks:
            outs.append(jax.ShapeDtypeStruct((blocks, 8, PAIR), f32))
        if answer:
            outs.append(jax.ShapeDtypeStruct((decs, attn_cols), bf16))
        kernel = functools.partial(
            chunk_kernel, i, 2, len(kvs), len(asks), bool(answer), kv_only
        )
        extra = [*kvs, *asks, *answer]
        return pl.pallas_call(
            kernel,
            in_specs=[SMEM] * 2 + [HBM] * 5 + [VMEM] * (4 + len(extra)) + [ANY],
            out_specs=[VMEM] * len(outs),
            out_shape=outs,
            scratch_shapes=scratch,
            compiler_params=params(12),
            name="chunk",
        )(
            idx, prompt_len, x, passed, stay(gain_row), stay(cos_t), stay(sin_t),
            near(wq), near(wo), own, sib, *extra, turn,
        )

    def add(a, b, start=0):
        return pl.pallas_call(
            functools.partial(add_kernel, start),
            in_specs=[VMEM] * 2,
            out_specs=VMEM,
            out_shape=jax.ShapeDtypeStruct(a.shape, bf16),
            compiler_params=params(8),
            name="add",
        )(a, b)

    kvs, back = [], []
    ahead = n_chip > 2
    if ahead:
        kvs = [
            chunk(2 + i, k, far_x[d, k], [], [], [], gain_row, True)[0]
            for i, (d, k) in enumerate(order)
        ]
    turn, new_raw, fresh = gain_row, None, None
    for i, (d, k) in enumerate(order):
        final = i == len(order) - 1
        others = [kv for n, kv in enumerate(kvs) if n != i]
        outs = chunk(
            2 + i, k, far_x[d, k], others, asks if i == 0 else [],
            [new_raw, new_cos, new_sin] if final else [], turn, False,
        )
        if not ahead:
            kvs.append(outs[0])
        if i == 0:
            new_raw = outs[2]
        if final:
            fresh = outs[-1]
        other = lax.ppermute(outs[1], "blk", toward(k))
        turn = add(outs[1], other)
        back.append(lax.ppermute(turn, "blk", hop(k, n_chip - d)))

    rets = [lax.ppermute(fresh, groups, perm) for perm in shift]
    own_part, sib_part, dec_part = pl.pallas_call(
        functools.partial(last_kernel, len(kvs), n_batch, n_rows),
        in_specs=[SMEM] * 4 + [VMEM] * (4 + len(kvs) + n_batch),
        out_specs=[VMEM] * 3,
        out_shape=[
            jax.ShapeDtypeStruct((rows, width), bf16),
            jax.ShapeDtypeStruct((rows + decs, width), bf16),
            jax.ShapeDtypeStruct((decs, width), bf16),
        ],
        scratch_shapes=[
            pltpu.VMEM((2 * rows + decs, attn_cols), bf16),
        ],
        compiler_params=params(12),
        name="last",
    )(idx, prompt_len, slot, assign, own, sib, *kvs, dec_attn, *rets, near(wo))
    from_sib = lax.ppermute(sib_part, "blk", swap)

    total = add(dec_part, from_sib, rows)
    reach = 1
    while reach < n_chip:
        other = lax.ppermute(total, "blk", [(i, i ^ (2 * reach)) for i in range(n_blk)])
        reach *= 2
        if reach < n_chip:
            total = add(total, other)
    dec_out = pl.pallas_call(
        dec_kernel,
        in_specs=[VMEM] * 3,
        out_specs=VMEM,
        out_shape=jax.ShapeDtypeStruct(dec_tokens.shape, bf16),
        compiler_params=params(8),
        name="dec",
    )(dec_tokens, total, other)
    base = pl.pallas_call(
        base_kernel,
        in_specs=[HBM, VMEM, VMEM],
        out_specs=VMEM,
        out_shape=jax.ShapeDtypeStruct((rows, width), f32),
        scratch_shapes=[pltpu.VMEM((rows, width), bf16), pltpu.SemaphoreType.DMA],
        compiler_params=params(8),
        name="base",
    )(stay(shard), own_part, from_sib)
    pieces = 4
    result = pl.pallas_call(
        functools.partial(sum_kernel, n_chip - 1),
        in_specs=[SMEM, VMEM] + [HBM] * len(back),
        out_specs=HBM,
        out_shape=jax.ShapeDtypeStruct((rows, width), bf16),
        scratch_shapes=[
            pltpu.VMEM((n_chip - 1, rows, width), bf16),
            pltpu.SemaphoreType.DMA((n_chip - 1, pieces)),
            pltpu.SemaphoreType.DMA((pieces,)),
        ],
        compiler_params=params(10),
        name="sum",
    )(idx, base, *back)
    return (result[None], dec_out)


def solution(mesh):
    return jax.shard_map(
        layer,
        mesh=mesh,
        in_specs=(
            P(("pool", "batch"), "blk", None),
            P("pool", "batch"),
            P(None, ("pool", "batch"), None),
            P(("pool", "batch"), None, "blk"),
            P(("pool", "batch"), None, "blk"),
            P(("pool", "batch")),
            P("pool", "batch"),
            P("pool", "batch"),
            P(),
            P(None, "blk"),
            P("blk", None),
        ),
        out_specs=(P(("pool", "batch"), "blk", None), P(None, ("pool", "batch"), None)),
        check_vma=False,
    )
```

time: 272 us -> 124 us (0.46)
  waiting for transfers between devices: 103 us -> 38.3 us
  local copies, waits for them, and re-layouts: 56.5 us -> 1.05 us
  matrix products: 51.7 us -> 0 us
  Pallas kernels: 0 us -> 46.8 us
  starting transfers between devices: 0.39 us -> 32.1 us
  other arithmetic: 29.2 us -> 1.18 us
  between operations: 16.2 us -> 3.06 us
  blocking collectives: 13 us -> 0 us
    dot_general x12 -> x0, matrix products: 51.7 us -> none  [the longest x1 10.7 us: body(): jnp.dot(lax.all_gather(normed, 'blk', axis=0, tiled=True), w_qkv, preferr...]
    pallas_call x0 -> x11, Pallas kernels: none -> 46.8 us  [the longest x2 13.9 us: chunk(): pl.pallas_call(kernel, in_specs=[SMEM] * 2 + [HBM] * 5 + [VMEM] * (4 + le...]
    reduce_scatter x1 -> x0, waiting for transfers between devices: 45.4 us -> none  [body(): lax.psum_scatter(jnp.dot(rows, w_out, preferred_element_type=f32).astype(...]
    ppermute x0 -> x19, waiting for transfers between devices: none -> 38.3 us  [the longest x1 23.5 us: layer(): lax.ppermute(total, 'blk', [(i, i ^ 2 * reach) for i in range(n_blk)])]
    all_gather x3 -> x0, waiting for transfers between devices: 36.9 us -> none  [the longest x1 36.8 us: body(): lax.all_gather(packet[1], ('pool', 'batch'), axis=0, tiled=True)]
    ppermute x0 -> x19, starting transfers between devices: none -> 32.1 us  [the longest x4 9.41 us: layer(): asks = [lax.ppermute(ask, groups, perm) for perm in shift]]
    reshape x2 -> x0, local copies, waits for them, and re-layouts: 25.3 us -> none  [the longest x1 12.7 us: body(): cache_value = cache_v.reshape(rows, cached, local, HEAD_DIM)]
    unnamed x45 -> x5, local copies, waits for them, and re-layouts: 25.2 us -> 0.06 us
  transfers between devices with their start and end apart: 5 -> 19, of which waited for: 3 -> 6; matrix products, arithmetic and copies ran while one was open for 36% -> 2% of each run, Pallas kernels for 0% -> 31%
where the time goes in v1:
time: 124 us; the launch traced here: 122 us
  Pallas kernels  46.8 us (38%)
  waiting for transfers between devices  38.3 us (31%)
  starting transfers between devices  32.1 us (26%)
  between operations  3.06 us (2%)
    ppermute x1, waiting for transfers between devices, layer(): lax.ppermute(total, 'blk', [(i, i ^ 2 * reach) for i in range(n_blk)])  23.5 us
    pallas_call x2, Pallas kernels, chunk(): pl.pallas_call(kernel, in_specs=[SMEM] * 2 + [HBM] * 5 + [VMEM] * (4 + le...  13.9 us
    pallas_call x1, Pallas kernels, layer(): pl.pallas_call(first_kernel, in_specs=[SMEM] + [HBM] * 8 + [ANY] * 5, out...  13.5 us
    pallas_call x1, Pallas kernels, layer(): pl.pallas_call(decode_kernel, in_specs=[SMEM] * 2 + [VMEM] * 3 + [HBM] *...  9.59 us
    ppermute x4, starting transfers between devices, layer(): asks = [lax.ppermute(ask, groups, perm) for perm in shift]  9.41 us
    ppermute x1, waiting for transfers between devices, layer(): far_x[d, k] = lax.ppermute(shard, 'blk', hop(k, d))  8.73 us
    ppermute x4, starting transfers between devices, layer(): rets = [lax.ppermute(fresh, groups, perm) for perm in shift]  6.14 us
    pallas_call x1, Pallas kernels, layer(): pl.pallas_call(functools.partial(last_kernel, len(kvs), n_batch, n_rows),...  5.07 us
  transfers between devices with their start and end apart: 19, of which 6 were waited for; matrix products, arithmetic and copies ran while one was open for 2% of the time, Pallas kernels for 31%

profile of v1, /device:TPU:0, one launch (start us, length us, event | category | flops | bytes accessed | tf_op | source)
XLA Modules:
  0.0 122.5 jit_solution(4781733821457268940)
XLA Ops:
  0.6 0.6 collective-permute-start
  1.2 4.4 %collective-permute-start.1 = (bf16[128,4096]{1,0:T(8,128)(2,1)}, bf16[128,4096]{1,0:T(8,128)(2,1)S(1)}, u32[]{:S(2)}, u32[]{:S(2)}) collective-permute-start(bf16[128,4096]{1,0:T(8,128)(2,1)} %bitcast.14), channel_id=1, source_target_pairs={{0,8},{8,0},{1,9},{9,1},{2,10},{10,2},{3,11},{11,3},{16,24},{24,16... | collective-permute-start | bytes 3145736 | tf_op jit(solution)/shard_map/ppermute | solution.py:540
  6.9 1.0 constant_dynamic-slice_fusion
  8.7 0.1 fusion.7
  8.8 0.1 pad_maximum_fusion.2
  8.9 0.7 add_convert_fusion
  9.6 0.1 fusion.6
  9.8 0.1 pad_maximum_fusion
  9.8 8.7 %collective-permute-done.1.refs_2_ = bf16[128,4096]{1,0:T(8,128)(2,1)S(1)} collective-permute-done((bf16[128,4096]{1,0:T(8,128)(2,1)}, bf16[128,4096]{1,0:T(8,128)(2,1)S(1)}, u32[]{:S(2)}, u32[]{:S(2)}) %collective-permute-start.1) | collective-permute-done | bytes 1048608 | tf_op jit(solution)/shard_map/ppermute | solution.py:540
  18.6 1.3 %collective-permute-start.2 = (bf16[128,4096]{1,0:T(8,128)(2,1)S(1)}, bf16[128,4096]{1,0:T(8,128)(2,1)S(1)}, u32[]{:S(2)}, u32[]{:S(2)}) collective-permute-start(bf16[128,4096]{1,0:T(8,128)(2,1)S(1)} %collective-permute-done.1.refs_2_), channel_id=1, source_target_pairs={{0,4},{8,12},{1,5},{9,13},{2,6},{10,14},{3,7},{11,15},{16,20},{24,... | collective-permute-start | bytes 3145736 | tf_op jit(solution)/shard_map/ppermute | solution.py:604
  19.9 0.0 collective-permute-done.sib_hbm
  19.9 13.5 %first.1 = (bf16[6,128,256]{2,1,0:T(8,128)(2,1)S(1)}, bf16[6,128,256]{2,1,0:T(8,128)(2,1)S(1)}, f32[4,6,4,256]{3,2,1,0:T(4,128)S(1)}, bf16[6,4096,256]{2,1,0:T(8...) custom-call(s32[5]{0:T(128)S(1)} %compare_select_fusion.5.idx.refs_0_, ...), custom_call_target="tpu_custom_call" | custom-call | tf_op jit(solution)/shard_map/first/pallas_call | solution.py:543
  33.4 0.7 collective-permute-start.7
  34.2 2.1 %collective-permute-start.3 = (bf16[8,4096]{1,0:T(8,128)(2,1)S(1)}, bf16[8,4096]{1,0:T(8,128)(2,1)S(1)}, u32[]{:S(2)}, u32[]{:S(2)}) collective-permute-start(bf16[8,4096]{1,0:T(8,128)(2,1)S(1)} %concatenate.15._a), channel_id=1, source_target_pairs={{0,16},{1,17},{2,18},{3,19},{16,0},{17,1},{18,2},{19,3},{4,20},{5,... | collective-permute-start | bytes 196616 | tf_op jit(solution)/shard_map/ppermute | solution.py:541
  36.3 1.5 %collective-permute-start.4 = (bf16[8,4096]{1,0:T(8,128)(2,1)S(1)}, bf16[8,4096]{1,0:T(8,128)(2,1)S(1)}, u32[]{:S(2)}, u32[]{:S(2)}) collective-permute-start(bf16[8,4096]{1,0:T(8,128)(2,1)S(1)} %concatenate.15._a), channel_id=1, source_target_pairs={{0,17},{1,18},{2,19},{3,16},{16,1},{17,2},{18,3},{19,0},{4,21},{5,... | collective-permute-start | bytes 196616 | tf_op jit(solution)/shard_map/ppermute | solution.py:541
  37.8 3.5 %collective-permute-start.5 = (bf16[8,4096]{1,0:T(8,128)(2,1)S(1)}, bf16[8,4096]{1,0:T(8,128)(2,1)S(1)}, u32[]{:S(2)}, u32[]{:S(2)}) collective-permute-start(bf16[8,4096]{1,0:T(8,128)(2,1)S(1)} %concatenate.15._a), channel_id=1, source_target_pairs={{0,18},{1,19},{2,16},{3,17},{16,2},{17,3},{18,0},{19,1},{4,22},{5,... | collective-permute-start | bytes 196616 | tf_op jit(solution)/shard_map/ppermute | solution.py:541
  41.3 0.0 collective-permute-done.3.refs_11_
  41.3 2.2 %collective-permute-start.6 = (bf16[8,4096]{1,0:T(8,128)(2,1)S(1)}, bf16[8,4096]{1,0:T(8,128)(2,1)S(1)}, u32[]{:S(2)}, u32[]{:S(2)}) collective-permute-start(bf16[8,4096]{1,0:T(8,128)(2,1)S(1)} %concatenate.15._a), channel_id=1, source_target_pairs={{0,19},{1,16},{2,17},{3,18},{16,3},{17,0},{18,1},{19,2},{4,23},{5,... | collective-permute-start | bytes 196616 | tf_op jit(solution)/shard_map/ppermute | solution.py:541
  43.6 0.0 collective-permute-done.4.refs_12_
  43.6 0.4 collective-permute-done.5.refs_13_
  43.9 2.6 %collective-permute-done.6.refs_14_ = bf16[8,4096]{1,0:T(8,128)(2,1)S(1)} collective-permute-done((bf16[8,4096]{1,0:T(8,128)(2,1)S(1)}, bf16[8,4096]{1,0:T(8,128)(2,1)S(1)}, u32[]{:S(2)}, u32[]{:S(2)}) %collective-permute-start.6) | collective-permute-done | bytes 65568 | tf_op jit(solution)/shard_map/ppermute | solution.py:541
  46.5 0.0 collective-permute-done.2.refs_3_
  46.5 6.7 %chunk.2 = (bf16[2,128,256]{2,1,0:T(8,128)(2,1)S(1)}, bf16[128,4096]{1,0:T(8,128)(2,1)S(1)}, f32[6,8,256]{2,1,0:T(8,128)S(1)}) custom-call(s32[5]{0:T(128)S(1)} %compare_select_fusion.5.idx.refs_0_, s32[1,1]{1,0:T(1,128)} %copy.18.refs_1_, bf16[128,4096]{1,0:T(8,128)(2,1)S(1)} %collective-permute-done.1.refs_2_, ...), custom_call_target="tpu_custom_call" | custom-call | tf_op jit(solution)/shard_map/chunk/pallas_call | solution.py:626
  53.2 1.3 %collective-permute-start.9 = (bf16[128,4096]{1,0:T(8,128)(2,1)S(1)}, bf16[128,4096]{1,0:T(8,128)(2,1)S(1)}, u32[]{:S(2)}, u32[]{:S(2)}) collective-permute-start(bf16[128,4096]{1,0:T(8,128)(2,1)S(1)} %get-tuple-element.24.a), channel_id=1, source_target_pairs={{4,0},{12,8},{5,1},{13,9},{6,2},{14,10},{7,3},{15,11},{20,16},{28,... | collective-permute-start | bytes 3145736 | tf_op jit(solution)/shard_map/ppermute | solution.py:670
  54.5 0.0 collective-permute-done.7.refs_2_
  54.5 1.3 %collective-permute-start.8 = (bf16[128,4096]{1,0:T(8,128)(2,1)S(1)}, bf16[128,4096]{1,0:T(8,128)(2,1)S(1)}, u32[]{:S(2)}, u32[]{:S(2)}) collective-permute-start(bf16[128,4096]{1,0:T(8,128)(2,1)S(1)} %collective-permute-done.7.refs_2_), channel_id=1, source_target_pairs={{4,0},{12,8},{5,1},{13,9},{6,2},{14,10},{7,3},{15,11},{20,16},{28,... | collective-permute-start | bytes 3145736 | tf_op jit(solution)/shard_map/ppermute | solution.py:604
  55.8 1.9 %collective-permute-done.9.b = bf16[128,4096]{1,0:T(8,128)(2,1)S(1)} collective-permute-done((bf16[128,4096]{1,0:T(8,128)(2,1)S(1)}, bf16[128,4096]{1,0:T(8,128)(2,1)S(1)}, u32[]{:S(2)}, u32[]{:S(2)}) %collective-permute-start.9) | collective-permute-done | bytes 1048608 | tf_op jit(solution)/shard_map/ppermute | solution.py:670
  57.8 0.3 add.129.refs_15_
  58.0 1.2 collective-permute-done.8.refs_3_
  59.2 0.0 copy-start.1
  59.3 7.3 %chunk.3 = (bf16[2,128,256]{2,1,0:T(8,128)(2,1)S(1)}, bf16[128,4096]{1,0:T(8,128)(2,1)S(1)}, bf16[16,1024]{1,0:T(8,128)(2,1)S(1)}) custom-call(s32[5]{0:T(128)S(1)} %compare_select_fusion.5.idx.refs_0_, s32[1,1]{1,0:T(1,128)} %copy.18.refs_1_, bf16[128,4096]{1,0:T(8,128)(2,1)S(1)} %collective-permute-done.7.refs_2_, ...), custom_call_target="tpu_custom_call" | custom-call | tf_op jit(solution)/shard_map/chunk/pallas_call | solution.py:626
  66.5 2.1 %collective-permute-start.16 = (bf16[128,4096]{1,0:T(8,128)(2,1)S(1)}, bf16[128,4096]{1,0:T(8,128)(2,1)S(1)}, u32[]{:S(2)}, u32[]{:S(2)}) collective-permute-start(bf16[128,4096]{1,0:T(8,128)(2,1)S(1)} %get-tuple-element.30.a), channel_id=1, source_target_pairs={{0,4},{8,12},{1,5},{9,13},{2,6},{10,14},{3,7},{11,15},{16,20},{24,... | collective-permute-start | bytes 3145736 | tf_op jit(solution)/shard_map/ppermute | solution.py:670
  68.6 0.6 collective-permute-start.10
  69.2 1.2 collective-permute-start.11
  70.4 4.4 %collective-permute-start.12 = (bf16[16,1024]{1,0:T(8,128)(2,1)S(1)}, bf16[16,1024]{1,0:T(8,128)(2,1)S(1)}, u32[]{:S(2)}, u32[]{:S(2)}) collective-permute-start(bf16[16,1024]{1,0:T(8,128)(2,1)S(1)} %get-tuple-element.27), channel_id=1, source_target_pairs={{0,18},{1,19},{2,16},{3,17},{16,2},{17,3},{18,0},{19,1},{4,22},{5,... | collective-permute-start | bytes 98312 | tf_op jit(solution)/shard_map/ppermute | solution.py:674
  74.8 0.0 collective-permute-start.13
  74.8 0.0 copy-done.1
  74.8 9.6 %decode.1.refs_8_ = f32[16,1024]{1,0:T(8,128)S(1)} custom-call(s32[4]{0:T(128)S(1)} %copy-done.1, s32[1,1]{1,0:T(1,128)} %copy.20.slot.refs_2_, f32[4,6,4,256]{3,2,1,0:T(4,128)S(1)} %get-tuple-element.26.raw_ref, f32[4,4,128]{2,1,0:T(4,128)S(1)} %get-tuple-element.38._b.cos_ref, f32[4,4,128]{2,1,0:T(4,128)S(1)} %get-tuple-element.39._c.sin_ref, ...), custom_call_target="tpu_custom_call" | custom-call | tf_op jit(solution)/shard_map/decode/pallas_call | solution.py:582
  84.4 0.0 collective-permute-done.10.refs_9_
  84.4 0.0 collective-permute-done.11.refs_10_
  84.4 0.0 collective-permute-done.12.refs_11_
  84.4 0.0 collective-permute-done.13.refs_12_
  84.4 0.0 copy-start
  84.4 5.1 %last.1 = (bf16[128,4096]{1,0:T(8,128)(2,1)S(1)}, bf16[144,4096]{1,0:T(8,128)(2,1)S(1)}, bf16[16,4096]{1,0:T(8,128)(2,1)S(1)}) custom-call(s32[5]{0:T(128)S(1)} %compare_select_fusion.5.idx.refs_0_, s32[1,1]{1,0:T(1,128)} %copy.18.refs_1_, s32[1,1]{1,0:T(1,128)} %copy.20.slot.refs_2_, s32[1,1]{1,0:T(1,128)S(6)} %copy.19.refs_3_, ...), custom_call_target="tpu_custom_call" | custom-call | tf_op jit(solution)/shard_map/last/pallas_call | solution.py:675
  89.5 0.1 collective-permute-start.14
  89.6 3.4 %collective-permute-start.15 = (bf16[128,4096]{1,0:T(8,128)(2,1)S(1)}, bf16[128,4096]{1,0:T(8,128)(2,1)S(1)}, u32[]{:S(2)}, u32[]{:S(2)}) collective-permute-start(bf16[128,4096]{1,0:T(8,128)(2,1)S(1)} %add.129.refs_15_), channel_id=1, source_target_pairs={{0,8},{8,0},{1,9},{9,1},{2,10},{10,2},{3,11},{11,3},{16,24},{24,16... | collective-permute-start | bytes 3145736 | tf_op jit(solution)/shard_map/ppermute | solution.py:672
  93.0 0.0 collective-permute-done.16.b
  93.0 0.3 add.130
  93.3 0.7 collective-permute-start.17
  94.0 0.0 collective-permute-done.14.sib.b
  94.1 0.6 collective-permute-start.18
  94.7 1.6 %base.1 = f32[128,4096]{1,0:T(8,128)S(1)} custom-call(bf16[128,4096]{1,0:T(8,128)(2,1)} %bitcast.16, bf16[128,4096]{1,0:T(8,128)(2,1)S(1)} %get-tuple-element.28.own, bf16[144,4096]{1,0:T(8,128)(2,1)S(1)} %collective-permute-done.14.sib.b), custom_call_target="tpu_custom_call" | custom-call | tf_op jit(solution)/shard_map/base/pallas_call | solution.py:707
  96.3 23.5 %collective-permute-done.18.b = bf16[16,4096]{1,0:T(8,128)(2,1)S(1)} collective-permute-done((bf16[16,4096]{1,0:T(8,128)(2,1)S(1)}, bf16[16,4096]{1,0:T(8,128)(2,1)S(1)}, u32[]{:S(2)}, u32[]{:S(2)}) %collective-permute-start.18) | collective-permute-done | bytes 131104 | tf_op jit(solution)/shard_map/ppermute | solution.py:695
  119.8 0.0 copy-done
  119.8 0.7 dec.1
  120.5 0.0 collective-permute-done.15.refs_0_
  120.5 0.0 collective-permute-done.17.refs_1_
  120.5 1.8 %sum.1 = bf16[128,4096]{1,0:T(8,128)(2,1)} custom-call(s32[5]{0:T(128)S(1)} %compare_select_fusion.5.idx.refs_0_, f32[128,4096]{1,0:T(8,128)S(1)} %base.1, bf16[128,4096]{1,0:T(8,128)(2,1)S(1)} %collective-permute-done.15.refs_0_, bf16[128,4096]{1,0:T(8,128)(2,1)S(1)} %collective-permute-done.17.refs_1_), custom_call_target="tpu_custom_call" | custom-call | tf_op jit(solution)/shard_map/sum/pallas_call | solution.py:717
  (6 shorter events, 0.1 us)
Async XLA Ops:
  0.6 19.3 %collective-permute-start = (bf16[128,4096]{1,0:T(8,128)(2,1)}, bf16[128,4096]{1,0:T(8,128)(2,1)S(1)}, u32[]{:S(2)}, u32[]{:S(2)}) collective-permute-start(bf16[128,4096]{1,0:T(8,128)(2,1)} %bitcast.13), channel_id=1, source_target_pairs={{0,4},{4,0},{8,12},{12,8},{1,5},{5,1},{9,13},{13,9},{2,6},{6,2},{1... | collective-permute-start | bytes 3145736 | tf_op jit(solution)/shard_map/ppermute | solution.py:535
  1.2 17.4 %collective-permute-start.1 = (bf16[128,4096]{1,0:T(8,128)(2,1)}, bf16[128,4096]{1,0:T(8,128)(2,1)S(1)}, u32[]{:S(2)}, u32[]{:S(2)}) collective-permute-start(bf16[128,4096]{1,0:T(8,128)(2,1)} %bitcast.14), channel_id=1, source_target_pairs={{0,8},{8,0},{1,9},{9,1},{2,10},{10,2},{3,11},{11,3},{16,24},{24,16... | collective-permute-start | bytes 3145736 | tf_op jit(solution)/shard_map/ppermute | solution.py:540
  18.6 27.9 %collective-permute-start.2 = (bf16[128,4096]{1,0:T(8,128)(2,1)S(1)}, bf16[128,4096]{1,0:T(8,128)(2,1)S(1)}, u32[]{:S(2)}, u32[]{:S(2)}) collective-permute-start(bf16[128,4096]{1,0:T(8,128)(2,1)S(1)} %collective-permute-done.1.refs_2_), channel_id=1, source_target_pairs={{0,4},{8,12},{1,5},{9,13},{2,6},{10,14},{3,7},{11,15},{16,20},{24,... | collective-permute-start | bytes 3145736 | tf_op jit(solution)/shard_map/ppermute | solution.py:604
  33.4 21.1 %collective-permute-start.7 = (bf16[128,4096]{1,0:T(8,128)(2,1)S(1)}, bf16[128,4096]{1,0:T(8,128)(2,1)S(1)}, u32[]{:S(2)}, u32[]{:S(2)}) collective-permute-start(bf16[128,4096]{1,0:T(8,128)(2,1)S(1)} %get-tuple-element.22), channel_id=1, source_target_pairs={{4,12},{12,4},{5,13},{13,5},{6,14},{14,6},{7,15},{15,7},{20,28},{2... | collective-permute-start | bytes 3145736 | tf_op jit(solution)/shard_map/ppermute | solution.py:575
  34.2 7.2 %collective-permute-start.3 = (bf16[8,4096]{1,0:T(8,128)(2,1)S(1)}, bf16[8,4096]{1,0:T(8,128)(2,1)S(1)}, u32[]{:S(2)}, u32[]{:S(2)}) collective-permute-start(bf16[8,4096]{1,0:T(8,128)(2,1)S(1)} %concatenate.15._a), channel_id=1, source_target_pairs={{0,16},{1,17},{2,18},{3,19},{16,0},{17,1},{18,2},{19,3},{4,20},{5,... | collective-permute-start | bytes 196616 | tf_op jit(solution)/shard_map/ppermute | solution.py:541
  36.3 7.3 %collective-permute-start.4 = (bf16[8,4096]{1,0:T(8,128)(2,1)S(1)}, bf16[8,4096]{1,0:T(8,128)(2,1)S(1)}, u32[]{:S(2)}, u32[]{:S(2)}) collective-permute-start(bf16[8,4096]{1,0:T(8,128)(2,1)S(1)} %concatenate.15._a), channel_id=1, source_target_pairs={{0,17},{1,18},{2,19},{3,16},{16,1},{17,2},{18,3},{19,0},{4,21},{5,... | collective-permute-start | bytes 196616 | tf_op jit(solution)/shard_map/ppermute | solution.py:541
  37.8 6.1 %collective-permute-start.5 = (bf16[8,4096]{1,0:T(8,128)(2,1)S(1)}, bf16[8,4096]{1,0:T(8,128)(2,1)S(1)}, u32[]{:S(2)}, u32[]{:S(2)}) collective-permute-start(bf16[8,4096]{1,0:T(8,128)(2,1)S(1)} %concatenate.15._a), channel_id=1, source_target_pairs={{0,18},{1,19},{2,16},{3,17},{16,2},{17,3},{18,0},{19,1},{4,22},{5,... | collective-permute-start | bytes 196616 | tf_op jit(solution)/shard_map/ppermute | solution.py:541
  41.3 5.2 %collective-permute-start.6 = (bf16[8,4096]{1,0:T(8,128)(2,1)S(1)}, bf16[8,4096]{1,0:T(8,128)(2,1)S(1)}, u32[]{:S(2)}, u32[]{:S(2)}) collective-permute-start(bf16[8,4096]{1,0:T(8,128)(2,1)S(1)} %concatenate.15._a), channel_id=1, source_target_pairs={{0,19},{1,16},{2,17},{3,18},{16,3},{17,0},{18,1},{19,2},{4,23},{5,... | collective-permute-start | bytes 196616 | tf_op jit(solution)/shard_map/ppermute | solution.py:541
  53.2 4.6 %collective-permute-start.9 = (bf16[128,4096]{1,0:T(8,128)(2,1)S(1)}, bf16[128,4096]{1,0:T(8,128)(2,1)S(1)}, u32[]{:S(2)}, u32[]{:S(2)}) collective-permute-start(bf16[128,4096]{1,0:T(8,128)(2,1)S(1)} %get-tuple-element.24.a), channel_id=1, source_target_pairs={{4,0},{12,8},{5,1},{13,9},{6,2},{14,10},{7,3},{15,11},{20,16},{28,... | collective-permute-start | bytes 3145736 | tf_op jit(solution)/shard_map/ppermute | solution.py:670
  54.5 4.7 %collective-permute-start.8 = (bf16[128,4096]{1,0:T(8,128)(2,1)S(1)}, bf16[128,4096]{1,0:T(8,128)(2,1)S(1)}, u32[]{:S(2)}, u32[]{:S(2)}) collective-permute-start(bf16[128,4096]{1,0:T(8,128)(2,1)S(1)} %collective-permute-done.7.refs_2_), channel_id=1, source_target_pairs={{4,0},{12,8},{5,1},{13,9},{6,2},{14,10},{7,3},{15,11},{20,16},{28,... | collective-permute-start | bytes 3145736 | tf_op jit(solution)/shard_map/ppermute | solution.py:604
  59.2 15.5 %copy-start.1 = (s32[4]{0:T(128)S(1)}, s32[4]{0:T(128)}, u32[]{:S(2)}) copy-start(s32[4]{0:T(128)} %lens.1) | copy-start | bytes 52
  66.5 26.5 %collective-permute-start.16 = (bf16[128,4096]{1,0:T(8,128)(2,1)S(1)}, bf16[128,4096]{1,0:T(8,128)(2,1)S(1)}, u32[]{:S(2)}, u32[]{:S(2)}) collective-permute-start(bf16[128,4096]{1,0:T(8,128)(2,1)S(1)} %get-tuple-element.30.a), channel_id=1, source_target_pairs={{0,4},{8,12},{1,5},{9,13},{2,6},{10,14},{3,7},{11,15},{16,20},{24,... | collective-permute-start | bytes 3145736 | tf_op jit(solution)/shard_map/ppermute | solution.py:670
  68.6 15.7 %collective-permute-start.10 = (bf16[16,1024]{1,0:T(8,128)(2,1)S(1)}, bf16[16,1024]{1,0:T(8,128)(2,1)S(1)}, u32[]{:S(2)}, u32[]{:S(2)}) collective-permute-start(bf16[16,1024]{1,0:T(8,128)(2,1)S(1)} %get-tuple-element.27), channel_id=1, source_target_pairs={{0,16},{1,17},{2,18},{3,19},{16,0},{17,1},{18,2},{19,3},{4,20},{5,... | collective-permute-start | bytes 98312 | tf_op jit(solution)/shard_map/ppermute | solution.py:674
  69.2 15.2 %collective-permute-start.11 = (bf16[16,1024]{1,0:T(8,128)(2,1)S(1)}, bf16[16,1024]{1,0:T(8,128)(2,1)S(1)}, u32[]{:S(2)}, u32[]{:S(2)}) collective-permute-start(bf16[16,1024]{1,0:T(8,128)(2,1)S(1)} %get-tuple-element.27), channel_id=1, source_target_pairs={{0,17},{1,18},{2,19},{3,16},{16,1},{17,2},{18,3},{19,0},{4,21},{5,... | collective-permute-start | bytes 98312 | tf_op jit(solution)/shard_map/ppermute | solution.py:674
  70.4 14.0 %collective-permute-start.12 = (bf16[16,1024]{1,0:T(8,128)(2,1)S(1)}, bf16[16,1024]{1,0:T(8,128)(2,1)S(1)}, u32[]{:S(2)}, u32[]{:S(2)}) collective-permute-start(bf16[16,1024]{1,0:T(8,128)(2,1)S(1)} %get-tuple-element.27), channel_id=1, source_target_pairs={{0,18},{1,19},{2,16},{3,17},{16,2},{17,3},{18,0},{19,1},{4,22},{5,... | collective-permute-start | bytes 98312 | tf_op jit(solution)/shard_map/ppermute | solution.py:674
  74.8 9.6 %collective-permute-start.13 = (bf16[16,1024]{1,0:T(8,128)(2,1)S(1)}, bf16[16,1024]{1,0:T(8,128)(2,1)S(1)}, u32[]{:S(2)}, u32[]{:S(2)}) collective-permute-start(bf16[16,1024]{1,0:T(8,128)(2,1)S(1)} %get-tuple-element.27), channel_id=1, source_target_pairs={{0,19},{1,16},{2,17},{3,18},{16,3},{17,0},{18,1},{19,2},{4,23},{5,... | collective-permute-start | bytes 98312 | tf_op jit(solution)/shard_map/ppermute | solution.py:674
  84.4 35.4 %copy-start = (bf16[4,4,4096]{2,1,0:T(4,128)(2,1)S(1)}, bf16[4,4,4096]{2,1,0:T(4,128)(2,1)}, u32[]{:S(2)}) copy-start(bf16[4,4,4096]{2,1,0:T(4,128)(2,1)} %tokens.1) | copy-start | bytes 393220
  89.5 4.5 %collective-permute-start.14 = (bf16[144,4096]{1,0:T(8,128)(2,1)S(1)}, bf16[144,4096]{1,0:T(8,128)(2,1)S(1)}, u32[]{:S(2)}, u32[]{:S(2)}) collective-permute-start(bf16[144,4096]{1,0:T(8,128)(2,1)S(1)} %get-tuple-element.29), channel_id=1, source_target_pairs={{0,4},{4,0},{8,12},{12,8},{1,5},{5,1},{9,13},{13,9},{2,6},{6,2},{1... | collective-permute-start | bytes 3538952 | tf_op jit(solution)/shard_map/ppermute | solution.py:690
  89.6 30.9 %collective-permute-start.15 = (bf16[128,4096]{1,0:T(8,128)(2,1)S(1)}, bf16[128,4096]{1,0:T(8,128)(2,1)S(1)}, u32[]{:S(2)}, u32[]{:S(2)}) collective-permute-start(bf16[128,4096]{1,0:T(8,128)(2,1)S(1)} %add.129.refs_15_), channel_id=1, source_target_pairs={{0,8},{8,0},{1,9},{9,1},{2,10},{10,2},{3,11},{11,3},{16,24},{24,16... | collective-permute-start | bytes 3145736 | tf_op jit(solution)/shard_map/ppermute | solution.py:672
  93.3 27.2 %collective-permute-start.17 = (bf16[128,4096]{1,0:T(8,128)(2,1)S(1)}, bf16[128,4096]{1,0:T(8,128)(2,1)S(1)}, u32[]{:S(2)}, u32[]{:S(2)}) collective-permute-start(bf16[128,4096]{1,0:T(8,128)(2,1)S(1)} %add.130), channel_id=1, source_target_pairs={{4,12},{12,4},{5,13},{13,5},{6,14},{14,6},{7,15},{15,7},{20,28},{2... | collective-permute-start | bytes 3145736 | tf_op jit(solution)/shard_map/ppermute | solution.py:672
  94.1 25.7 %collective-permute-start.18 = (bf16[16,4096]{1,0:T(8,128)(2,1)S(1)}, bf16[16,4096]{1,0:T(8,128)(2,1)S(1)}, u32[]{:S(2)}, u32[]{:S(2)}) collective-permute-start(bf16[16,4096]{1,0:T(8,128)(2,1)S(1)} %add.131.a), channel_id=1, source_target_pairs={{0,8},{4,12},{8,0},{12,4},{1,9},{5,13},{9,1},{13,5},{2,10},{6,14},... | collective-permute-start | bytes 393224 | tf_op jit(solution)/shard_map/ppermute | solution.py:695

commit v2 on v1

v2 whole, which is shorter than its diff:
```python
import functools

import jax
import jax.numpy as jnp
import numpy as np
from jax import lax
from jax.experimental import pallas as pl
from jax.experimental.pallas import tpu as pltpu
from jax.sharding import PartitionSpec as P


HEAD_DIM = 128
GROUP = 4
KINDS = GROUP + 2
PAIR = 2 * HEAD_DIM
BLOCKS = KINDS // 2
EPSILON = 1e-05
THETA = 500000.0
NEG = -1e30
SCALE = HEAD_DIM ** (-0.5)
OUT_COLS = 1024
f32 = jnp.float32
bf16 = jnp.bfloat16


VMEM = pl.BlockSpec(memory_space=pltpu.MemorySpace.VMEM)
SMEM = pl.BlockSpec(memory_space=pltpu.MemorySpace.SMEM)
HBM = pl.BlockSpec(memory_space=pltpu.MemorySpace.HBM)
ANY = pl.BlockSpec(memory_space=pl.ANY)


def dot(a, b):
    return jnp.dot(a, b, preferred_element_type=f32)


def dot_t(a, b):
    return lax.dot_general(a, b, (((1,), (1,)), ((), ())), preferred_element_type=f32)


def rot(u, cosine, sine):
    return u * cosine + pltpu.roll(u, HEAD_DIM // 2, 1) * sine


def angle_tables(places):
    half = HEAD_DIM // 2
    freqs = THETA ** (-(jnp.arange(HEAD_DIM) % half).astype(f32) / half)
    angles = places.astype(f32)[..., None] * freqs
    first = jnp.arange(HEAD_DIM) < half
    return jnp.where(first, jnp.cos(angles), jnp.sin(angles))


def spread(table):
    half = HEAD_DIM // 2
    turned = pltpu.roll(table, half, 1)
    first = lax.broadcasted_iota(jnp.int32, table.shape, 1) < half
    return jnp.where(first, table, turned), jnp.where(first, -turned, table)


def fixed_tables(count):
    half = HEAD_DIM // 2
    freqs = np.float32(THETA) ** (-np.arange(half, dtype=np.float32) / np.float32(half))
    angles = np.arange(count, dtype=np.float32)[:, None] * freqs.astype(np.float32)
    cosine, sine = np.cos(angles).astype(np.float32), np.sin(angles).astype(np.float32)
    return np.concatenate([cosine, cosine], -1), np.concatenate([-sine, sine], -1)


def norm_rows(src, dst, offset, gain_ref):
    rows = src.shape[0]

    def step(i, _):
        at = pl.multiple_of(i * 16, 16)
        wide = src[pl.ds(at, 16), :].astype(f32)
        factor = lax.rsqrt(jnp.mean(wide * wide, axis=-1, keepdims=True) + EPSILON)
        to = pl.multiple_of(offset + i * 16, 16)
        dst[pl.ds(to, 16), :] = (wide * factor * gain_ref[...]).astype(bf16)
        return 0

    lax.fori_loop(0, rows // 16, step, 0, unroll=2)


def weight_copies(w_hbm, w_vmem, sems, width):
    return [
        pltpu.make_async_copy(
            w_hbm.at[:, pl.ds(j * width, width)], w_vmem.at[j], sems.at[j]
        )
        for j in range(w_vmem.shape[0])
    ]


def rotated_pair(acc, cosine, sine, j):
    cosine, sine = cosine[...], sine[...]
    first = rot(acc[:, :HEAD_DIM], cosine, sine)
    second = acc[:, HEAD_DIM:]
    if j % BLOCKS != BLOCKS - 1:
        second = rot(second, cosine, sine)
    return jnp.concatenate([first, second], axis=1).astype(bf16)


def load(pairs, sems):
    copies = [pltpu.make_async_copy(src, dst, sems.at[i]) for i, (src, dst) in enumerate(pairs)]
    for copy in copies:
        copy.start()
    return copies


def norm_token_rows(parts, gain_ref):
    out = []
    for part in parts:
        wide = part.astype(f32)
        factor = lax.rsqrt(jnp.mean(wide * wide, axis=-1, keepdims=True) + EPSILON)
        out.append(wide * factor * gain_ref[...])
    return jnp.concatenate(out, axis=0).astype(bf16)


def first_kernel(
    idx, slot, assign, own_hbm, dec_hbm, gain_hbm, cos_hbm, sin_hbm, wq_hbm,
    _, own_out, raw_out, wq, ask_out,
    own, dec, gain, tabs, normed, q_sems, in_sems,
):
    rows = own.shape[0]
    steps, decs = dec.shape[:2]
    at = pl.ds(pl.multiple_of(idx[0] * rows, rows), rows)
    weights = weight_copies(wq_hbm, wq, q_sems, PAIR)
    ready = load(
        [
            (gain_hbm, gain), (own_hbm, own), (dec_hbm, dec),
            (cos_hbm.at[at], tabs.at[0]), (sin_hbm.at[at], tabs.at[1]),
        ],
        in_sems,
    )
    weights[0].start()
    ready[0].wait()
    ready[1].wait()
    for copy in weights[1:4]:
        copy.start()
    norm_rows(own, normed, 0, gain)
    ready[2].wait()
    tokens = [dec[s].astype(f32) for s in range(steps)]
    normed[rows:] = norm_token_rows(tokens, gain)
    fresh = []
    for s in range(steps):
        row = tokens[s][:1]
        for r in range(1, decs):
            row = jnp.where(slot[0, 0] == r, tokens[s][r : r + 1], row)
        fresh.append(row)
    fresh.append(jnp.full((steps, dec.shape[2]), assign[0, 0].astype(f32)))
    ask_out[...] = jnp.concatenate(fresh, axis=0).astype(bf16)
    for copy in ready[3:]:
        copy.wait()
    for j in range(wq.shape[0]):
        weights[j].wait()
        if j + 4 < len(weights):
            weights[j + 4].start()
        acc = dot(normed[...], wq[j])
        own_out[j] = rotated_pair(acc[:rows], tabs.at[0], tabs.at[1], j)
        for r in range(decs):
            for s in range(steps):
                row = rows + s * decs + r
                raw_out[r, j, s : s + 1] = acc[row : row + 1]


def project_kernel(which, n_ask, *refs):
    refs = list(refs)
    take = lambda n: [refs.pop(0) for _ in range(n)]
    idx, x_hbm, gain_hbm, cos_hbm, sin_hbm, wq = take(6)
    asks = take(n_ask)
    out = take(1)[0]
    raw_out = take(1)[0] if n_ask else None
    x, gain, tabs, normed, in_sem = take(5)
    rows = x.shape[0]
    at = pl.ds(pl.multiple_of(idx[which] * rows, rows), rows)
    ready = load(
        [(gain_hbm, gain), (x_hbm, x), (cos_hbm.at[at], tabs.at[0]), (sin_hbm.at[at], tabs.at[1])],
        in_sem,
    )
    ready[0].wait()
    if n_ask:
        here = idx[idx.shape[0] - 1].astype(f32)
        steps = asks[0].shape[0] // 2
        new = jnp.zeros((steps, x.shape[1]), f32)
        for ref in asks:
            wide = ref[...].astype(f32)
            new = jnp.where(wide[steps : steps + 1] == here, wide[:steps], new)
        fill = jnp.zeros((16 - steps, x.shape[1]), f32)
        normed[rows:] = norm_token_rows([new, fill], gain)
    ready[1].wait()
    norm_rows(x, normed, 0, gain)
    for copy in ready[2:]:
        copy.wait()
    for j in range(wq.shape[0]):
        acc = dot(normed[...], wq[j])
        out[j] = rotated_pair(acc[:rows], tabs.at[0], tabs.at[1], j)
        if n_ask:
            raw_out[j] = acc[rows : rows + raw_out.shape[1]]


def own_tail(q, k_own, steps):
    s = dot_t(q, k_own) * SCALE
    at = lax.broadcasted_iota(jnp.int32, s.shape, 0)
    t = lax.broadcasted_iota(jnp.int32, s.shape, 1)
    return jnp.where(t <= lax.rem(at, steps), s, NEG)


def stacked_queries(raw, h, cosine, sine):
    parts = []
    for g in range(GROUP):
        block = raw(h * BLOCKS + g // 2)
        parts.append(rot(block[:, (g % 2) * HEAD_DIM : (g % 2 + 1) * HEAD_DIM], cosine, sine))
    return jnp.concatenate(parts, axis=0).astype(bf16)


def own_pair(raw, h, cosine, sine, pad):
    block = raw(h * BLOCKS + BLOCKS - 1)
    key = rot(block[:, :HEAD_DIM], cosine, sine)
    fill = jnp.zeros((pad - key.shape[0], HEAD_DIM), f32)
    key = jnp.concatenate([key, fill], axis=0).astype(bf16)
    value = jnp.concatenate([block[:, HEAD_DIM:], fill], axis=0).astype(bf16)
    return key, value


def decode_kernel(first, loads, *refs):
    refs = list(refs)
    take = lambda n: [refs.pop(0) for _ in range(n)]
    lens, slot, raw_ref, angle_ref, k_hbm, v_hbm = take(6)
    wo_hbm = take(1)[0] if loads else None
    out_ref = take(1)[0]
    wo = take(1)[0] if loads else None
    k_s, v_s, q_s, ko_s, vo_s, m_s, l_s, acc_s, k_sem, v_sem = take(10)
    o_sem = take(1)[0] if loads else None
    group = raw_ref.shape[0]
    n_rows, count, width = k_s.shape[:3]
    steps = raw_ref.shape[2]
    heads = k_s.shape[3] // HEAD_DIM
    many = GROUP * steps

    def copies(r, j):
        at = pl.ds(j * width, width)
        return (
            pltpu.make_async_copy(k_hbm.at[first + r, at], k_s.at[r, j], k_sem.at[r, j]),
            pltpu.make_async_copy(v_hbm.at[first + r, at], v_s.at[r, j], v_sem.at[r, j]),
        )

    def live(r, j):
        return (j * width < lens[first + r]) & (slot[0, 0] != first + r)

    def fetch(r):
        for j in range(count):

            @pl.when(live(r, j))
            def _(r=r, j=j):
                for copy in copies(r, j):
                    copy.start()

    weights = weight_copies(wo_hbm, wo, o_sem, OUT_COLS) if loads else []
    fetch(0)
    for r in range(n_rows):
        raw = lambda b, r=r: raw_ref[first + r, b]
        turn = spread(angle_ref[first + r])
        q_s[r] = jnp.zeros_like(q_s[r])
        for h in range(heads):
            lanes = slice(h * HEAD_DIM, (h + 1) * HEAD_DIM)
            q_s[r, h * many : (h + 1) * many, lanes] = stacked_queries(raw, h, *turn)
            key, value = own_pair(raw, h, *turn, ko_s.shape[1])
            ko_s[r, :, lanes] = key
            vo_s[r, :, lanes] = value
    for r in range(n_rows):
        s = own_tail(q_s[r], ko_s[r], steps)
        m = jnp.max(s, axis=-1, keepdims=True)
        e = jnp.exp(s - m)
        m_s[r] = m
        l_s[r] = jnp.sum(e, axis=-1, keepdims=True)
        acc_s[r] = dot(e.astype(bf16), vo_s[r])

    for r in range(n_rows):
        if r + 1 < n_rows:
            fetch(r + 1)
        for j in range(count):

            @pl.when(live(r, j))
            def _(r=r, j=j):
                k_copy, v_copy = copies(r, j)
                k_copy.wait()
                s = dot_t(q_s[r], k_s[r, j]) * SCALE
                at = j * width + lax.broadcasted_iota(jnp.int32, s.shape, 1)
                s = jnp.where(at < lens[first + r], s, NEG)
                m = jnp.maximum(m_s[r], jnp.max(s, axis=-1, keepdims=True))
                fade = jnp.exp(m_s[r] - m)
                e = jnp.exp(s - m)
                m_s[r] = m
                l_s[r] = l_s[r] * fade + jnp.sum(e, axis=-1, keepdims=True)
                v_copy.wait()
                acc_s[r] = acc_s[r] * fade + dot(e.astype(bf16), v_s[r, j])

        for copy in weights[r * len(weights) // n_rows : (r + 1) * len(weights) // n_rows]:
            copy.start()

    for r in range(n_rows):
        mixed = acc_s[r] / l_s[r]
        for h in range(heads):
            for g in range(GROUP):
                to = (h * GROUP + g) * HEAD_DIM
                for s in range(steps):
                    at = h * many + g * steps + s
                    row = s * group + first + r
                    out_ref[row : row + 1, to : to + HEAD_DIM] = mixed[
                        at : at + 1, h * HEAD_DIM : (h + 1) * HEAD_DIM
                    ]
    for copy in weights:
        copy.wait()


def attend(queries, q_shard, pieces, plen, out_ref, offset, heads):
    for h in range(heads):
        parts = []
        for g in range(GROUP):
            block = queries(h * BLOCKS + g // 2)
            parts.append(block[:, (g % 2) * HEAD_DIM : (g % 2 + 1) * HEAD_DIM])
        rows = parts[0].shape[0]
        q = jnp.concatenate(parts, axis=0)
        q_at = q_shard * rows + lax.rem(lax.broadcasted_iota(jnp.int32, (GROUP * rows, 1), 0), rows)
        scores, values = [], []
        for kv, shard in pieces:
            pair = kv(h)
            count = pair.shape[0]
            k_at = shard * count + lax.broadcasted_iota(jnp.int32, (1, count), 1)
            k_at = jnp.where(k_at < plen, k_at, jnp.int32(1 << 30))
            s = dot_t(q, pair[:, :HEAD_DIM]) * SCALE
            scores.append(jnp.where(k_at <= q_at, s, NEG))
            values.append(pair[:, HEAD_DIM:])
        top = functools.reduce(jnp.maximum, scores)
        top = jnp.max(top, axis=-1, keepdims=True)
        total, mixed = None, None
        for s, value in zip(scores, values):
            e = jnp.exp(s - top)
            total = e if total is None else total + e
            term = dot(e.astype(bf16), value)
            mixed = term if mixed is None else mixed + term
        mixed = (mixed / jnp.sum(total, axis=-1, keepdims=True)).astype(bf16)
        for g in range(GROUP):
            to = (h * GROUP + g) * HEAD_DIM
            out_ref[offset : offset + rows, to : to + HEAD_DIM] = mixed[g * rows : (g + 1) * rows]


def attend_new(raw, cosine, sine, pieces, plen, out_ref, heads, steps):
    spread = out_ref.shape[0] // steps
    for h in range(heads):
        q = stacked_queries(raw, h, cosine, sine)
        key, value = own_pair(raw, h, cosine, sine, 16)
        scores, values = [own_tail(q, key, steps)], [value]
        for kv, shard in pieces:
            pair = kv(h)
            count = pair.shape[0]
            k_at = shard * count + lax.broadcasted_iota(jnp.int32, (1, count), 1)
            s = dot_t(q, pair[:, :HEAD_DIM]) * SCALE
            scores.append(jnp.where(k_at < plen, s, NEG))
            values.append(pair[:, HEAD_DIM:])
        top = functools.reduce(jnp.maximum, [jnp.max(s, axis=-1, keepdims=True) for s in scores])
        total, mixed = 0.0, 0.0
        for s, v in zip(scores, values):
            e = jnp.exp(s - top)
            total = total + jnp.sum(e, axis=-1, keepdims=True)
            mixed = mixed + dot(e.astype(bf16), v)
        mixed = mixed / total
        for g in range(GROUP):
            to = (h * GROUP + g) * HEAD_DIM
            rows = [
                jnp.broadcast_to(mixed[g * steps + s : g * steps + s + 1], (spread, HEAD_DIM))
                for s in range(steps)
            ]
            out_ref[:, to : to + HEAD_DIM] = jnp.concatenate(rows, axis=0).astype(bf16)


def chunk_kernel(which, n_full, n_kv, n_ask, kv_only, *refs):
    refs = list(refs)
    take = lambda n: [refs.pop(0) for _ in range(n)]
    idx, plen, passed, gain_hbm, cos_hbm, sin_hbm, direct, wq, wo = take(9)
    full, kvs = take(n_full), take(n_kv)
    raw_s, new_angle = take(2) if n_ask else (None, None)
    kv_out = take(1)[0]
    direct_out, passed_out = (None,) * 2 if kv_only else take(2)
    new_out = take(1)[0] if n_ask else None
    x, gain, tabs, normed, qkv, in_sem = take(6)
    attn = None if kv_only else take(1)[0]
    rows = x.shape[0]
    heads = kv_out.shape[0] // 2
    shards = [idx[n_full + 2 * which + i] for i in range(2)]
    at = pl.ds(pl.multiple_of(shards[1] * rows, rows), rows)
    ready = load(
        [(gain_hbm, gain), (passed, x), (cos_hbm.at[at], tabs.at[0]), (sin_hbm.at[at], tabs.at[1])],
        in_sem,
    )
    ready[0].wait()
    ready[1].wait()
    norm_rows(x, normed, 0, gain)
    for copy in ready[2:]:
        copy.wait()
    for j in range(wq.shape[0]):
        qkv[j] = rotated_pair(dot(normed[...], wq[j]), tabs.at[0], tabs.at[1], j)
    both = (direct, qkv)
    for i in range(2):
        for h in range(heads):
            kv_out[i * heads + h] = both[i][h * BLOCKS + BLOCKS - 1]
    if kv_only:
        return
    pieces = [(lambda h, ref=ref: ref[h * BLOCKS + BLOCKS - 1], idx[i]) for i, ref in enumerate(full)]
    others = [n for n in range(n_kv + 1) if n != which]
    for ref, n in zip(kvs, others):
        for i in range(2):
            pieces.append((lambda h, ref=ref, i=i: ref[i * heads + h], idx[n_full + 2 * n + i]))
    for i in range(2):
        pieces.append((lambda h, i=i: both[i][h * BLOCKS + BLOCKS - 1], shards[i]))
    for i in (1, 0):
        attend(lambda b, i=i: both[i][b], shards[i], pieces, plen[0, 0], attn, i * rows, heads)
    if n_ask:
        steps = new_angle.shape[0]
        raw = lambda b: raw_s[b, :steps]
        attend_new(raw, *spread(new_angle[...]), pieces, plen[0, 0], new_out, heads, steps)
    for j in range(wo.shape[0]):
        cols = slice(j * OUT_COLS, (j + 1) * OUT_COLS)
        part = dot(attn[...], wo[j]).astype(bf16)
        direct_out[:, cols] = part[:rows]
        passed_out[:, cols] = part[rows:]


def last_kernel(n_kv, n_ret, n_rows, *refs):
    refs = list(refs)
    take = lambda n: [refs.pop(0) for _ in range(n)]
    idx, plen, slot, assign, own, sib = take(6)
    kvs = take(n_kv)
    decs = take(2)
    rets = take(n_ret)
    wo, own_part, sib_part, dec_part, attn = take(5)
    rows = own.shape[1]
    heads = kvs[0].shape[0] // 2
    pieces = [(lambda h, ref=ref: ref[h * BLOCKS + BLOCKS - 1], idx[i]) for i, ref in enumerate((own, sib))]
    for n, ref in enumerate(kvs):
        for i in range(2):
            pieces.append((lambda h, ref=ref, i=i: ref[i * heads + h], idx[2 + 2 * n + i]))
    for i, ref in enumerate((own, sib)):
        attend(lambda b, ref=ref: ref[b], idx[i], pieces, plen[0, 0], attn, i * rows, heads)
    pick = lax.rem(idx[idx.shape[0] - 1] - assign[0, 0] + n_ret, n_ret)
    new = rets[0][...].astype(f32)
    for k in range(1, n_ret):
        new = jnp.where(pick == k, rets[k][...].astype(f32), new)
    at = lax.rem(lax.broadcasted_iota(jnp.int32, new.shape, 0), n_rows)
    dec = jnp.where(at < n_rows // 2, decs[0][...], decs[1][...])
    attn[2 * rows :] = jnp.where(at == slot[0, 0], new, dec).astype(bf16)
    for j in range(wo.shape[0]):
        part = dot(attn[...], wo[j]).astype(bf16)
        cols = slice(j * OUT_COLS, (j + 1) * OUT_COLS)
        own_part[:, cols] = part[:rows]
        sib_part[:, cols] = part[rows:]
        dec_part[:, cols] = part[2 * rows :]


def add_kernel(start, a, b, out):
    rows = out.shape[0]

    def step(i, _):
        at = pl.ds(pl.multiple_of(i * 16, 16), 16)
        to = pl.ds(pl.multiple_of(start + i * 16, 16), 16)
        out[at, :] = (a[at, :].astype(f32) + b[to, :].astype(f32)).astype(bf16)
        return 0

    lax.fori_loop(0, rows // 16, step, 0)


def base_kernel(shard_hbm, own, sib, out, shard, sem):
    copy = pltpu.make_async_copy(shard_hbm, shard, sem)
    copy.start()
    copy.wait()

    def step(i, _):
        at = pl.ds(pl.multiple_of(i * 16, 16), 16)
        out[at, :] = shard[at, :].astype(f32) + own[at, :].astype(f32) + sib[at, :].astype(f32)
        return 0

    lax.fori_loop(0, out.shape[0] // 16, step, 0)


def sum_kernel(count, base, *refs):
    parts, out, got, sems, out_sem = refs[:count], *refs[count:]
    pieces = sems.shape[1]
    rows = out.shape[0] // pieces
    copies = [
        [
            pltpu.make_async_copy(parts[d].at[pl.ds(n * rows, rows)], got.at[d, pl.ds(n * rows, rows)], sems.at[d, n])
            for d in range(count)
        ]
        for n in range(pieces)
    ]
    for copy in sum(copies, []):
        copy.start()
    done = []
    for n in range(pieces):
        at = slice(n * rows, (n + 1) * rows)
        total = base[at]
        for d in range(count):
            copies[n][d].wait()
            total = total + got[d, at].astype(f32)
        got[0, at] = total.astype(bf16)
        done.append(pltpu.make_async_copy(got.at[0, pl.ds(n * rows, rows)], out.at[pl.ds(n * rows, rows)], out_sem.at[n]))
        done[-1].start()
    for copy in done:
        copy.wait()


def dec_kernel(tokens, a, b, out):
    steps, n_rows = tokens.shape[:2]
    total = a[...].astype(f32) + b[...].astype(f32)
    for s in range(steps):
        rows = total[s * n_rows : (s + 1) * n_rows]
        out[s] = (tokens[s].astype(f32) + rows).astype(bf16)


def params(mib):
    return pltpu.CompilerParams(vmem_limit_bytes=mib << 20)


def layer(
    prompt, prompt_len, dec_tokens, cache_k, cache_v, cache_len, assign, slot, gain, w_qkv, w_out
):
    n_blk, n_pool, n_batch = lax.axis_size("blk"), lax.axis_size("pool"), lax.axis_size("batch")
    n_chip = n_blk // 2
    shard = prompt[0]
    rows, width = shard.shape
    steps, n_rows = dec_tokens.shape[:2]
    heads = w_qkv.shape[1] // (KINDS * HEAD_DIM)
    blocks = heads * BLOCKS
    attn_cols = heads * GROUP * HEAD_DIM
    out_blocks = width // OUT_COLS
    decs = steps * n_rows

    blk = lax.axis_index("blk")
    chip, core = blk // 2, blk % 2
    batch = lax.axis_index("batch")
    at = jnp.arange(n_blk + 1, dtype=jnp.int32)
    far = (chip + n_chip - at // 2) % n_chip
    idx = jnp.where(at == n_blk, batch, 2 * far + (core + at) % 2).astype(jnp.int32)
    gain_row = gain.reshape(1, width)
    cos_t, sin_t = (jnp.asarray(t) for t in fixed_tables(n_blk * rows))
    place = jnp.concatenate([cache_len, prompt_len[0]])[:, None]
    angles = angle_tables(place + jnp.arange(steps, dtype=jnp.int32)[None, :])
    dec_angle, new_angle = angles[:n_rows], angles[n_rows]

    swap = [(i, i ^ 1) for i in range(n_blk)]
    hop = lambda d: [(2 * c + k, 2 * ((c + d) % n_chip) + k) for c in range(n_chip) for k in range(2)]
    shift = [
        [
            (p * n_batch + b, ((p + n_pool // 2) % n_pool) * n_batch + (b + k) % n_batch)
            for p in range(n_pool)
            for b in range(n_batch)
        ]
        for k in range(n_batch)
    ]
    groups = ("pool", "batch")
    near = lambda x: pltpu.with_memory_space_constraint(x, pltpu.MemorySpace.VMEM)
    stay = lambda x: pltpu.with_memory_space_constraint(x, pltpu.MemorySpace.HBM)

    sib_x = lax.ppermute(shard, "blk", swap)
    far_x = []
    for d in range(1, n_chip):
        far_x.append(lax.ppermute(shard, "blk", hop(d)))

    own, raw, wq, ask = pl.pallas_call(
        first_kernel,
        in_specs=[SMEM] * 3 + [HBM] * 6 + [ANY],
        out_specs=[VMEM] * 4,
        out_shape=[
            jax.ShapeDtypeStruct((blocks, rows, PAIR), bf16),
            jax.ShapeDtypeStruct((n_rows, blocks, steps, PAIR), f32),
            pltpu.VMEM((blocks, width, PAIR), bf16),
            jax.ShapeDtypeStruct((2 * steps, width), bf16),
        ],
        scratch_shapes=[
            pltpu.VMEM((rows, width), bf16),
            pltpu.VMEM((steps, n_rows, width), bf16),
            pltpu.VMEM((1, width), f32),
            pltpu.VMEM((2, rows, HEAD_DIM), f32),
            pltpu.VMEM((rows + decs, width), bf16),
            pltpu.SemaphoreType.DMA((blocks,)),
            pltpu.SemaphoreType.DMA((5,)),
        ],
        compiler_params=params(8),
        name="first",
    )(
        idx, slot, assign, stay(shard), stay(dec_tokens), stay(gain_row), stay(cos_t),
        stay(sin_t), stay(w_qkv), angles,
    )

    def project(which, x, asks):
        outs = [jax.ShapeDtypeStruct((blocks, rows, PAIR), bf16)]
        if asks:
            outs.append(jax.ShapeDtypeStruct((blocks, 8, PAIR), f32))
        return pl.pallas_call(
            functools.partial(project_kernel, which, len(asks)),
            in_specs=[SMEM] + [HBM] * 4 + [VMEM] * (1 + len(asks)),
            out_specs=[VMEM] * len(outs),
            out_shape=outs,
            scratch_shapes=[
                pltpu.VMEM((rows, width), bf16),
                pltpu.VMEM((1, width), f32),
                pltpu.VMEM((2, rows, HEAD_DIM), f32),
                pltpu.VMEM((rows + (16 if asks else 0), width), bf16),
                pltpu.SemaphoreType.DMA((4,)),
            ],
            compiler_params=params(8),
            name="project",
        )(idx, x, stay(gain_row), stay(cos_t), stay(sin_t), near(wq), *asks)

    sib = project(1, sib_x, [])[0]
    asks = [lax.ppermute(ask, groups, perm) for perm in shift]

    cached = cache_k.shape[1]
    step_rows = min(2048, cached)
    count = cached // step_rows
    kv_width = heads * HEAD_DIM
    many = GROUP * steps * heads
    half_rows = n_rows // 2

    def decode(part):
        loads = part == 0
        return pl.pallas_call(
            functools.partial(decode_kernel, part * half_rows, loads),
            in_specs=[SMEM] * 2 + [VMEM] * 2 + [HBM] * (3 if loads else 2),
            out_specs=[VMEM] * (2 if loads else 1),
            out_shape=[
                jax.ShapeDtypeStruct((decs, attn_cols), f32),
                pltpu.VMEM((out_blocks, attn_cols, OUT_COLS), bf16),
            ][: 2 if loads else 1],
            scratch_shapes=[
                pltpu.VMEM((half_rows, count, step_rows, kv_width), bf16),
                pltpu.VMEM((half_rows, count, step_rows, kv_width), bf16),
                pltpu.VMEM((half_rows, many, kv_width), bf16),
                pltpu.VMEM((half_rows, 16, kv_width), bf16),
                pltpu.VMEM((half_rows, 16, kv_width), bf16),
                pltpu.VMEM((half_rows, many, 1), f32),
                pltpu.VMEM((half_rows, many, 1), f32),
                pltpu.VMEM((half_rows, many, kv_width), f32),
                pltpu.SemaphoreType.DMA((half_rows, count)),
                pltpu.SemaphoreType.DMA((half_rows, count)),
            ] + ([pltpu.SemaphoreType.DMA((out_blocks,))] if loads else []),
            compiler_params=params(12),
            name="decode",
        )(
            cache_len, slot, raw, dec_angle, stay(cache_k), stay(cache_v),
            *([stay(w_out)] if loads else []),
        )

    dec_low, wo = decode(0)
    dec_high = decode(1)[0]

    def chunk(n, kvs, asks, kv_only):
        passed = lax.ppermute(far_x[n], "blk", swap)
        direct, *news = project(2 + 2 * n, far_x[n], asks)
        outs = [jax.ShapeDtypeStruct((2 * heads, rows, PAIR), bf16)]
        scratch = [
            pltpu.VMEM((rows, width), bf16),
            pltpu.VMEM((1, width), f32),
            pltpu.VMEM((2, rows, HEAD_DIM), f32),
            pltpu.VMEM((rows, width), bf16),
            pltpu.VMEM((blocks, rows, PAIR), bf16),
            pltpu.SemaphoreType.DMA((4,)),
        ]
        if not kv_only:
            outs += [jax.ShapeDtypeStruct((rows, width), bf16)] * 2
            scratch.append(pltpu.VMEM((2 * rows, attn_cols), bf16))
        extra = []
        if asks:
            outs.append(jax.ShapeDtypeStruct((decs, attn_cols), bf16))
            extra = [*news, new_angle]
        kernel = functools.partial(chunk_kernel, n, 2, len(kvs), len(asks), kv_only)
        return pl.pallas_call(
            kernel,
            in_specs=[SMEM] * 2 + [HBM] * 4 + [VMEM] * (5 + len(kvs) + len(extra)),
            out_specs=[VMEM] * len(outs),
            out_shape=outs,
            scratch_shapes=scratch,
            compiler_params=params(16),
            name="chunk",
        )(
            idx, prompt_len, passed, stay(gain_row), stay(cos_t), stay(sin_t),
            direct, near(wq), near(wo), own, sib, *kvs, *extra,
        )

    def add(a, b, start=0):
        return pl.pallas_call(
            functools.partial(add_kernel, start),
            in_specs=[VMEM] * 2,
            out_specs=VMEM,
            out_shape=jax.ShapeDtypeStruct(a.shape, bf16),
            compiler_params=params(8),
            name="add",
        )(a, b)

    kvs, back, fresh = [], [], None
    ahead = n_chip > 2
    if ahead:
        kvs = [chunk(n, [], [], True)[0] for n in range(n_chip - 1)]
    for n in range(n_chip - 1):
        final = n == n_chip - 2
        others = [kv for i, kv in enumerate(kvs) if i != n]
        outs = chunk(n, others, asks if final else [], False)
        if not ahead:
            kvs.append(outs[0])
        if final:
            fresh = outs[3]
        other = lax.ppermute(outs[2], "blk", swap)
        both = add(outs[1], other)
        back.append(lax.ppermute(both, "blk", hop(n_chip - 1 - n)))

    rets = [lax.ppermute(fresh, groups, perm) for perm in shift]
    own_part, sib_part, dec_part = pl.pallas_call(
        functools.partial(last_kernel, len(kvs), n_batch, n_rows),
        in_specs=[SMEM] * 4 + [VMEM] * (5 + len(kvs) + n_batch),
        out_specs=[VMEM] * 3,
        out_shape=[
            jax.ShapeDtypeStruct((rows, width), bf16),
            jax.ShapeDtypeStruct((rows + decs, width), bf16),
            jax.ShapeDtypeStruct((decs, width), bf16),
        ],
        scratch_shapes=[
            pltpu.VMEM((2 * rows + decs, attn_cols), bf16),
        ],
        compiler_params=params(12),
        name="last",
    )(idx, prompt_len, slot, assign, own, sib, *kvs, dec_low, dec_high, *rets, near(wo))
    from_sib = lax.ppermute(sib_part, "blk", swap)

    total = add(dec_part, from_sib, rows)
    reach = 1
    while reach < n_chip:
        other = lax.ppermute(total, "blk", [(i, i ^ (2 * reach)) for i in range(n_blk)])
        reach *= 2
        if reach < n_chip:
            total = add(total, other)
    dec_out = pl.pallas_call(
        dec_kernel,
        in_specs=[VMEM] * 3,
        out_specs=VMEM,
        out_shape=jax.ShapeDtypeStruct(dec_tokens.shape, bf16),
        compiler_params=params(8),
        name="dec",
    )(dec_tokens, total, other)
    base = pl.pallas_call(
        base_kernel,
        in_specs=[HBM, VMEM, VMEM],
        out_specs=VMEM,
        out_shape=jax.ShapeDtypeStruct((rows, width), f32),
        scratch_shapes=[pltpu.VMEM((rows, width), bf16), pltpu.SemaphoreType.DMA],
        compiler_params=params(8),
        name="base",
    )(stay(shard), own_part, from_sib)
    pieces = 4
    result = pl.pallas_call(
        functools.partial(sum_kernel, n_chip - 1),
        in_specs=[VMEM] + [HBM] * len(back),
        out_specs=HBM,
        out_shape=jax.ShapeDtypeStruct((rows, width), bf16),
        scratch_shapes=[
            pltpu.VMEM((n_chip - 1, rows, width), bf16),
            pltpu.SemaphoreType.DMA((n_chip - 1, pieces)),
            pltpu.SemaphoreType.DMA((pieces,)),
        ],
        compiler_params=params(10),
        name="sum",
    )(base, *back)
    return (result[None], dec_out)


def solution(mesh):
    return jax.shard_map(
        layer,
        mesh=mesh,
        in_specs=(
            P(("pool", "batch"), "blk", None),
            P("pool", "batch"),
            P(None, ("pool", "batch"), None),
            P(("pool", "batch"), None, "blk"),
            P(("pool", "batch"), None, "blk"),
            P(("pool", "batch")),
            P("pool", "batch"),
            P("pool", "batch"),
            P(),
            P(None, "blk"),
            P("blk", None),
        ),
        out_specs=(P(("pool", "batch"), "blk", None), P(None, ("pool", "batch"), None)),
        check_vma=False,
    )
```

time: 124 us -> 122 us (0.984)
  starting transfers between devices: 32.1 us -> 22.4 us
  waiting for transfers between devices: 38.3 us -> 47.1 us
    ppermute x8 -> x4, waiting for transfers between devices: 11.9 us -> 23.4 us  [the longest x1 23.4 us: layer(): far_x.append(lax.ppermute(shard, 'blk', hop(d)))]
    ppermute x8 -> x4, starting transfers between devices: 15.3 us -> 4.66 us  [the longest x1 3.03 us: layer(): far_x.append(lax.ppermute(shard, 'blk', hop(d)))]
    ppermute x4, waiting for transfers between devices: 2.93 us -> 0.01 us  [layer(): asks = [lax.ppermute(ask, groups, perm) for perm in shift]]
    ppermute x4, starting transfers between devices: 6.14 us -> 8.84 us  [layer(): rets = [lax.ppermute(fresh, groups, perm) for perm in shift]]
    ppermute x4, starting transfers between devices: 9.41 us -> 7.28 us  [layer(): asks = [lax.ppermute(ask, groups, perm) for perm in shift]]
    pallas_call x5 -> x7, Pallas kernels: 38.8 us -> 39.8 us  [the longest x2 13.5 us: decode(): pl.pallas_call(functools.partial(decode_kernel, part * half_rows, loads),...]
  transfers between devices with their start and end apart: 19 -> 15, of which waited for: 6 -> 3; matrix products, arithmetic and copies ran while one was open for 2% -> 1% of each run, Pallas kernels for 31% -> 31%
where the time goes in v2:
time: 122 us; the launch traced here: 121 us
  Pallas kernels  47.6 us (39%)
  waiting for transfers between devices  47.1 us (39%)
  starting transfers between devices  22.4 us (18%)
  between operations  2.97 us (2%)
    ppermute x1, waiting for transfers between devices, layer(): far_x.append(lax.ppermute(shard, 'blk', hop(d)))  23.4 us
    ppermute x1, waiting for transfers between devices, layer(): lax.ppermute(total, 'blk', [(i, i ^ 2 * reach) for i in range(n_blk)])  22.7 us
    pallas_call x2, Pallas kernels, decode(): pl.pallas_call(functools.partial(decode_kernel, part * half_rows, loads),...  13.5 us
    ppermute x4, starting transfers between devices, layer(): rets = [lax.ppermute(fresh, groups, perm) for perm in shift]  8.84 us
    pallas_call x1, Pallas kernels, chunk(): pl.pallas_call(kernel, in_specs=[SMEM] * 2 + [HBM] * 4 + [VMEM] * (5 + le...  8.69 us
    pallas_call x2, Pallas kernels, project(): pl.pallas_call(functools.partial(project_kernel, which, len(asks)), in_sp...  8.61 us
    pallas_call x1, Pallas kernels, layer(): pl.pallas_call(first_kernel, in_specs=[SMEM] * 3 + [HBM] * 6 + [ANY], out...  7.83 us
    ppermute x4, starting transfers between devices, layer(): asks = [lax.ppermute(ask, groups, perm) for perm in shift]  7.28 us
  transfers between devices with their start and end apart: 15, of which 3 were waited for; matrix products, arithmetic and copies ran while one was open for 1% of the time, Pallas kernels for 31%

profile of v2, /device:TPU:0, one launch (start us, length us, event | category | flops | bytes accessed | tf_op | source)
XLA Modules:
  0.0 121.0 jit_solution(9525284481293812016)
XLA Ops:
  0.6 0.0 copy-start.1
  0.6 3.0 %collective-permute-start.1 = (bf16[128,4096]{1,0:T(8,128)(2,1)}, bf16[128,4096]{1,0:T(8,128)(2,1)S(1)}, u32[]{:S(2)}, u32[]{:S(2)}) collective-permute-start(bf16[128,4096]{1,0:T(8,128)(2,1)} %bitcast.7), channel_id=1, source_target_pairs={{0,8},{4,12},{8,0},{12,4},{1,9},{5,13},{9,1},{13,5},{2,10},{6,14},... | collective-permute-start | bytes 3145736 | tf_op jit(solution)/shard_map/ppermute | solution.py:563
  3.7 0.0 collective-permute-start
  3.7 23.4 %collective-permute-done.1.refs_1_ = bf16[128,4096]{1,0:T(8,128)(2,1)S(1)} collective-permute-done((bf16[128,4096]{1,0:T(8,128)(2,1)}, bf16[128,4096]{1,0:T(8,128)(2,1)S(1)}, u32[]{:S(2)}, u32[]{:S(2)}) %collective-permute-start.1) | collective-permute-done | bytes 1048608 | tf_op jit(solution)/shard_map/ppermute | solution.py:563
  27.0 0.0 collective-permute-start.2
  29.0 0.7 pad_add_fusion
  29.8 0.1 add_convert_fusion
  29.8 0.2 fusion._
  30.0 7.8 %first.1 = (bf16[6,128,256]{2,1,0:T(8,128)(2,1)S(1)}, f32[4,6,4,256]{3,2,1,0:T(4,128)S(1)}, bf16[6,4096,256]{2,1,0:T(8,128)(2,1)S(1)}, bf16[8,4096]{1,0:T(8,128)(2,1)S(1)}) custom-call(s32[5]{0:T(128)S(1)} %compare_select_fusion.4.idx.refs_0_, s32[1,1]{1,0:T(1,128)S(6)} %copy.17.slot.refs_1_.refs_2_, s32[1,1]{1,0:T(1,128)S(6)} %copy.16.assign.refs_3_, ...), custom_call_target="tpu_custom_call" | custom-call | tf_op jit(solution)/shard_map/first/pallas_call | solution.py:565
  37.8 4.9 %collective-permute-start.6 = (bf16[8,4096]{1,0:T(8,128)(2,1)S(1)}, bf16[8,4096]{1,0:T(8,128)(2,1)S(1)}, u32[]{:S(2)}, u32[]{:S(2)}) collective-permute-start(bf16[8,4096]{1,0:T(8,128)(2,1)S(1)} %get-tuple-element.19), channel_id=1, source_target_pairs={{0,19},{1,16},{2,17},{3,18},{16,3},{17,0},{18,1},{19,2},{4,23},{5,... | collective-permute-start | bytes 196616 | tf_op jit(solution)/shard_map/ppermute | solution.py:612
  42.7 0.0 collective-permute-start.5
  42.7 1.9 %collective-permute-start.4 = (bf16[8,4096]{1,0:T(8,128)(2,1)S(1)}, bf16[8,4096]{1,0:T(8,128)(2,1)S(1)}, u32[]{:S(2)}, u32[]{:S(2)}) collective-permute-start(bf16[8,4096]{1,0:T(8,128)(2,1)S(1)} %get-tuple-element.19), channel_id=1, source_target_pairs={{0,17},{1,18},{2,19},{3,16},{16,1},{17,2},{18,3},{19,0},{4,21},{5,... | collective-permute-start | bytes 196616 | tf_op jit(solution)/shard_map/ppermute | solution.py:612
  44.6 0.0 collective-permute-done.refs_1_
  44.6 0.5 collective-permute-start.3
  45.1 0.0 copy-done.1
  45.1 6.6 %decode.2 = (f32[16,1024]{1,0:T(8,128)S(1)}, bf16[4,1024,1024]{2,1,0:T(8,128)(2,1)S(1)}) custom-call(s32[4]{0:T(128)S(1)} %copy-done.1, s32[1,1]{1,0:T(1,128)S(6)} %copy.17.slot.refs_1_.refs_2_, f32[4,6,4,256]{3,2,1,0:T(4,128)S(1)} %get-tuple-element.21.refs_2_, f32[4,4,128]{2,1,0:T(4,128)S(1)} %slice.8.refs_3_, bf16[4,4096,256]{2,1,0:T(8,128)(2,1)} %refs_4_.6, ...), custom_call_target="tpu_custom_call" | custom-call | tf_op jit(solution)/shard_map/decode/pallas_call | solution.py:623
  51.7 4.1 %project.2.refs_10_.refs_5_ = bf16[6,128,256]{2,1,0:T(8,128)(2,1)S(1)} custom-call(s32[5]{0:T(128)S(1)} %compare_select_fusion.4.idx.refs_0_, bf16[128,4096]{1,0:T(8,128)(2,1)S(1)} %collective-permute-done.refs_1_, f32[1,4096]{1,0:T(1,128)} %bitcast.13, f32[512,128]{1,0:T(8,128)} %constant.83.clone.cos_hbm.refs_3_.refs_4_, ...), custom_call_target="tpu_custom_call" | custom-call | tf_op jit(solution)/shard_map/project/pallas_call | solution.py:595
  55.8 0.0 collective-permute-done.6.refs_9_
  55.8 0.0 collective-permute-done.5.refs_8_
  55.8 0.0 collective-permute-done.4.refs_7_
  55.8 0.0 collective-permute-done.3.refs_6_
  55.8 4.6 %project.3 = (bf16[6,128,256]{2,1,0:T(8,128)(2,1)S(1)}, f32[6,8,256]{2,1,0:T(8,128)S(1)}) custom-call(s32[5]{0:T(128)S(1)} %compare_select_fusion.4.idx.refs_0_, bf16[128,4096]{1,0:T(8,128)(2,1)S(1)} %collective-permute-done.1.refs_1_, f32[1,4096]{1,0:T(1,128)} %bitcast.14, f32[512,128]{1,0:T(8,128)} %constant.83.clone.cos_hbm.refs_3_.refs_4_, ...), custom_call_target="tpu_custom_call" | custom-call | tf_op jit(solution)/shard_map/project/pallas_call | solution.py:595
  60.4 0.0 collective-permute-done.2.refs_2_
  60.4 8.7 %chunk.1 = (bf16[4,128,256]{2,1,0:T(8,128)(2,1)S(1)}, bf16[128,4096]{1,0:T(8,128)(2,1)S(1)}, bf16[128,4096]{1,0:T(8,128)(2,1)S(1)}, bf16[16,1024]{1,0:T(8,128)(2,1)S(1)}) custom-call(s32[5]{0:T(128)S(1)} %compare_select_fusion.4.idx.refs_0_, s32[1,1]{1,0:T(1,128)} %copy.15.refs_1_, bf16[128,4096]{1,0:T(8,128)(2,1)S(1)} %collective-permute-done.2.refs_2_, ...), custom_call_target="tpu_custom_call" | custom-call | tf_op jit(solution)/shard_map/chunk/pallas_call | solution.py:673
  69.1 0.1 collective-permute-start.12
  69.2 4.7 %collective-permute-start.10 = (bf16[16,1024]{1,0:T(8,128)(2,1)S(1)}, bf16[16,1024]{1,0:T(8,128)(2,1)S(1)}, u32[]{:S(2)}, u32[]{:S(2)}) collective-permute-start(bf16[16,1024]{1,0:T(8,128)(2,1)S(1)} %get-tuple-element.26), channel_id=1, source_target_pairs={{0,19},{1,16},{2,17},{3,18},{16,3},{17,0},{18,1},{19,2},{4,23},{5,... | collective-permute-start | bytes 98312 | tf_op jit(solution)/shard_map/ppermute | solution.py:712
  73.9 1.6 %collective-permute-start.9 = (bf16[16,1024]{1,0:T(8,128)(2,1)S(1)}, bf16[16,1024]{1,0:T(8,128)(2,1)S(1)}, u32[]{:S(2)}, u32[]{:S(2)}) collective-permute-start(bf16[16,1024]{1,0:T(8,128)(2,1)S(1)} %get-tuple-element.26), channel_id=1, source_target_pairs={{0,18},{1,19},{2,16},{3,17},{16,2},{17,3},{18,0},{19,1},{4,22},{5,... | collective-permute-start | bytes 98312 | tf_op jit(solution)/shard_map/ppermute | solution.py:712
  75.5 0.0 collective-permute-start.8
  75.5 2.5 %collective-permute-start.7 = (bf16[16,1024]{1,0:T(8,128)(2,1)S(1)}, bf16[16,1024]{1,0:T(8,128)(2,1)S(1)}, u32[]{:S(2)}, u32[]{:S(2)}) collective-permute-start(bf16[16,1024]{1,0:T(8,128)(2,1)S(1)} %get-tuple-element.26), channel_id=1, source_target_pairs={{0,16},{1,17},{2,18},{3,19},{16,0},{17,1},{18,2},{19,3},{4,20},{5,... | collective-permute-start | bytes 98312 | tf_op jit(solution)/shard_map/ppermute | solution.py:712
  78.0 6.9 %decode.3.refs_8_ = f32[16,1024]{1,0:T(8,128)S(1)} custom-call(s32[4]{0:T(128)S(1)} %copy-done.1, s32[1,1]{1,0:T(1,128)S(6)} %copy.17.slot.refs_1_.refs_2_, f32[4,6,4,256]{3,2,1,0:T(4,128)S(1)} %get-tuple-element.21.refs_2_, f32[4,4,128]{2,1,0:T(4,128)S(1)} %slice.8.refs_3_, bf16[4,4096,256]{2,1,0:T(8,128)(2,1)} %refs_4_.6, bf16[4,4096,256]{2,1,0:T(8,128)(2,1)} %refs_5_.4), custom_call_target="tpu_custom_call" | custom-call | tf_op jit(solution)/shard_map/decode/pallas_call | solution.py:623
  84.9 0.0 collective-permute-done.10.refs_12_
  84.9 0.0 collective-permute-done.9.refs_11_
  84.9 0.0 collective-permute-done.8.refs_10_
  84.9 0.0 collective-permute-done.7.refs_9_
  85.0 0.0 copy-start
  85.0 5.1 %last.1 = (bf16[128,4096]{1,0:T(8,128)(2,1)S(1)}, bf16[144,4096]{1,0:T(8,128)(2,1)S(1)}, bf16[16,4096]{1,0:T(8,128)(2,1)S(1)}) custom-call(s32[5]{0:T(128)S(1)} %compare_select_fusion.4.idx.refs_0_, s32[1,1]{1,0:T(1,128)} %copy.15.refs_1_, s32[1,1]{1,0:T(1,128)S(6)} %copy.17.slot.refs_1_.refs_2_, s32[1,1]{1,0:T(1,128)S(6)} %copy.16.assign.refs_3_, ...), custom_call_target="tpu_custom_call" | custom-call | tf_op jit(solution)/shard_map/last/pallas_call | solution.py:713
  90.1 0.1 collective-permute-start.11
  90.1 0.0 collective-permute-done.12.b
  90.2 0.3 add.97
  90.4 1.6 %collective-permute-start.13 = (bf16[128,4096]{1,0:T(8,128)(2,1)S(1)}, bf16[128,4096]{1,0:T(8,128)(2,1)S(1)}, u32[]{:S(2)}, u32[]{:S(2)}) collective-permute-start(bf16[128,4096]{1,0:T(8,128)(2,1)S(1)} %add.97), channel_id=1, source_target_pairs={{0,8},{4,12},{8,0},{12,4},{1,9},{5,13},{9,1},{13,5},{2,10},{6,14},... | collective-permute-start | bytes 3145736 | tf_op jit(solution)/shard_map/ppermute | solution.py:710
  92.0 1.0 collective-permute-done.11.sib.b
  93.0 1.6 %collective-permute-start.14 = (bf16[16,4096]{1,0:T(8,128)(2,1)S(1)}, bf16[16,4096]{1,0:T(8,128)(2,1)S(1)}, u32[]{:S(2)}, u32[]{:S(2)}) collective-permute-start(bf16[16,4096]{1,0:T(8,128)(2,1)S(1)} %add.98.a), channel_id=1, source_target_pairs={{0,8},{4,12},{8,0},{12,4},{1,9},{5,13},{9,1},{13,5},{2,10},{6,14},... | collective-permute-start | bytes 393224 | tf_op jit(solution)/shard_map/ppermute | solution.py:733
  94.6 1.6 %base.1 = f32[128,4096]{1,0:T(8,128)S(1)} custom-call(bf16[128,4096]{1,0:T(8,128)(2,1)} %bitcast.10, bf16[128,4096]{1,0:T(8,128)(2,1)S(1)} %get-tuple-element.27.own, bf16[144,4096]{1,0:T(8,128)(2,1)S(1)} %collective-permute-done.11.sib.b), custom_call_target="tpu_custom_call" | custom-call | tf_op jit(solution)/shard_map/base/pallas_call | solution.py:745
  96.2 22.7 %collective-permute-done.14.b = bf16[16,4096]{1,0:T(8,128)(2,1)S(1)} collective-permute-done((bf16[16,4096]{1,0:T(8,128)(2,1)S(1)}, bf16[16,4096]{1,0:T(8,128)(2,1)S(1)}, u32[]{:S(2)}, u32[]{:S(2)}) %collective-permute-start.14) | collective-permute-done | bytes 131104 | tf_op jit(solution)/shard_map/ppermute | solution.py:733
  118.9 0.0 copy-done
  118.9 0.7 dec.1
  119.6 0.0 collective-permute-done.13.refs_0_
  119.6 1.2 %sum.1 = bf16[128,4096]{1,0:T(8,128)(2,1)} custom-call(f32[128,4096]{1,0:T(8,128)S(1)} %base.1, bf16[128,4096]{1,0:T(8,128)(2,1)S(1)} %collective-permute-done.13.refs_0_), custom_call_target="tpu_custom_call" | custom-call | tf_op jit(solution)/shard_map/sum/pallas_call | solution.py:755
  (6 shorter events, 0.1 us)
Async XLA Ops:
  0.6 44.5 %copy-start.1 = (s32[4]{0:T(128)S(1)}, s32[4]{0:T(128)}, u32[]{:S(2)}) copy-start(s32[4]{0:T(128)} %refs_0_.3) | copy-start | bytes 52
  0.6 26.4 %collective-permute-start.1 = (bf16[128,4096]{1,0:T(8,128)(2,1)}, bf16[128,4096]{1,0:T(8,128)(2,1)S(1)}, u32[]{:S(2)}, u32[]{:S(2)}) collective-permute-start(bf16[128,4096]{1,0:T(8,128)(2,1)} %bitcast.7), channel_id=1, source_target_pairs={{0,8},{4,12},{8,0},{12,4},{1,9},{5,13},{9,1},{13,5},{2,10},{6,14},... | collective-permute-start | bytes 3145736 | tf_op jit(solution)/shard_map/ppermute | solution.py:563
  3.7 40.9 %collective-permute-start = (bf16[128,4096]{1,0:T(8,128)(2,1)}, bf16[128,4096]{1,0:T(8,128)(2,1)S(1)}, u32[]{:S(2)}, u32[]{:S(2)}) collective-permute-start(bf16[128,4096]{1,0:T(8,128)(2,1)} %bitcast.8), channel_id=1, source_target_pairs={{0,4},{4,0},{8,12},{12,8},{1,5},{5,1},{9,13},{13,9},{2,6},{6,2},{1... | collective-permute-start | bytes 3145736 | tf_op jit(solution)/shard_map/ppermute | solution.py:560
  27.0 33.4 %collective-permute-start.2 = (bf16[128,4096]{1,0:T(8,128)(2,1)S(1)}, bf16[128,4096]{1,0:T(8,128)(2,1)S(1)}, u32[]{:S(2)}, u32[]{:S(2)}) collective-permute-start(bf16[128,4096]{1,0:T(8,128)(2,1)S(1)} %collective-permute-done.1.refs_1_), channel_id=1, source_target_pairs={{0,4},{4,0},{8,12},{12,8},{1,5},{5,1},{9,13},{13,9},{2,6},{6,2},{1... | collective-permute-start | bytes 3145736 | tf_op jit(solution)/shard_map/ppermute | solution.py:654
  37.8 18.0 %collective-permute-start.6 = (bf16[8,4096]{1,0:T(8,128)(2,1)S(1)}, bf16[8,4096]{1,0:T(8,128)(2,1)S(1)}, u32[]{:S(2)}, u32[]{:S(2)}) collective-permute-start(bf16[8,4096]{1,0:T(8,128)(2,1)S(1)} %get-tuple-element.19), channel_id=1, source_target_pairs={{0,19},{1,16},{2,17},{3,18},{16,3},{17,0},{18,1},{19,2},{4,23},{5,... | collective-permute-start | bytes 196616 | tf_op jit(solution)/shard_map/ppermute | solution.py:612
  42.7 13.1 %collective-permute-start.5 = (bf16[8,4096]{1,0:T(8,128)(2,1)S(1)}, bf16[8,4096]{1,0:T(8,128)(2,1)S(1)}, u32[]{:S(2)}, u32[]{:S(2)}) collective-permute-start(bf16[8,4096]{1,0:T(8,128)(2,1)S(1)} %get-tuple-element.19), channel_id=1, source_target_pairs={{0,18},{1,19},{2,16},{3,17},{16,2},{17,3},{18,0},{19,1},{4,22},{5,... | collective-permute-start | bytes 196616 | tf_op jit(solution)/shard_map/ppermute | solution.py:612
  42.7 13.1 %collective-permute-start.4 = (bf16[8,4096]{1,0:T(8,128)(2,1)S(1)}, bf16[8,4096]{1,0:T(8,128)(2,1)S(1)}, u32[]{:S(2)}, u32[]{:S(2)}) collective-permute-start(bf16[8,4096]{1,0:T(8,128)(2,1)S(1)} %get-tuple-element.19), channel_id=1, source_target_pairs={{0,17},{1,18},{2,19},{3,16},{16,1},{17,2},{18,3},{19,0},{4,21},{5,... | collective-permute-start | bytes 196616 | tf_op jit(solution)/shard_map/ppermute | solution.py:612
  44.6 11.2 %collective-permute-start.3 = (bf16[8,4096]{1,0:T(8,128)(2,1)S(1)}, bf16[8,4096]{1,0:T(8,128)(2,1)S(1)}, u32[]{:S(2)}, u32[]{:S(2)}) collective-permute-start(bf16[8,4096]{1,0:T(8,128)(2,1)S(1)} %get-tuple-element.19), channel_id=1, source_target_pairs={{0,16},{1,17},{2,18},{3,19},{16,0},{17,1},{18,2},{19,3},{4,20},{5,... | collective-permute-start | bytes 196616 | tf_op jit(solution)/shard_map/ppermute | solution.py:612
  69.1 21.0 %collective-permute-start.12 = (bf16[128,4096]{1,0:T(8,128)(2,1)S(1)}, bf16[128,4096]{1,0:T(8,128)(2,1)S(1)}, u32[]{:S(2)}, u32[]{:S(2)}) collective-permute-start(bf16[128,4096]{1,0:T(8,128)(2,1)S(1)} %get-tuple-element.30), channel_id=1, source_target_pairs={{0,4},{4,0},{8,12},{12,8},{1,5},{5,1},{9,13},{13,9},{2,6},{6,2},{1... | collective-permute-start | bytes 3145736 | tf_op jit(solution)/shard_map/ppermute | solution.py:708
  69.2 15.7 %collective-permute-start.10 = (bf16[16,1024]{1,0:T(8,128)(2,1)S(1)}, bf16[16,1024]{1,0:T(8,128)(2,1)S(1)}, u32[]{:S(2)}, u32[]{:S(2)}) collective-permute-start(bf16[16,1024]{1,0:T(8,128)(2,1)S(1)} %get-tuple-element.26), channel_id=1, source_target_pairs={{0,19},{1,16},{2,17},{3,18},{16,3},{17,0},{18,1},{19,2},{4,23},{5,... | collective-permute-start | bytes 98312 | tf_op jit(solution)/shard_map/ppermute | solution.py:712
  73.9 11.0 %collective-permute-start.9 = (bf16[16,1024]{1,0:T(8,128)(2,1)S(1)}, bf16[16,1024]{1,0:T(8,128)(2,1)S(1)}, u32[]{:S(2)}, u32[]{:S(2)}) collective-permute-start(bf16[16,1024]{1,0:T(8,128)(2,1)S(1)} %get-tuple-element.26), channel_id=1, source_target_pairs={{0,18},{1,19},{2,16},{3,17},{16,2},{17,3},{18,0},{19,1},{4,22},{5,... | collective-permute-start | bytes 98312 | tf_op jit(solution)/shard_map/ppermute | solution.py:712
  75.5 9.4 %collective-permute-start.8 = (bf16[16,1024]{1,0:T(8,128)(2,1)S(1)}, bf16[16,1024]{1,0:T(8,128)(2,1)S(1)}, u32[]{:S(2)}, u32[]{:S(2)}) collective-permute-start(bf16[16,1024]{1,0:T(8,128)(2,1)S(1)} %get-tuple-element.26), channel_id=1, source_target_pairs={{0,17},{1,18},{2,19},{3,16},{16,1},{17,2},{18,3},{19,0},{4,21},{5,... | collective-permute-start | bytes 98312 | tf_op jit(solution)/shard_map/ppermute | solution.py:712
  75.5 9.4 %collective-permute-start.7 = (bf16[16,1024]{1,0:T(8,128)(2,1)S(1)}, bf16[16,1024]{1,0:T(8,128)(2,1)S(1)}, u32[]{:S(2)}, u32[]{:S(2)}) collective-permute-start(bf16[16,1024]{1,0:T(8,128)(2,1)S(1)} %get-tuple-element.26), channel_id=1, source_target_pairs={{0,16},{1,17},{2,18},{3,19},{16,0},{17,1},{18,2},{19,3},{4,20},{5,... | collective-permute-start | bytes 98312 | tf_op jit(solution)/shard_map/ppermute | solution.py:712
  85.0 33.9 %copy-start = (bf16[4,4,4096]{2,1,0:T(4,128)(2,1)S(1)}, bf16[4,4,4096]{2,1,0:T(4,128)(2,1)}, u32[]{:S(2)}) copy-start(bf16[4,4,4096]{2,1,0:T(4,128)(2,1)} %tokens.1) | copy-start | bytes 393220
  90.1 2.9 %collective-permute-start.11 = (bf16[144,4096]{1,0:T(8,128)(2,1)S(1)}, bf16[144,4096]{1,0:T(8,128)(2,1)S(1)}, u32[]{:S(2)}, u32[]{:S(2)}) collective-permute-start(bf16[144,4096]{1,0:T(8,128)(2,1)S(1)} %get-tuple-element.28), channel_id=1, source_target_pairs={{0,4},{4,0},{8,12},{12,8},{1,5},{5,1},{9,13},{13,9},{2,6},{6,2},{1... | collective-permute-start | bytes 3538952 | tf_op jit(solution)/shard_map/ppermute | solution.py:728
  90.4 29.2 %collective-permute-start.13 = (bf16[128,4096]{1,0:T(8,128)(2,1)S(1)}, bf16[128,4096]{1,0:T(8,128)(2,1)S(1)}, u32[]{:S(2)}, u32[]{:S(2)}) collective-permute-start(bf16[128,4096]{1,0:T(8,128)(2,1)S(1)} %add.97), channel_id=1, source_target_pairs={{0,8},{4,12},{8,0},{12,4},{1,9},{5,13},{9,1},{13,5},{2,10},{6,14},... | collective-permute-start | bytes 3145736 | tf_op jit(solution)/shard_map/ppermute | solution.py:710
  93.0 25.8 %collective-permute-start.14 = (bf16[16,4096]{1,0:T(8,128)(2,1)S(1)}, bf16[16,4096]{1,0:T(8,128)(2,1)S(1)}, u32[]{:S(2)}, u32[]{:S(2)}) collective-permute-start(bf16[16,4096]{1,0:T(8,128)(2,1)S(1)} %add.98.a), channel_id=1, source_target_pairs={{0,8},{4,12},{8,0},{12,4},{1,9},{5,13},{9,1},{13,5},{2,10},{6,14},... | collective-permute-start | bytes 393224 | tf_op jit(solution)/shard_map/ppermute | solution.py:733

commit v3 on v2

--- a/solution.py
+++ b/solution.py
@@ -113,22 +113,21 @@
 
 
 def first_kernel(
-    idx, slot, assign, own_hbm, dec_hbm, gain_hbm, cos_hbm, sin_hbm, wq_hbm,
-    _, own_out, raw_out, wq, ask_out,
-    own, dec, gain, tabs, normed, q_sems, in_sems,
+    idx, slot, assign, own_hbm, sib_hbm, dec_hbm, gain_hbm, cos_hbm, sin_hbm, wq_hbm,
+    _a, _b, own_out, sib_out, raw_out, wq, ask_out,
+    own, sib, dec, gain, tabs, normed, q_sems, in_sems,
 ):
     rows = own.shape[0]
     steps, decs = dec.shape[:2]
-    at = pl.ds(pl.multiple_of(idx[0] * rows, rows), rows)
     weights = weight_copies(wq_hbm, wq, q_sems, PAIR)
-    ready = load(
-        [
-            (gain_hbm, gain), (own_hbm, own), (dec_hbm, dec),
-            (cos_hbm.at[at], tabs.at[0]), (sin_hbm.at[at], tabs.at[1]),
-        ],
-        in_sems,
-    )
+    ready = load([(gain_hbm, gain), (own_hbm, own), (dec_hbm, dec), (sib_hbm, sib)], in_sems)
     weights[0].start()
+    for i in range(2):
+        at = pl.ds(pl.multiple_of(idx[i] * rows, rows), rows)
+        ready += load(
+            [(cos_hbm.at[at], tabs.at[2 * i]), (sin_hbm.at[at], tabs.at[2 * i + 1])],
+            in_sems.at[pl.ds(4 + 2 * i, 2)],
+        )
     ready[0].wait()
     ready[1].wait()
     for copy in weights[1:4]:
@@ -136,7 +135,7 @@
     norm_rows(own, normed, 0, gain)
     ready[2].wait()
     tokens = [dec[s].astype(f32) for s in range(steps)]
-    normed[rows:] = norm_token_rows(tokens, gain)
+    normed[2 * rows :] = norm_token_rows(tokens, gain)
     fresh = []
     for s in range(steps):
         row = tokens[s][:1]
@@ -145,7 +144,9 @@
         fresh.append(row)
     fresh.append(jnp.full((steps, dec.shape[2]), assign[0, 0].astype(f32)))
     ask_out[...] = jnp.concatenate(fresh, axis=0).astype(bf16)
-    for copy in ready[3:]:
+    ready[3].wait()
+    norm_rows(sib, normed, rows, gain)
+    for copy in ready[4:]:
         copy.wait()
     for j in range(wq.shape[0]):
         weights[j].wait()
@@ -153,20 +154,22 @@
             weights[j + 4].start()
         acc = dot(normed[...], wq[j])
         own_out[j] = rotated_pair(acc[:rows], tabs.at[0], tabs.at[1], j)
+        sib_out[j] = rotated_pair(acc[rows : 2 * rows], tabs.at[2], tabs.at[3], j)
         for r in range(decs):
             for s in range(steps):
-                row = rows + s * decs + r
+                row = 2 * rows + s * decs + r
                 raw_out[r, j, s : s + 1] = acc[row : row + 1]
 
 
-def project_kernel(which, n_ask, *refs):
+def project_kernel(which, loads, *refs):
     refs = list(refs)
     take = lambda n: [refs.pop(0) for _ in range(n)]
     idx, x_hbm, gain_hbm, cos_hbm, sin_hbm, wq = take(6)
-    asks = take(n_ask)
+    wo_hbm = take(1)[0] if loads else None
     out = take(1)[0]
-    raw_out = take(1)[0] if n_ask else None
+    wo = take(1)[0] if loads else None
     x, gain, tabs, normed, in_sem = take(5)
+    weights = weight_copies(wo_hbm, wo, take(1)[0], OUT_COLS) if loads else []
     rows = x.shape[0]
     at = pl.ds(pl.multiple_of(idx[which] * rows, rows), rows)
     ready = load(
@@ -174,24 +177,16 @@
         in_sem,
     )
     ready[0].wait()
-    if n_ask:
-        here = idx[idx.shape[0] - 1].astype(f32)
-        steps = asks[0].shape[0] // 2
-        new = jnp.zeros((steps, x.shape[1]), f32)
-        for ref in asks:
-            wide = ref[...].astype(f32)
-            new = jnp.where(wide[steps : steps + 1] == here, wide[:steps], new)
-        fill = jnp.zeros((16 - steps, x.shape[1]), f32)
-        normed[rows:] = norm_token_rows([new, fill], gain)
     ready[1].wait()
+    for copy in weights:
+        copy.start()
     norm_rows(x, normed, 0, gain)
     for copy in ready[2:]:
         copy.wait()
     for j in range(wq.shape[0]):
-        acc = dot(normed[...], wq[j])
-        out[j] = rotated_pair(acc[:rows], tabs.at[0], tabs.at[1], j)
-        if n_ask:
-            raw_out[j] = acc[rows : rows + raw_out.shape[1]]
+        out[j] = rotated_pair(dot(normed[...], wq[j]), tabs.at[0], tabs.at[1], j)
+    for copy in weights:
+        copy.wait()
 
 
 def own_tail(q, k_own, steps):
@@ -218,15 +213,12 @@
     return key, value
 
 
-def decode_kernel(first, loads, *refs):
+def decode_kernel(first, *refs):
     refs = list(refs)
     take = lambda n: [refs.pop(0) for _ in range(n)]
     lens, slot, raw_ref, angle_ref, k_hbm, v_hbm = take(6)
-    wo_hbm = take(1)[0] if loads else None
     out_ref = take(1)[0]
-    wo = take(1)[0] if loads else None
     k_s, v_s, q_s, ko_s, vo_s, m_s, l_s, acc_s, k_sem, v_sem = take(10)
-    o_sem = take(1)[0] if loads else None
     group = raw_ref.shape[0]
     n_rows, count, width = k_s.shape[:3]
     steps = raw_ref.shape[2]
@@ -251,7 +243,6 @@
                 for copy in copies(r, j):
                     copy.start()
 
-    weights = weight_copies(wo_hbm, wo, o_sem, OUT_COLS) if loads else []
     fetch(0)
     for r in range(n_rows):
         raw = lambda b, r=r: raw_ref[first + r, b]
@@ -291,9 +282,6 @@
                 v_copy.wait()
                 acc_s[r] = acc_s[r] * fade + dot(e.astype(bf16), v_s[r, j])
 
-        for copy in weights[r * len(weights) // n_rows : (r + 1) * len(weights) // n_rows]:
-            copy.start()
-
     for r in range(n_rows):
         mixed = acc_s[r] / l_s[r]
         for h in range(heads):
@@ -305,8 +293,6 @@
                     out_ref[row : row + 1, to : to + HEAD_DIM] = mixed[
                         at : at + 1, h * HEAD_DIM : (h + 1) * HEAD_DIM
                     ]
-    for copy in weights:
-        copy.wait()
 
 
 def attend(queries, q_shard, pieces, plen, out_ref, offset, heads):
@@ -375,12 +361,14 @@
     take = lambda n: [refs.pop(0) for _ in range(n)]
     idx, plen, passed, gain_hbm, cos_hbm, sin_hbm, direct, wq, wo = take(9)
     full, kvs = take(n_full), take(n_kv)
-    raw_s, new_angle = take(2) if n_ask else (None, None)
+    asks = take(n_ask)
+    new_angle = take(1)[0] if n_ask else None
     kv_out = take(1)[0]
     direct_out, passed_out = (None,) * 2 if kv_only else take(2)
     new_out = take(1)[0] if n_ask else None
     x, gain, tabs, normed, qkv, in_sem = take(6)
     attn = None if kv_only else take(1)[0]
+    raw_s = take(1)[0] if n_ask else None
     rows = x.shape[0]
     heads = kv_out.shape[0] // 2
     shards = [idx[n_full + 2 * which + i] for i in range(2)]
@@ -390,12 +378,24 @@
         in_sem,
     )
     ready[0].wait()
+    if n_ask:
+        here = idx[idx.shape[0] - 1].astype(f32)
+        steps = asks[0].shape[0] // 2
+        new = jnp.zeros((steps, x.shape[1]), f32)
+        for ref in asks:
+            wide = ref[...].astype(f32)
+            new = jnp.where(wide[steps : steps + 1] == here, wide[:steps], new)
+        fill = jnp.zeros((16 - steps, x.shape[1]), f32)
+        normed[rows:] = norm_token_rows([new, fill], gain)
     ready[1].wait()
     norm_rows(x, normed, 0, gain)
     for copy in ready[2:]:
         copy.wait()
     for j in range(wq.shape[0]):
-        qkv[j] = rotated_pair(dot(normed[...], wq[j]), tabs.at[0], tabs.at[1], j)
+        acc = dot(normed[...], wq[j])
+        qkv[j] = rotated_pair(acc[:rows], tabs.at[0], tabs.at[1], j)
+        if n_ask:
+            raw_s[j] = acc[rows : rows + raw_s.shape[1]]
     both = (direct, qkv)
     for i in range(2):
         for h in range(heads):
@@ -422,7 +422,7 @@
         passed_out[:, cols] = part[rows:]
 
 
-def last_kernel(n_kv, n_ret, n_rows, *refs):
+def last_kernel(n_kv, n_ret, n_rows, low_rows, *refs):
     refs = list(refs)
     take = lambda n: [refs.pop(0) for _ in range(n)]
     idx, plen, slot, assign, own, sib = take(6)
@@ -443,7 +443,7 @@
     for k in range(1, n_ret):
         new = jnp.where(pick == k, rets[k][...].astype(f32), new)
     at = lax.rem(lax.broadcasted_iota(jnp.int32, new.shape, 0), n_rows)
-    dec = jnp.where(at < n_rows // 2, decs[0][...], decs[1][...])
+    dec = jnp.where(at < low_rows, decs[0][...], decs[1][...])
     attn[2 * rows :] = jnp.where(at == slot[0, 0], new, dec).astype(bf16)
     for j in range(wo.shape[0]):
         part = dot(attn[...], wo[j]).astype(bf16)
@@ -482,24 +482,22 @@
     parts, out, got, sems, out_sem = refs[:count], *refs[count:]
     pieces = sems.shape[1]
     rows = out.shape[0] // pieces
+    at = [pl.ds(n * rows, rows) for n in range(pieces)]
     copies = [
-        [
-            pltpu.make_async_copy(parts[d].at[pl.ds(n * rows, rows)], got.at[d, pl.ds(n * rows, rows)], sems.at[d, n])
-            for d in range(count)
-        ]
+        [pltpu.make_async_copy(part.at[at[n]], got.at[d, at[n]], sems.at[d, n]) for d, part in enumerate(parts)]
         for n in range(pieces)
     ]
     for copy in sum(copies, []):
         copy.start()
     done = []
     for n in range(pieces):
-        at = slice(n * rows, (n + 1) * rows)
-        total = base[at]
+        here = slice(n * rows, (n + 1) * rows)
+        total = base[here]
         for d in range(count):
             copies[n][d].wait()
-            total = total + got[d, at].astype(f32)
-        got[0, at] = total.astype(bf16)
-        done.append(pltpu.make_async_copy(got.at[0, pl.ds(n * rows, rows)], out.at[pl.ds(n * rows, rows)], out_sem.at[n]))
+            total = total + got[d, here].astype(f32)
+        got[0, here] = total.astype(bf16)
+        done.append(pltpu.make_async_copy(got.at[0, at[n]], out.at[at[n]], out_sem.at[n]))
         done[-1].start()
     for copy in done:
         copy.wait()
@@ -532,16 +530,16 @@
     decs = steps * n_rows
 
     blk = lax.axis_index("blk")
-    chip, core = blk // 2, blk % 2
+    chip, core = lax.shift_right_logical(blk, 1), blk & 1
     batch = lax.axis_index("batch")
     at = jnp.arange(n_blk + 1, dtype=jnp.int32)
-    far = (chip + n_chip - at // 2) % n_chip
-    idx = jnp.where(at == n_blk, batch, 2 * far + (core + at) % 2).astype(jnp.int32)
+    far = lax.rem(chip + n_chip - lax.shift_right_logical(at, 1), n_chip)
+    idx = jnp.where(at == n_blk, batch, 2 * far + ((core + at) & 1)).astype(jnp.int32)
     gain_row = gain.reshape(1, width)
     cos_t, sin_t = (jnp.asarray(t) for t in fixed_tables(n_blk * rows))
-    place = jnp.concatenate([cache_len, prompt_len[0]])[:, None]
-    angles = angle_tables(place + jnp.arange(steps, dtype=jnp.int32)[None, :])
-    dec_angle, new_angle = angles[:n_rows], angles[n_rows]
+    ticks = jnp.arange(steps, dtype=jnp.int32)
+    dec_angle = angle_tables(cache_len[:, None] + ticks[None, :])
+    new_angle = angle_tables(prompt_len[0, 0] + ticks)
 
     swap = [(i, i ^ 1) for i in range(n_blk)]
     hop = lambda d: [(2 * c + k, 2 * ((c + d) % n_chip) + k) for c in range(n_chip) for k in range(2)]
@@ -562,11 +560,12 @@
     for d in range(1, n_chip):
         far_x.append(lax.ppermute(shard, "blk", hop(d)))
 
-    own, raw, wq, ask = pl.pallas_call(
+    own, sib, raw, wq, ask = pl.pallas_call(
         first_kernel,
-        in_specs=[SMEM] * 3 + [HBM] * 6 + [ANY],
-        out_specs=[VMEM] * 4,
+        in_specs=[SMEM] * 3 + [HBM] * 7 + [ANY] * 2,
+        out_specs=[VMEM] * 5,
         out_shape=[
+            jax.ShapeDtypeStruct((blocks, rows, PAIR), bf16),
             jax.ShapeDtypeStruct((blocks, rows, PAIR), bf16),
             jax.ShapeDtypeStruct((n_rows, blocks, steps, PAIR), f32),
             pltpu.VMEM((blocks, width, PAIR), bf16),
@@ -574,41 +573,44 @@
         ],
         scratch_shapes=[
             pltpu.VMEM((rows, width), bf16),
+            pltpu.VMEM((rows, width), bf16),
             pltpu.VMEM((steps, n_rows, width), bf16),
             pltpu.VMEM((1, width), f32),
-            pltpu.VMEM((2, rows, HEAD_DIM), f32),
-            pltpu.VMEM((rows + decs, width), bf16),
+            pltpu.VMEM((4, rows, HEAD_DIM), f32),
+            pltpu.VMEM((2 * rows + decs, width), bf16),
             pltpu.SemaphoreType.DMA((blocks,)),
-            pltpu.SemaphoreType.DMA((5,)),
+            pltpu.SemaphoreType.DMA((8,)),
         ],
-        compiler_params=params(8),
+        compiler_params=params(10),
         name="first",
     )(
-        idx, slot, assign, stay(shard), stay(dec_tokens), stay(gain_row), stay(cos_t),
-        stay(sin_t), stay(w_qkv), angles,
+        idx, slot, assign, stay(shard), sib_x, stay(dec_tokens), stay(gain_row), stay(cos_t),
+        stay(sin_t), stay(w_qkv), dec_angle, new_angle,
     )
 
-    def project(which, x, asks):
+    def project(which, x, loads):
         outs = [jax.ShapeDtypeStruct((blocks, rows, PAIR), bf16)]
-        if asks:
-            outs.append(jax.ShapeDtypeStruct((blocks, 8, PAIR), f32))
+        if loads:
+            outs.append(pltpu.VMEM((out_blocks, attn_cols, OUT_COLS), bf16))
         return pl.pallas_call(
-            functools.partial(project_kernel, which, len(asks)),
-            in_specs=[SMEM] + [HBM] * 4 + [VMEM] * (1 + len(asks)),
+            functools.partial(project_kernel, which, loads),
+            in_specs=[SMEM] + [HBM] * 4 + [VMEM] + [HBM] * loads,
             out_specs=[VMEM] * len(outs),
             out_shape=outs,
             scratch_shapes=[
                 pltpu.VMEM((rows, width), bf16),
                 pltpu.VMEM((1, width), f32),
                 pltpu.VMEM((2, rows, HEAD_DIM), f32),
-                pltpu.VMEM((rows + (16 if asks else 0), width), bf16),
+                pltpu.VMEM((rows, width), bf16),
                 pltpu.SemaphoreType.DMA((4,)),
-            ],
+            ] + [pltpu.SemaphoreType.DMA((out_blocks,))] * loads,
             compiler_params=params(8),
             name="project",
-        )(idx, x, stay(gain_row), stay(cos_t), stay(sin_t), near(wq), *asks)
-
-    sib = project(1, sib_x, [])[0]
+        )(
+            idx, x, stay(gain_row), stay(cos_t), stay(sin_t), near(wq),
+            *([stay(w_out)] if loads else []),
+        )
+
     asks = [lax.ppermute(ask, groups, perm) for perm in shift]
 
     cached = cache_k.shape[1]
@@ -616,49 +618,49 @@
     count = cached // step_rows
     kv_width = heads * HEAD_DIM
     many = GROUP * steps * heads
-    half_rows = n_rows // 2
-
-    def decode(part):
-        loads = part == 0
+    low_rows = max(n_rows // 4, 1)
+
+    def decode(first, many_rows):
         return pl.pallas_call(
-            functools.partial(decode_kernel, part * half_rows, loads),
-            in_specs=[SMEM] * 2 + [VMEM] * 2 + [HBM] * (3 if loads else 2),
-            out_specs=[VMEM] * (2 if loads else 1),
-            out_shape=[
-                jax.ShapeDtypeStruct((decs, attn_cols), f32),
-                pltpu.VMEM((out_blocks, attn_cols, OUT_COLS), bf16),
-            ][: 2 if loads else 1],
+            functools.partial(decode_kernel, first),
+            in_specs=[SMEM] * 2 + [VMEM] * 2 + [HBM] * 2,
+            out_specs=VMEM,
+            out_shape=jax.ShapeDtypeStruct((decs, attn_cols), f32),
             scratch_shapes=[
-                pltpu.VMEM((half_rows, count, step_rows, kv_width), bf16),
-                pltpu.VMEM((half_rows, count, step_rows, kv_width), bf16),
-                pltpu.VMEM((half_rows, many, kv_width), bf16),
-                pltpu.VMEM((half_rows, 16, kv_width), bf16),
-                pltpu.VMEM((half_rows, 16, kv_width), bf16),
-                pltpu.VMEM((half_rows, many, 1), f32),
-                pltpu.VMEM((half_rows, many, 1), f32),
-                pltpu.VMEM((half_rows, many, kv_width), f32),
-                pltpu.SemaphoreType.DMA((half_rows, count)),
-                pltpu.SemaphoreType.DMA((half_rows, count)),
-            ] + ([pltpu.SemaphoreType.DMA((out_blocks,))] if loads else []),
-            compiler_params=params(12),
+                pltpu.VMEM((many_rows, count, step_rows, kv_width), bf16),
+                pltpu.VMEM((many_rows, count, step_rows, kv_width), bf16),
+                pltpu.VMEM((many_rows, many, kv_width), bf16),
+                pltpu.VMEM((many_rows, 16, kv_width), bf16),
+                pltpu.VMEM((many_rows, 16, kv_width), bf16),
+                pltpu.VMEM((many_rows, many, 1), f32),
+                pltpu.VMEM((many_rows, many, 1), f32),
+                pltpu.VMEM((many_rows, many, kv_width), f32),
+                pltpu.SemaphoreType.DMA((many_rows, count)),
+                pltpu.SemaphoreType.DMA((many_rows, count)),
+            ],
+            compiler_params=params(16),
             name="decode",
-        )(
-            cache_len, slot, raw, dec_angle, stay(cache_k), stay(cache_v),
-            *([stay(w_out)] if loads else []),
-        )
-
-    dec_low, wo = decode(0)
-    dec_high = decode(1)[0]
+        )(cache_len, slot, raw, dec_angle, stay(cache_k), stay(cache_v))
+
+    dec_low = decode(0, low_rows)
+    dec_high = decode(low_rows, n_rows - low_rows)
+
+    fronts, wo = [], None
+    for n in range(n_chip - 1):
+        passed = lax.ppermute(far_x[n], "blk", swap)
+        outs = project(2 + 2 * n, far_x[n], n == 0)
+        fronts.append((passed, outs[0]))
+        if n == 0:
+            wo = outs[1]
 
     def chunk(n, kvs, asks, kv_only):
-        passed = lax.ppermute(far_x[n], "blk", swap)
-        direct, *news = project(2 + 2 * n, far_x[n], asks)
+        passed, direct = fronts[n]
         outs = [jax.ShapeDtypeStruct((2 * heads, rows, PAIR), bf16)]
         scratch = [
             pltpu.VMEM((rows, width), bf16),
             pltpu.VMEM((1, width), f32),
             pltpu.VMEM((2, rows, HEAD_DIM), f32),
-            pltpu.VMEM((rows, width), bf16),
+            pltpu.VMEM((rows + (16 if asks else 0), width), bf16),
             pltpu.VMEM((blocks, rows, PAIR), bf16),
             pltpu.SemaphoreType.DMA((4,)),
         ]
@@ -668,7 +670,8 @@
         extra = []
         if asks:
             outs.append(jax.ShapeDtypeStruct((decs, attn_cols), bf16))
-            extra = [*news, new_angle]
+            scratch.append(pltpu.VMEM((blocks, 8, PAIR), f32))
+            extra = [*asks, new_angle]
         kernel = functools.partial(chunk_kernel, n, 2, len(kvs), len(asks), kv_only)
         return pl.pallas_call(
             kernel,
@@ -709,9 +712,11 @@
         both = add(outs[1], other)
         back.append(lax.ppermute(both, "blk", hop(n_chip - 1 - n)))
 
-    rets = [lax.ppermute(fresh, groups, perm) for perm in shift]
+    rets = []
+    for perm in shift:
+        rets.append(lax.ppermute(fresh, groups, perm))
     own_part, sib_part, dec_part = pl.pallas_call(
-        functools.partial(last_kernel, len(kvs), n_batch, n_rows),
+        functools.partial(last_kernel, len(kvs), n_batch, n_rows, low_rows),
         in_specs=[SMEM] * 4 + [VMEM] * (5 + len(kvs) + n_batch),
         out_specs=[VMEM] * 3,
         out_shape=[
@@ -754,7 +759,7 @@
     pieces = 4
     result = pl.pallas_call(
         functools.partial(sum_kernel, n_chip - 1),
-        in_specs=[VMEM] + [HBM] * len(back),
+        in_specs=[VMEM] + [HBM] * (n_chip - 1),
         out_specs=HBM,
         out_shape=jax.ShapeDtypeStruct((rows, width), bf16),
         scratch_shapes=[

time: 122 us -> 116 us (0.951)
  the two profiles are of different devices: /device:TPU:0 before, /device:TPU:14 now
where the time goes in v3:
time: 116 us
  waiting for transfers between devices  48.2 us (42%)
  Pallas kernels  47.4 us (41%)
  starting transfers between devices  16.5 us (14%)
  between operations  2.97 us (3%)
    ppermute x1, waiting for transfers between devices, layer(): lax.ppermute(total, 'blk', [(i, i ^ 2 * reach) for i in range(n_blk)])  23.6 us
    ppermute x1, waiting for transfers between devices, layer(): far_x.append(lax.ppermute(shard, 'blk', hop(d)))  22.6 us
    pallas_call x2, Pallas kernels, decode(): pl.pallas_call(functools.partial(decode_kernel, first), in_specs=[SMEM] *...  12.6 us
    pallas_call x1, Pallas kernels, layer(): pl.pallas_call(first_kernel, in_specs=[SMEM] * 3 + [HBM] * 7 + [ANY] * 2,...  11.8 us
    pallas_call x1, Pallas kernels, chunk(): pl.pallas_call(kernel, in_specs=[SMEM] * 2 + [HBM] * 4 + [VMEM] * (5 + le...  9.15 us
    ppermute x4, starting transfers between devices, layer(): rets.append(lax.ppermute(fresh, groups, perm))  7.52 us
    ppermute x4, starting transfers between devices, layer(): asks = [lax.ppermute(ask, groups, perm) for perm in shift]  7.04 us
    pallas_call x1, Pallas kernels, layer(): pl.pallas_call(functools.partial(last_kernel, len(kvs), n_batch, n_rows,...  5.11 us
  transfers between devices with their start and end apart: 15, of which 3 were waited for; matrix products, arithmetic and copies ran while one was open for 1% of the time, Pallas kernels for 32%

profile of v3, /device:TPU:14, one launch (start us, length us, event | category | flops | bytes accessed | tf_op | source)
XLA Modules:
  0.0 116.1 jit_solution(6843391436413230254)
XLA Ops:
  0.6 0.6 collective-permute-start.1
  1.2 0.0 collective-permute-start
  3.2 22.6 %collective-permute-done.1.refs_1_ = bf16[128,4096]{1,0:T(8,128)(2,1)S(1)} collective-permute-done((bf16[128,4096]{1,0:T(8,128)(2,1)}, bf16[128,4096]{1,0:T(8,128)(2,1)S(1)}, u32[]{:S(2)}, u32[]{:S(2)}) %collective-permute-start.1) | collective-permute-done | bytes 1048608 | tf_op jit(solution)/shard_map/ppermute | solution.py:561
  25.8 0.0 collective-permute-start.2
  25.8 0.7 add_convert_fusion
  26.6 0.1 fusion.1._b.refs_15_
  26.7 0.1 fusion._a.refs_3_
  26.8 0.0 collective-permute-done.sib_hbm
  26.8 11.8 %first.1 = (bf16[6,128,256]{2,1,0:T(8,128)(2,1)S(1)}, bf16[6,128,256]{2,1,0:T(8,128)(2,1)S(1)}, f32[4,6,4,256]{3,2,1,0:T(4,128)S(1)}, bf16[6,4096,256]{2,1,0:T(8,128)(2,1)S(1)}, bf16[8,4096]{1,0:T(8,128)(2,1)S(1)}) custom-call(s32[5]{0:T(128)S(1)} %compare_select_fusion.2.idx.refs_0_, s32[1,1]{1,0:T(1,128)S(6)} %copy.17.slot.refs_1_.refs_2_, ...), custom_call_target="tpu_custom_call" | custom-call | tf_op jit(solution)/shard_map/first/pallas_call | solution.py:563
  38.6 0.6 collective-permute-start.3
  39.2 2.5 %collective-permute-start.4 = (bf16[8,4096]{1,0:T(8,128)(2,1)S(1)}, bf16[8,4096]{1,0:T(8,128)(2,1)S(1)}, u32[]{:S(2)}, u32[]{:S(2)}) collective-permute-start(bf16[8,4096]{1,0:T(8,128)(2,1)S(1)} %get-tuple-element.21), channel_id=1, source_target_pairs={{0,17},{1,18},{2,19},{3,16},{16,1},{17,2},{18,3},{19,0},{4,21},{5,... | collective-permute-start | bytes 196616 | tf_op jit(solution)/shard_map/ppermute | solution.py:614
  41.7 1.2 %collective-permute-start.5 = (bf16[8,4096]{1,0:T(8,128)(2,1)S(1)}, bf16[8,4096]{1,0:T(8,128)(2,1)S(1)}, u32[]{:S(2)}, u32[]{:S(2)}) collective-permute-start(bf16[8,4096]{1,0:T(8,128)(2,1)S(1)} %get-tuple-element.21), channel_id=1, source_target_pairs={{0,18},{1,19},{2,16},{3,17},{16,2},{17,3},{18,0},{19,1},{4,22},{5,... | collective-permute-start | bytes 196616 | tf_op jit(solution)/shard_map/ppermute | solution.py:614
  42.9 2.8 %collective-permute-start.6 = (bf16[8,4096]{1,0:T(8,128)(2,1)S(1)}, bf16[8,4096]{1,0:T(8,128)(2,1)S(1)}, u32[]{:S(2)}, u32[]{:S(2)}) collective-permute-start(bf16[8,4096]{1,0:T(8,128)(2,1)S(1)} %get-tuple-element.21), channel_id=1, source_target_pairs={{0,19},{1,16},{2,17},{3,18},{16,3},{17,0},{18,1},{19,2},{4,23},{5,... | collective-permute-start | bytes 196616 | tf_op jit(solution)/shard_map/ppermute | solution.py:614
  45.7 4.8 %project.1 = (bf16[6,128,256]{2,1,0:T(8,128)(2,1)S(1)}, bf16[4,1024,1024]{2,1,0:T(8,128)(2,1)S(1)}) custom-call(s32[5]{0:T(128)S(1)} %compare_select_fusion.2.idx.refs_0_, bf16[128,4096]{1,0:T(8,128)(2,1)S(1)} %collective-permute-done.1.refs_1_, f32[1,4096]{1,0:T(1,128)} %bitcast.11, f32[512,128]{1,0:T(8,128)} %constant.49.clone.cos_hbm.refs_3_.refs_4_, ...), custom_call_target="tpu_custom_call" | custom-call | tf_op jit(solution)/shard_map/project/pallas_call | solution.py:595
  50.5 0.0 collective-permute-done.3.refs_11_
  50.5 0.0 collective-permute-done.4.refs_12_
  50.5 0.0 collective-permute-done.5.refs_13_
  50.6 0.0 collective-permute-done.6.refs_14_
  50.6 0.0 collective-permute-done.2.refs_2_
  50.6 0.0 copy-start.1
  50.6 9.2 %chunk.1 = (bf16[4,128,256]{2,1,0:T(8,128)(2,1)S(1)}, bf16[128,4096]{1,0:T(8,128)(2,1)S(1)}, bf16[128,4096]{1,0:T(8,128)(2,1)S(1)}, bf16[16,1024]{1,0:T(8,128)(2,1)S(1)}) custom-call(s32[5]{0:T(128)S(1)} %compare_select_fusion.2.idx.refs_0_, s32[1,1]{1,0:T(1,128)} %copy.15.refs_1_, bf16[128,4096]{1,0:T(8,128)(2,1)S(1)} %collective-permute-done.2.refs_2_, ...), custom_call_target="tpu_custom_call" | custom-call | tf_op jit(solution)/shard_map/chunk/pallas_call | solution.py:676
  59.7 0.1 collective-permute-start.12
  59.8 1.3 %collective-permute-start.10 = (bf16[16,1024]{1,0:T(8,128)(2,1)S(1)}, bf16[16,1024]{1,0:T(8,128)(2,1)S(1)}, u32[]{:S(2)}, u32[]{:S(2)}) collective-permute-start(bf16[16,1024]{1,0:T(8,128)(2,1)S(1)} %get-tuple-element.24), channel_id=1, source_target_pairs={{0,19},{1,16},{2,17},{3,18},{16,3},{17,0},{18,1},{19,2},{4,23},{5,... | collective-permute-start | bytes 98312 | tf_op jit(solution)/shard_map/ppermute | solution.py:717
  61.2 1.5 %collective-permute-start.7 = (bf16[16,1024]{1,0:T(8,128)(2,1)S(1)}, bf16[16,1024]{1,0:T(8,128)(2,1)S(1)}, u32[]{:S(2)}, u32[]{:S(2)}) collective-permute-start(bf16[16,1024]{1,0:T(8,128)(2,1)S(1)} %get-tuple-element.24), channel_id=1, source_target_pairs={{0,16},{1,17},{2,18},{3,19},{16,0},{17,1},{18,2},{19,3},{4,20},{5,... | collective-permute-start | bytes 98312 | tf_op jit(solution)/shard_map/ppermute | solution.py:717
  62.7 0.6 collective-permute-start.8
  63.3 4.0 %collective-permute-start.9 = (bf16[16,1024]{1,0:T(8,128)(2,1)S(1)}, bf16[16,1024]{1,0:T(8,128)(2,1)S(1)}, u32[]{:S(2)}, u32[]{:S(2)}) collective-permute-start(bf16[16,1024]{1,0:T(8,128)(2,1)S(1)} %get-tuple-element.24), channel_id=1, source_target_pairs={{0,18},{1,19},{2,16},{3,17},{16,2},{17,3},{18,0},{19,1},{4,22},{5,... | collective-permute-start | bytes 98312 | tf_op jit(solution)/shard_map/ppermute | solution.py:717
  67.3 0.0 copy-done.1
  67.4 4.3 %decode.2.refs_7_ = f32[16,1024]{1,0:T(8,128)S(1)} custom-call(s32[4]{0:T(128)S(1)} %copy-done.1, s32[1,1]{1,0:T(1,128)S(6)} %copy.17.slot.refs_1_.refs_2_, f32[4,6,4,256]{3,2,1,0:T(4,128)S(1)} %get-tuple-element.23.refs_2_, f32[4,4,128]{2,1,0:T(4,128)S(1)} %fusion._a.refs_3_, bf16[4,4096,256]{2,1,0:T(8,128)(2,1)} %refs_4_.5, bf16[4,4096,256]{2,1,0:T(8,128)(2,1)} %refs_5_.4), custom_call_target="tpu_custom_call" | custom-call | tf_op jit(solution)/shard_map/decode/pallas_call | solution.py:624
  71.7 8.3 %decode.3.refs_8_ = f32[16,1024]{1,0:T(8,128)S(1)} custom-call(s32[4]{0:T(128)S(1)} %copy-done.1, s32[1,1]{1,0:T(1,128)S(6)} %copy.17.slot.refs_1_.refs_2_, f32[4,6,4,256]{3,2,1,0:T(4,128)S(1)} %get-tuple-element.23.refs_2_, f32[4,4,128]{2,1,0:T(4,128)S(1)} %fusion._a.refs_3_, bf16[4,4096,256]{2,1,0:T(8,128)(2,1)} %refs_4_.5, bf16[4,4096,256]{2,1,0:T(8,128)(2,1)} %refs_5_.4), custom_call_target="tpu_custom_call" | custom-call | tf_op jit(solution)/shard_map/decode/pallas_call | solution.py:624
  80.0 0.0 collective-permute-done.10.refs_12_
  80.0 0.0 collective-permute-done.7.refs_9_
  80.0 0.0 collective-permute-done.8.refs_10_
  80.0 0.0 collective-permute-done.9.refs_11_
  80.0 0.0 copy-start
  80.0 5.1 %last.1 = (bf16[128,4096]{1,0:T(8,128)(2,1)S(1)}, bf16[144,4096]{1,0:T(8,128)(2,1)S(1)}, bf16[16,4096]{1,0:T(8,128)(2,1)S(1)}) custom-call(s32[5]{0:T(128)S(1)} %compare_select_fusion.2.idx.refs_0_, s32[1,1]{1,0:T(1,128)} %copy.15.refs_1_, s32[1,1]{1,0:T(1,128)S(6)} %copy.17.slot.refs_1_.refs_2_, s32[1,1]{1,0:T(1,128)S(6)} %copy.16.assign.refs_3_, ...), custom_call_target="tpu_custom_call" | custom-call | tf_op jit(solution)/shard_map/last/pallas_call | solution.py:718
  85.1 0.1 collective-permute-start.11
  85.2 0.0 collective-permute-done.12.b
  85.2 0.3 add.88
  85.5 0.6 collective-permute-start.13
  86.1 1.9 %collective-permute-done.11.sib.b = bf16[144,4096]{1,0:T(8,128)(2,1)S(1)} collective-permute-done((bf16[144,4096]{1,0:T(8,128)(2,1)S(1)}, bf16[144,4096]{1,0:T(8,128)(2,1)S(1)}, u32[]{:S(2)}, u32[]{:S(2)}) %collective-permute-start.11) | collective-permute-done | bytes 1179680 | tf_op jit(solution)/shard_map/ppermute | solution.py:733
  88.1 0.6 collective-permute-start.14
  88.7 1.6 %base.1 = f32[128,4096]{1,0:T(8,128)S(1)} custom-call(bf16[128,4096]{1,0:T(8,128)(2,1)} %bitcast.8, bf16[128,4096]{1,0:T(8,128)(2,1)S(1)} %get-tuple-element.25.own, bf16[144,4096]{1,0:T(8,128)(2,1)S(1)} %collective-permute-done.11.sib.b), custom_call_target="tpu_custom_call" | custom-call | tf_op jit(solution)/shard_map/base/pallas_call | solution.py:750
  90.3 23.6 %collective-permute-done.14.b = bf16[16,4096]{1,0:T(8,128)(2,1)S(1)} collective-permute-done((bf16[16,4096]{1,0:T(8,128)(2,1)S(1)}, bf16[16,4096]{1,0:T(8,128)(2,1)S(1)}, u32[]{:S(2)}, u32[]{:S(2)}) %collective-permute-start.14) | collective-permute-done | bytes 131104 | tf_op jit(solution)/shard_map/ppermute | solution.py:738
  113.9 0.0 copy-done
  113.9 0.7 dec.1
  114.7 0.0 collective-permute-done.13.refs_0_
  114.7 1.2 %sum.1 = bf16[128,4096]{1,0:T(8,128)(2,1)} custom-call(f32[128,4096]{1,0:T(8,128)S(1)} %base.1, bf16[128,4096]{1,0:T(8,128)(2,1)S(1)} %collective-permute-done.13.refs_0_), custom_call_target="tpu_custom_call" | custom-call | tf_op jit(solution)/shard_map/sum/pallas_call | solution.py:760
  (5 shorter events, 0.1 us)
Async XLA Ops:
  0.6 25.2 %collective-permute-start.1 = (bf16[128,4096]{1,0:T(8,128)(2,1)}, bf16[128,4096]{1,0:T(8,128)(2,1)S(1)}, u32[]{:S(2)}, u32[]{:S(2)}) collective-permute-start(bf16[128,4096]{1,0:T(8,128)(2,1)} %bitcast.5), channel_id=1, source_target_pairs={{0,8},{4,12},{8,0},{12,4},{1,9},{5,13},{9,1},{13,5},{2,10},{6,14},... | collective-permute-start | bytes 3145736 | tf_op jit(solution)/shard_map/ppermute | solution.py:561
  1.2 25.6 %collective-permute-start = (bf16[128,4096]{1,0:T(8,128)(2,1)}, bf16[128,4096]{1,0:T(8,128)(2,1)S(1)}, u32[]{:S(2)}, u32[]{:S(2)}) collective-permute-start(bf16[128,4096]{1,0:T(8,128)(2,1)} %bitcast.6), channel_id=1, source_target_pairs={{0,4},{4,0},{8,12},{12,8},{1,5},{5,1},{9,13},{13,9},{2,6},{6,2},{1... | collective-permute-start | bytes 3145736 | tf_op jit(solution)/shard_map/ppermute | solution.py:558
  25.8 24.8 %collective-permute-start.2 = (bf16[128,4096]{1,0:T(8,128)(2,1)S(1)}, bf16[128,4096]{1,0:T(8,128)(2,1)S(1)}, u32[]{:S(2)}, u32[]{:S(2)}) collective-permute-start(bf16[128,4096]{1,0:T(8,128)(2,1)S(1)} %collective-permute-done.1.refs_1_), channel_id=1, source_target_pairs={{0,4},{4,0},{8,12},{12,8},{1,5},{5,1},{9,13},{13,9},{2,6},{6,2},{1... | collective-permute-start | bytes 3145736 | tf_op jit(solution)/shard_map/ppermute | solution.py:650
  38.6 11.9 %collective-permute-start.3 = (bf16[8,4096]{1,0:T(8,128)(2,1)S(1)}, bf16[8,4096]{1,0:T(8,128)(2,1)S(1)}, u32[]{:S(2)}, u32[]{:S(2)}) collective-permute-start(bf16[8,4096]{1,0:T(8,128)(2,1)S(1)} %get-tuple-element.21), channel_id=1, source_target_pairs={{0,16},{1,17},{2,18},{3,19},{16,0},{17,1},{18,2},{19,3},{4,20},{5,... | collective-permute-start | bytes 196616 | tf_op jit(solution)/shard_map/ppermute | solution.py:614
  39.2 11.3 %collective-permute-start.4 = (bf16[8,4096]{1,0:T(8,128)(2,1)S(1)}, bf16[8,4096]{1,0:T(8,128)(2,1)S(1)}, u32[]{:S(2)}, u32[]{:S(2)}) collective-permute-start(bf16[8,4096]{1,0:T(8,128)(2,1)S(1)} %get-tuple-element.21), channel_id=1, source_target_pairs={{0,17},{1,18},{2,19},{3,16},{16,1},{17,2},{18,3},{19,0},{4,21},{5,... | collective-permute-start | bytes 196616 | tf_op jit(solution)/shard_map/ppermute | solution.py:614
  41.7 8.8 %collective-permute-start.5 = (bf16[8,4096]{1,0:T(8,128)(2,1)S(1)}, bf16[8,4096]{1,0:T(8,128)(2,1)S(1)}, u32[]{:S(2)}, u32[]{:S(2)}) collective-permute-start(bf16[8,4096]{1,0:T(8,128)(2,1)S(1)} %get-tuple-element.21), channel_id=1, source_target_pairs={{0,18},{1,19},{2,16},{3,17},{16,2},{17,3},{18,0},{19,1},{4,22},{5,... | collective-permute-start | bytes 196616 | tf_op jit(solution)/shard_map/ppermute | solution.py:614
  42.9 7.6 %collective-permute-start.6 = (bf16[8,4096]{1,0:T(8,128)(2,1)S(1)}, bf16[8,4096]{1,0:T(8,128)(2,1)S(1)}, u32[]{:S(2)}, u32[]{:S(2)}) collective-permute-start(bf16[8,4096]{1,0:T(8,128)(2,1)S(1)} %get-tuple-element.21), channel_id=1, source_target_pairs={{0,19},{1,16},{2,17},{3,18},{16,3},{17,0},{18,1},{19,2},{4,23},{5,... | collective-permute-start | bytes 196616 | tf_op jit(solution)/shard_map/ppermute | solution.py:614
  50.6 16.8 %copy-start.1 = (s32[4]{0:T(128)S(1)}, s32[4]{0:T(128)}, u32[]{:S(2)}) copy-start(s32[4]{0:T(128)} %refs_0_.3) | copy-start | bytes 52
  59.7 25.5 %collective-permute-start.12 = (bf16[128,4096]{1,0:T(8,128)(2,1)S(1)}, bf16[128,4096]{1,0:T(8,128)(2,1)S(1)}, u32[]{:S(2)}, u32[]{:S(2)}) collective-permute-start(bf16[128,4096]{1,0:T(8,128)(2,1)S(1)} %get-tuple-element.28), channel_id=1, source_target_pairs={{0,4},{4,0},{8,12},{12,8},{1,5},{5,1},{9,13},{13,9},{2,6},{6,2},{1... | collective-permute-start | bytes 3145736 | tf_op jit(solution)/shard_map/ppermute | solution.py:711
  59.8 20.1 %collective-permute-start.10 = (bf16[16,1024]{1,0:T(8,128)(2,1)S(1)}, bf16[16,1024]{1,0:T(8,128)(2,1)S(1)}, u32[]{:S(2)}, u32[]{:S(2)}) collective-permute-start(bf16[16,1024]{1,0:T(8,128)(2,1)S(1)} %get-tuple-element.24), channel_id=1, source_target_pairs={{0,19},{1,16},{2,17},{3,18},{16,3},{17,0},{18,1},{19,2},{4,23},{5,... | collective-permute-start | bytes 98312 | tf_op jit(solution)/shard_map/ppermute | solution.py:717
  61.2 18.8 %collective-permute-start.7 = (bf16[16,1024]{1,0:T(8,128)(2,1)S(1)}, bf16[16,1024]{1,0:T(8,128)(2,1)S(1)}, u32[]{:S(2)}, u32[]{:S(2)}) collective-permute-start(bf16[16,1024]{1,0:T(8,128)(2,1)S(1)} %get-tuple-element.24), channel_id=1, source_target_pairs={{0,16},{1,17},{2,18},{3,19},{16,0},{17,1},{18,2},{19,3},{4,20},{5,... | collective-permute-start | bytes 98312 | tf_op jit(solution)/shard_map/ppermute | solution.py:717
  62.7 17.3 %collective-permute-start.8 = (bf16[16,1024]{1,0:T(8,128)(2,1)S(1)}, bf16[16,1024]{1,0:T(8,128)(2,1)S(1)}, u32[]{:S(2)}, u32[]{:S(2)}) collective-permute-start(bf16[16,1024]{1,0:T(8,128)(2,1)S(1)} %get-tuple-element.24), channel_id=1, source_target_pairs={{0,17},{1,18},{2,19},{3,16},{16,1},{17,2},{18,3},{19,0},{4,21},{5,... | collective-permute-start | bytes 98312 | tf_op jit(solution)/shard_map/ppermute | solution.py:717
  63.3 16.7 %collective-permute-start.9 = (bf16[16,1024]{1,0:T(8,128)(2,1)S(1)}, bf16[16,1024]{1,0:T(8,128)(2,1)S(1)}, u32[]{:S(2)}, u32[]{:S(2)}) collective-permute-start(bf16[16,1024]{1,0:T(8,128)(2,1)S(1)} %get-tuple-element.24), channel_id=1, source_target_pairs={{0,18},{1,19},{2,16},{3,17},{16,2},{17,3},{18,0},{19,1},{4,22},{5,... | collective-permute-start | bytes 98312 | tf_op jit(solution)/shard_map/ppermute | solution.py:717
  80.0 33.9 %copy-start = (bf16[4,4,4096]{2,1,0:T(4,128)(2,1)S(1)}, bf16[4,4,4096]{2,1,0:T(4,128)(2,1)}, u32[]{:S(2)}) copy-start(bf16[4,4,4096]{2,1,0:T(4,128)(2,1)} %tokens.1) | copy-start | bytes 393220
  85.1 2.9 %collective-permute-start.11 = (bf16[144,4096]{1,0:T(8,128)(2,1)S(1)}, bf16[144,4096]{1,0:T(8,128)(2,1)S(1)}, u32[]{:S(2)}, u32[]{:S(2)}) collective-permute-start(bf16[144,4096]{1,0:T(8,128)(2,1)S(1)} %get-tuple-element.26), channel_id=1, source_target_pairs={{0,4},{4,0},{8,12},{12,8},{1,5},{5,1},{9,13},{13,9},{2,6},{6,2},{1... | collective-permute-start | bytes 3538952 | tf_op jit(solution)/shard_map/ppermute | solution.py:733
  85.5 29.2 %collective-permute-start.13 = (bf16[128,4096]{1,0:T(8,128)(2,1)S(1)}, bf16[128,4096]{1,0:T(8,128)(2,1)S(1)}, u32[]{:S(2)}, u32[]{:S(2)}) collective-permute-start(bf16[128,4096]{1,0:T(8,128)(2,1)S(1)} %add.88), channel_id=1, source_target_pairs={{0,8},{4,12},{8,0},{12,4},{1,9},{5,13},{9,1},{13,5},{2,10},{6,14},... | collective-permute-start | bytes 3145736 | tf_op jit(solution)/shard_map/ppermute | solution.py:713
  88.1 25.8 %collective-permute-start.14 = (bf16[16,4096]{1,0:T(8,128)(2,1)S(1)}, bf16[16,4096]{1,0:T(8,128)(2,1)S(1)}, u32[]{:S(2)}, u32[]{:S(2)}) collective-permute-start(bf16[16,4096]{1,0:T(8,128)(2,1)S(1)} %add.89.a), channel_id=1, source_target_pairs={{0,8},{4,12},{8,0},{12,4},{1,9},{5,13},{9,1},{13,5},{2,10},{6,14},... | collective-permute-start | bytes 393224 | tf_op jit(solution)/shard_map/ppermute | solution.py:738
